TPU v7x, 32 devices: a whole 2x2x4 slice. The times are simulated.
32 devices in a mesh: seq: 8 (over y, x, core), head: 4 (over z).
Axes of the slice: x: 2, y: 2, z: 4, core: 2. Of those that a mesh axis runs over, the one named last changes fastest.
Arguments:
- queries: bfloat16 [2048, 4096], P('seq', 'head'), may hold values from -7.1875 to 7.1875
- keys: bfloat16 [2048, 1024], P(('seq', 'head')), may hold values from -7.1875 to 7.1875
- values: bfloat16 [2048, 1024], P(('seq', 'head')), may hold values from -6 to 6
- outputs: bfloat16 [2048, 4096], P('seq', 'head'), may hold values from -1.1953125 to 1.1953125
- out_grad: bfloat16 [2048, 4096], P('seq', 'head'), may hold values from -6 to 6
- log_norm: float32 [32, 2048], P('head', 'seq'), as said below
- block_order: int32 [16], replicated, may hold values from 0 to 15, as said below
Outputs:
- query_grad: bfloat16 [2048, 4096], P('seq', 'head')
- key_gradient_rows: bfloat16 [2048, 1024], P(('seq', 'head'))
- value_gradient_rows: bfloat16 [2048, 1024], P(('seq', 'head'))
Inputs may be any that keep to these rules, and one draw needn't show every extreme that they name: `block_order`: A permutation of 0 to 15. log_norm[h, i] lies within 0.6 of one plus the natural logarithm of 1 + pos[i].
All inputs are finite; a program needn't handle non-finite values.
Results may differ from a plain program's by a relative error of at most 0.014.
Values may be sent and summed in bfloat16 or wider, within the bound.
No kernel may reach another device: no remote copies, remote signals or barrier semaphores. Data moves between devices by JAX's collectives and lax.ppermute only.
A program may use at most 192 MiB of HBM per device.

v0:
```python
import jax
import jax.numpy as jnp
from jax import lax
from jax.sharding import PartitionSpec as P

QUERY_HEADS = 32
KEY_VALUE_HEADS = 8
HEAD_SIZE = 128


def row_positions(block_order, first_row, count, half):
    rows_here = first_row + jnp.arange(count, dtype=jnp.int32)
    blocks = rows_here // half
    table = jnp.arange(block_order.shape[0], dtype=jnp.int32)
    picked = jnp.sum(jnp.where(blocks[:, None] == table[None, :], block_order[None, :], 0), 1)
    return picked * half + rows_here % half


def masked_terms(q_blk, dout_blk, lse_blk, delta_blk, q_pos, k_blk, v_blk, k_pos):
    scale = HEAD_SIZE ** (-0.5)
    scores = jnp.einsum("tgrd,ngd->grtn", q_blk, k_blk, preferred_element_type=jnp.float32) * scale
    visible = k_pos[None, :] <= q_pos[:, None]
    prob = jnp.where(visible, jnp.exp(scores - lse_blk[..., None]), 0.0)
    dprob = jnp.einsum("tgrd,ngd->grtn", dout_blk, v_blk, preferred_element_type=jnp.float32)
    dscore = prob * (dprob - delta_blk[..., None])
    prob_low = prob.astype(jnp.bfloat16)
    dscore_low = dscore.astype(jnp.bfloat16)
    queries_gradient = (
        jnp.einsum("grtn,ngd->tgrd", dscore_low, k_blk, preferred_element_type=jnp.float32) * scale
    )
    keys_gradient = (
        jnp.einsum("grtn,tgrd->ngd", dscore_low, q_blk, preferred_element_type=jnp.float32) * scale
    )
    values_gradient = jnp.einsum(
        "grtn,tgrd->ngd", prob_low, dout_blk, preferred_element_type=jnp.float32
    )
    return (queries_gradient, keys_gradient, values_gradient)


def step_rows(count):
    step = count
    while step > 1024 and step % 2 == 0:
        step = step // 2
    return step


def local(queries, keys, values, outputs, out_grad, log_norm, block_order):
    index = lax.axis_index("seq")
    rows = queries.shape[0]
    half = rows // 2
    group_ratio = QUERY_HEADS // KEY_VALUE_HEADS
    k_loc, v_loc = (
        lax.all_to_all(keys, "head", split_axis=1, concat_axis=0, tiled=True),
        lax.all_to_all(values, "head", split_axis=1, concat_axis=0, tiled=True),
    )
    q_cols = queries.shape[1]
    heads_here = q_cols // HEAD_SIZE
    groups = heads_here // group_ratio
    k_cols = k_loc.shape[1]
    delta = jnp.sum(
        (out_grad.astype(jnp.float32) * outputs.astype(jnp.float32)).reshape(
            rows, heads_here, HEAD_SIZE
        ),
        -1,
    )
    own_pair = lax.dynamic_slice(block_order, (2 * index,), (2,))
    own_blocks = (own_pair[0], own_pair[1])
    offset = jnp.arange(half, dtype=jnp.int32)
    own_pos = jnp.concatenate([own_blocks[0] * half + offset, own_blocks[1] * half + offset], 0)
    k_own = k_loc.reshape(rows, groups, HEAD_SIZE)
    v_own = v_loc.reshape(rows, groups, HEAD_SIZE)
    keys_gradient = None
    values_gradient = None
    all_lse, all_delta = (
        lax.all_gather(log_norm.T, "seq", axis=0, tiled=True),
        lax.all_gather(delta, "seq", axis=0, tiled=True),
    )
    k_zero = jnp.zeros((rows, groups, HEAD_SIZE), jnp.float32)
    grad_k = k_zero
    grad_v = k_zero
    q_piece = lax.all_gather(queries, "seq", axis=0, tiled=True)
    dout_piece = lax.all_gather(out_grad, "seq", axis=0, tiled=True)
    count = q_piece.shape[0]
    step = step_rows(count)

    def one(acc, i):
        q_blk = lax.dynamic_slice_in_dim(q_piece, i * step, step, 0).reshape(
            step, groups, group_ratio, HEAD_SIZE
        )
        dout_blk = lax.dynamic_slice_in_dim(dout_piece, i * step, step, 0).reshape(
            step, groups, group_ratio, HEAD_SIZE
        )
        row0 = i * step
        lse_blk = lax.dynamic_slice_in_dim(all_lse, row0, step, 0).T.reshape(
            groups, group_ratio, step
        )
        delta_blk = lax.dynamic_slice_in_dim(all_delta, row0, step, 0).T.reshape(
            groups, group_ratio, step
        )
        q_pos = row_positions(block_order, row0, step, half)
        terms = masked_terms(q_blk, dout_blk, lse_blk, delta_blk, q_pos, k_own, v_own, own_pos)
        return ((acc[0] + terms[1], acc[1] + terms[2]), terms[0].reshape(step, q_cols))

    (grad_k, grad_v), stacked = lax.scan(
        one, (grad_k, grad_v), jnp.arange(count // step, dtype=jnp.int32)
    )
    grad_q_all = stacked.reshape(count, q_cols)
    grad_k, grad_v, grad_q_all = (grad_k, grad_v, grad_q_all)
    queries_gradient = lax.psum_scatter(
        grad_q_all.astype(jnp.bfloat16), "seq", scatter_dimension=0, tiled=True
    )
    keys_gradient = grad_k.reshape(rows, k_cols)
    values_gradient = grad_v.reshape(rows, k_cols)
    low_k = keys_gradient.astype(jnp.bfloat16)
    low_v = values_gradient.astype(jnp.bfloat16)
    key_gradient_rows, value_gradient_rows = (
        lax.all_to_all(low_k, "head", split_axis=0, concat_axis=1, tiled=True),
        lax.all_to_all(low_v, "head", split_axis=0, concat_axis=1, tiled=True),
    )
    return (queries_gradient, key_gradient_rows, value_gradient_rows)


def solution(mesh):
    in_specs = (
        P("seq", "head"),
        P(("seq", "head"), None),
        P(("seq", "head"), None),
        P("seq", "head"),
        P("seq", "head"),
        P("head", "seq"),
        P(),
    )
    out_specs = (P("seq", "head"), P(("seq", "head"), None), P(("seq", "head"), None))
    return jax.shard_map(local, mesh=mesh, in_specs=in_specs, out_specs=out_specs, check_vma=False)
```

profile of v0, /device:TPU:0, one launch (start us, length us, event | category | flops | bytes accessed | tf_op | source)
XLA Modules:
  0.0 188.3 jit_solution(1644582682500245099)
XLA Ops:
  7.2 0.0 copy-start.2
  7.2 0.0 copy-start.3
  7.2 0.0 all-gather.3.cloned.1.call-start
  7.2 2.1 %copy.61 = bf16[256,1024]{0,1:T(8,128)(2,1)} copy(bf16[256,1024]{1,0:T(8,128)(2,1)} %param.9) | data formatting | bytes 1048576 | tf_op args[0]
  9.3 0.0 all-gather.3.cloned.1.call-update
  9.4 0.0 all-gather.5.cloned.1.call-start
  9.4 2.1 %copy.63 = bf16[256,1024]{0,1:T(8,128)(2,1)} copy(bf16[256,1024]{1,0:T(8,128)(2,1)} %param.13) | data formatting | bytes 1048576 | tf_op args[4]
  11.5 0.0 all-gather.5.cloned.1.call-update
  11.5 0.0 copy-start.5
  11.6 1.6 copy.90
  13.1 6.3 %all-to-all-start = ((bf16[64,4,256]{2,0,1:T(8,128)(2,1)}), bf16[64,4,256]{2,0,1:T(8,128)(2,1)S(1)}, u32[]{:S(2)}, u32[]{:S(2)}) async-start(bf16[64,4,256]{2,0,1:T(8,128)(2,1)} %bitcast.94), calls=%async_computation | async-start | bytes 262144 | tf_op jit(solution)/shard_map/all_to_all | solution.py:53
  19.5 0.7 dynamic_slice.34
  20.2 0.6 fusion.29
  22.1 1.6 copy.89
  23.7 0.2 multiply_bitcast_fusion
  23.8 0.2 copy.86
  24.0 0.3 reduce_sum.21
  24.4 12.3 %all_gather.15 = f32[2048,8]{1,0:T(8,128)S(1)} all-gather(f32[256,8]{1,0:T(8,128)S(1)} %reduce_sum.21), channel_id=1, replica_groups=mesh['seq'=8,'head'=4] {'seq'}, dimensions={0}, use_global_device_ids=true | all-gather | bytes 73728 | tf_op jit(solution)/shard_map/all_gather | solution.py:76
  36.6 0.3 copy.67
  36.9 8.4 %all_gather.13 = f32[2048,8]{0,1:T(8,128)S(1)} all-gather(f32[256,8]{0,1:T(8,128)S(1)} %bitcast.150), channel_id=1, replica_groups=mesh['seq'=8,'head'=4] {'seq'}, dimensions={0}, use_global_device_ids=true | all-gather | bytes 73728 | tf_op jit(solution)/shard_map/all_gather | solution.py:75
  45.3 0.0 all-to-all-done
  45.3 5.0 %all-to-all-start.1 = ((bf16[64,4,256]{2,0,1:T(8,128)(2,1)}), bf16[64,4,256]{2,0,1:T(8,128)(2,1)S(1)}, u32[]{:S(2)}, u32[]{:S(2)}) async-start(bf16[64,4,256]{2,0,1:T(8,128)(2,1)} %bitcast.93), calls=%async_computation.1 | async-start | bytes 262144 | tf_op jit(solution)/shard_map/all_to_all | solution.py:54
  50.4 0.1 copy.65
  50.5 6.2 %all-to-all-done.1 = bf16[64,4,256]{2,0,1:T(8,128)(2,1)S(1)} async-done(((bf16[64,4,256]{2,0,1:T(8,128)(2,1)}), bf16[64,4,256]{2,0,1:T(8,128)(2,1)S(1)}, u32[]{:S(2)}, u32[]{:S(2)}) %all-to-all-start.1) | async-done | bytes 131104 | tf_op jit(solution)/shard_map/all_to_all | solution.py:54
  56.8 0.0 all-gather.3.cloned.1.call-done
  56.8 33.3 %all-gather.5.cloned.1.call-done = bf16[2048,1024]{0,1:T(8,128)(2,1)} async-done(((bf16[256,1024]{0,1:T(8,128)(2,1)}), bf16[2048,1024]{0,1:T(8,128)(2,1)}) %all-gather.5.cloned.1.call-update) | async-done | bytes 4194320 | tf_op jit(solution)/shard_map/all_gather | solution.py:82
  90.2 34.1 %while.17 = (s32[]{:T(128)}, f32[256,2,128]{0,2,1:T(8,128)S(1)}, f32[256,2,128]{0,2,1:T(8,128)S(1)}, bf16[2,1024,1024]{1,2,0:T(8,128)(2,1)}, s32[2]{0:T(128)S(1)...) while((s32[]{:T(128)}, f32[256,2,128]{0,2,1:T(8,128)S(1)}, ...), condition=%wide.region_3.4_spmd.clone, body=%wide.region_1.3_spmd.clone.sunk | while | flops 2708091904 | bytes 96986472 | solution.py:104
  90.2 0.6 dynamic_slice.49
  91.4 0.1 select_reduce_fusion.2
  91.6 0.2 broadcast_compare_fusion.2
  91.8 2.7 %constant_dynamic-slice_fusion.3 = (bf16[1024,1024]{0,1:T(8,128)(2,1)S(1)}, bf16[1024,1024]{0,1:T(8,128)(2,1)S(1)}) fusion(bf16[2048,1024]{0,1:T(8,128)(2,1)} %get-tuple-element.431, s32[]{:T(128)S(6)} %select_n.86, bf16[2048,1024]{0,1:T(8,128)(2,1)} %get-tuple-element.426), kind=kLoop, calls=%fused_computation.39.clone.1 | loop fusion | bytes 8388612 | tf_op jit(solution)/shard_map/while/body/eval_jaxpr/dynamic_slice | solution.py:90
  94.5 1.3 fusion.61
  95.8 2.0 %fusion.65 = f32[256,2,128]{0,2,1:T(8,128)S(1)} fusion(bf16[1024,2,4,128]{0,3,2,1:T(8,128)(2,1)S(1)} %bitcast.138, f32[2,1024,4,256]{3,1,2,0:T(8,128)S(1)} %fusion.61, f32[2,4,1024]{2,1,0:T(4,128)S(1)} %sub.96, pred[1024,256]{1,0:T(8,128)(4,1)S(1)} %broadcast_compare_fusion.2, f32[256,2,128]{0,2,1:T(8,128)S(1)} %get-tuple-element.406, pred[]{:T(512)S(6)} %compare.15), kind=kOutput, calls=%fused_computation.15.clone.1 | convolution fusion | flops 545390592 | bytes 11304961 | tf_op jit(solution)/shard_map/while/body/eval_jaxpr/grtn,tgrd->ngd/dot_general | solution.py:34
  97.8 4.2 %fusion.63 = bf16[2,4,1024,256]{3,2,1,0:T(8,128)(2,1)S(1)} fusion(f32[2,1024,4,256]{3,1,2,0:T(8,128)S(1)} %fusion.61, f32[2,4,1024]{2,1,0:T(4,128)S(1)} %sub.95, f32[2,4,1024]{2,1,0:T(4,128)S(1)} %sub.96, pred[1024,256]{1,0:T(8,128)(4,1)S(1)} %broadcast_compare_fusion.2, bf16[1024,2,4,128]{0,3,2,1:T(8,128)(2,1)S(1)} %bitcast.139, ...), kind=kOutput, calls=%fused_computation.2.clone.1 | convolution fusion | flops 549453824 | bytes 15138816 | tf_op jit(solution)/shard_map/while/body/eval_jaxpr/tgrd,ngd->grtn/dot_general | solution.py:24
  102.0 0.7 fusion.64
  102.8 1.5 convolution_multiply_fusion.2
  104.3 0.7 copy-done
  105.0 0.3 constant_dynamic-update-slice_fusion.2
  105.3 2.0 %copy-done.1 = bf16[2,1024,1024]{1,2,0:T(8,128)(2,1)} copy-done((bf16[2,1024,1024]{1,2,0:T(8,128)(2,1)}, bf16[2,1024,1024]{1,2,0:T(8,128)(2,1)S(1)}, u32[]{:S(2)}) %copy-start.1) | copy-done | bytes 4194328 | tf_op jit(solution)/shard_map/while
  107.2 0.6 dynamic_slice.49
  108.5 0.1 select_reduce_fusion.2
  108.7 0.2 broadcast_compare_fusion.2
  108.9 2.7 %constant_dynamic-slice_fusion.3 = (bf16[1024,1024]{0,1:T(8,128)(2,1)S(1)}, bf16[1024,1024]{0,1:T(8,128)(2,1)S(1)}) fusion(bf16[2048,1024]{0,1:T(8,128)(2,1)} %get-tuple-element.431, s32[]{:T(128)S(6)} %select_n.86, bf16[2048,1024]{0,1:T(8,128)(2,1)} %get-tuple-element.426), kind=kLoop, calls=%fused_computation.39.clone.1 | loop fusion | bytes 8388612 | tf_op jit(solution)/shard_map/while/body/eval_jaxpr/dynamic_slice | solution.py:90
  111.5 1.3 fusion.61
  112.8 2.0 %fusion.65 = f32[256,2,128]{0,2,1:T(8,128)S(1)} fusion(bf16[1024,2,4,128]{0,3,2,1:T(8,128)(2,1)S(1)} %bitcast.138, f32[2,1024,4,256]{3,1,2,0:T(8,128)S(1)} %fusion.61, f32[2,4,1024]{2,1,0:T(4,128)S(1)} %sub.96, pred[1024,256]{1,0:T(8,128)(4,1)S(1)} %broadcast_compare_fusion.2, f32[256,2,128]{0,2,1:T(8,128)S(1)} %get-tuple-element.406, pred[]{:T(512)S(6)} %compare.15), kind=kOutput, calls=%fused_computation.15.clone.1 | convolution fusion | flops 545390592 | bytes 11304961 | tf_op jit(solution)/shard_map/while/body/eval_jaxpr/grtn,tgrd->ngd/dot_general | solution.py:34
  114.8 4.2 %fusion.63 = bf16[2,4,1024,256]{3,2,1,0:T(8,128)(2,1)S(1)} fusion(f32[2,1024,4,256]{3,1,2,0:T(8,128)S(1)} %fusion.61, f32[2,4,1024]{2,1,0:T(4,128)S(1)} %sub.95, f32[2,4,1024]{2,1,0:T(4,128)S(1)} %sub.96, pred[1024,256]{1,0:T(8,128)(4,1)S(1)} %broadcast_compare_fusion.2, bf16[1024,2,4,128]{0,3,2,1:T(8,128)(2,1)S(1)} %bitcast.139, ...), kind=kOutput, calls=%fused_computation.2.clone.1 | convolution fusion | flops 549453824 | bytes 15138816 | tf_op jit(solution)/shard_map/while/body/eval_jaxpr/tgrd,ngd->grtn/dot_general | solution.py:24
  119.1 0.7 fusion.64
  119.8 1.5 convolution_multiply_fusion.2
  121.3 0.7 copy-done
  122.0 0.3 constant_dynamic-update-slice_fusion.2
  122.3 2.0 %copy-done.1 = bf16[2,1024,1024]{1,2,0:T(8,128)(2,1)} copy-done((bf16[2,1024,1024]{1,2,0:T(8,128)(2,1)}, bf16[2,1024,1024]{1,2,0:T(8,128)(2,1)S(1)}, u32[]{:S(2)}) %copy-start.1) | copy-done | bytes 4194328 | tf_op jit(solution)/shard_map/while
  124.3 6.2 %copy.68 = bf16[2,1024,1024]{2,1,0:T(8,128)(2,1)} copy(bf16[2,1024,1024]{1,2,0:T(8,128)(2,1)} %get-tuple-element.169) | data formatting | bytes 8388608 | tf_op jit(solution)/shard_map/convert_element_type | solution.py:110
  130.5 0.0 reduce-scatter.2.cloned.1.call-update
  130.5 0.1 copy.69
  130.6 0.7 convert_element_type.43
  131.4 4.6 %all-to-all-start.2 = ((bf16[4,64,256]{2,1,0:T(8,128)(2,1)}), bf16[4,64,256]{2,1,0:T(8,128)(2,1)S(1)}, u32[]{:S(2)}, u32[]{:S(2)}) async-start(bf16[4,64,256]{2,1,0:T(8,128)(2,1)} %convert_element_type.43), calls=%async_computation.3 | async-start | bytes 262144 | tf_op jit(solution)/shard_map/all_to_all | solution.py:117
  136.0 0.1 copy.71
  136.1 0.7 convert_element_type.45
  136.9 5.4 %all-to-all-done.2 = bf16[4,64,256]{2,1,0:T(8,128)(2,1)S(1)} async-done(((bf16[4,64,256]{2,1,0:T(8,128)(2,1)}), bf16[4,64,256]{2,1,0:T(8,128)(2,1)S(1)}, u32[]{:S(2)}, u32[]{:S(2)}) %all-to-all-start.2) | async-done | bytes 131104 | tf_op jit(solution)/shard_map/all_to_all | solution.py:117
  142.3 3.3 %all-to-all-start.3 = ((bf16[4,64,256]{2,1,0:T(8,128)(2,1)}), bf16[4,64,256]{2,1,0:T(8,128)(2,1)S(1)}, u32[]{:S(2)}, u32[]{:S(2)}) async-start(bf16[4,64,256]{2,1,0:T(8,128)(2,1)} %convert_element_type.45), calls=%async_computation.4 | async-start | bytes 262144 | tf_op jit(solution)/shard_map/all_to_all | solution.py:118
  145.6 0.7 copy.84
  146.3 5.2 %all-to-all-done.3 = bf16[4,64,256]{2,1,0:T(8,128)(2,1)S(1)} async-done(((bf16[4,64,256]{2,1,0:T(8,128)(2,1)}), bf16[4,64,256]{2,1,0:T(8,128)(2,1)S(1)}, u32[]{:S(2)}, u32[]{:S(2)}) %all-to-all-start.3) | async-done | bytes 131104 | tf_op jit(solution)/shard_map/all_to_all | solution.py:118
  151.5 0.7 copy.85
  152.2 29.6 %reduce-scatter.2.cloned.1.call-done = bf16[256,1024]{1,0:T(8,128)(2,1)} async-done(((bf16[2048,1024]{1,0:T(8,128)(2,1)}), bf16[256,1024]{1,0:T(8,128)(2,1)}) %reduce-scatter.2.cloned.1.call-update) | async-done | bytes 524304 | tf_op jit(solution)/shard_map/reduce_scatter | solution.py:109
  (31 shorter events, 0.3 us)
Async XLA Ops:
  7.2 16.5 %copy-start.2 = (bf16[256,1024]{1,0:T(8,128)(2,1)S(1)}, bf16[256,1024]{1,0:T(8,128)(2,1)}, u32[]{:S(2)}) copy-start(bf16[256,1024]{1,0:T(8,128)(2,1)} %param.13) | copy-start | bytes 1572868
  7.2 16.5 %copy-start.3 = (bf16[256,1024]{1,0:T(8,128)(2,1)S(1)}, bf16[256,1024]{1,0:T(8,128)(2,1)}, u32[]{:S(2)}) copy-start(bf16[256,1024]{1,0:T(8,128)(2,1)} %param.12) | copy-start | bytes 1572868
  7.2 49.7 %all-gather.3.cloned.1.call-start = ((), (), s32[]{:S(2)}) async-start(), calls=%async_computation.5 | async-start | bytes 4718592 | tf_op jit(solution)/shard_map/all_gather | solution.py:81
  9.4 80.8 %all-gather.5.cloned.1.call-start = ((), (), s32[]{:S(2)}) async-start(), calls=%async_computation.6 | async-start | bytes 4718592 | tf_op jit(solution)/shard_map/all_gather | solution.py:82
  11.5 25.4 %copy-start.5 = (f32[8,256]{1,0:T(8,128)S(1)}, f32[8,256]{1,0:T(8,128)}, u32[]{:S(2)}) copy-start(f32[8,256]{1,0:T(8,128)} %param.14) | copy-start | bytes 24580
  13.1 32.2 %all-to-all-start = ((bf16[64,4,256]{2,0,1:T(8,128)(2,1)}), bf16[64,4,256]{2,0,1:T(8,128)(2,1)S(1)}, u32[]{:S(2)}, u32[]{:S(2)}) async-start(bf16[64,4,256]{2,0,1:T(8,128)(2,1)} %bitcast.94), calls=%async_computation | async-start | bytes 262144 | tf_op jit(solution)/shard_map/all_to_all | solution.py:53
  23.7 66.5 %copy-start.4 = (s32[16]{0:T(128)S(1)}, s32[16]{0:T(128)}, u32[]{:S(2)}) copy-start(s32[16]{0:T(128)} %param.15) | copy-start | bytes 196
  45.3 11.4 %all-to-all-start.1 = ((bf16[64,4,256]{2,0,1:T(8,128)(2,1)}), bf16[64,4,256]{2,0,1:T(8,128)(2,1)S(1)}, u32[]{:S(2)}, u32[]{:S(2)}) async-start(bf16[64,4,256]{2,0,1:T(8,128)(2,1)} %bitcast.93), calls=%async_computation.1 | async-start | bytes 262144 | tf_op jit(solution)/shard_map/all_to_all | solution.py:54
  50.3 131.5 %reduce-scatter.2.cloned.1.call-start = ((), (), s32[]{:S(2)}) async-start(), calls=%async_computation.7 | async-start | bytes 4718592 | tf_op jit(solution)/shard_map/reduce_scatter | solution.py:109
  102.8 2.2 %copy-start = (bf16[2,1024,1024]{1,2,0:T(8,128)(2,1)S(1)}, bf16[2,1024,1024]{1,2,0:T(8,128)(2,1)}, u32[]{:S(2)}) copy-start(bf16[2,1024,1024]{1,2,0:T(8,128)(2,1)} %get-tuple-element.407) | copy-start | bytes 12582916 | tf_op jit(solution)/shard_map/while
  105.3 2.0 %copy-start.1 = (bf16[2,1024,1024]{1,2,0:T(8,128)(2,1)}, bf16[2,1024,1024]{1,2,0:T(8,128)(2,1)S(1)}, u32[]{:S(2)}) copy-start(bf16[2,1024,1024]{1,2,0:T(8,128)(2,1)S(1)} %constant_dynamic-update-slice_fusion.2) | copy-start | bytes 12582916 | tf_op jit(solution)/shard_map/while
  119.8 2.2 %copy-start = (bf16[2,1024,1024]{1,2,0:T(8,128)(2,1)S(1)}, bf16[2,1024,1024]{1,2,0:T(8,128)(2,1)}, u32[]{:S(2)}) copy-start(bf16[2,1024,1024]{1,2,0:T(8,128)(2,1)} %get-tuple-element.407) | copy-start | bytes 12582916 | tf_op jit(solution)/shard_map/while
  122.3 2.0 %copy-start.1 = (bf16[2,1024,1024]{1,2,0:T(8,128)(2,1)}, bf16[2,1024,1024]{1,2,0:T(8,128)(2,1)S(1)}, u32[]{:S(2)}) copy-start(bf16[2,1024,1024]{1,2,0:T(8,128)(2,1)S(1)} %constant_dynamic-update-slice_fusion.2) | copy-start | bytes 12582916 | tf_op jit(solution)/shard_map/while
  131.4 10.9 %all-to-all-start.2 = ((bf16[4,64,256]{2,1,0:T(8,128)(2,1)}), bf16[4,64,256]{2,1,0:T(8,128)(2,1)S(1)}, u32[]{:S(2)}, u32[]{:S(2)}) async-start(bf16[4,64,256]{2,1,0:T(8,128)(2,1)} %convert_element_type.43), calls=%async_computation.3 | async-start | bytes 262144 | tf_op jit(solution)/shard_map/all_to_all | solution.py:117
  142.3 9.2 %all-to-all-start.3 = ((bf16[4,64,256]{2,1,0:T(8,128)(2,1)}), bf16[4,64,256]{2,1,0:T(8,128)(2,1)S(1)}, u32[]{:S(2)}, u32[]{:S(2)}) async-start(bf16[4,64,256]{2,1,0:T(8,128)(2,1)} %convert_element_type.45), calls=%async_computation.4 | async-start | bytes 262144 | tf_op jit(solution)/shard_map/all_to_all | solution.py:118
Sparse Core Ops, SparseCore 0:
  10.4 40.4 all-gather.2
  52.8 37.3 all-gather.4
  130.6 51.1 reduce-scatter.1
where the time goes:
time: 189 us; the launch traced here: 188 us
  waiting for transfers between devices  79.9 us (42%)
  local copies, waits for them, and re-layouts  31.1 us (16%)
  blocking collectives  20.6 us (11%)
  matrix products  19.5 us (10%)
  starting transfers between devices  19.4 us (10%)
  between operations  15.1 us (8%)
    all_gather x1, waiting for transfers between devices, local(): dout_piece = lax.all_gather(out_grad, 'seq', axis=0, tiled=True)  33.3 us
    reduce_scatter x1, waiting for transfers between devices, local(): lax.psum_scatter(grad_q_all.astype(jnp.bfloat16), 'seq', scatter_dimensio...  29.6 us
    all_gather x1, blocking collectives, local(): lax.all_gather(delta, 'seq', axis=0, tiled=True)  12.3 us
    dot_general x2, matrix products, masked_terms(): jnp.einsum('tgrd,ngd->grtn', dout_blk, v_blk, preferred_element_type=jnp....  8.49 us
    all_gather x1, blocking collectives, local(): lax.all_gather(log_norm.T, 'seq', axis=0, tiled=True)  8.37 us
    all_to_all x1, starting transfers between devices, local(): lax.all_to_all(keys, 'head', split_axis=1, concat_axis=0, tiled=True)  6.35 us
    all_to_all x1, waiting for transfers between devices, local(): lax.all_to_all(values, 'head', split_axis=1, concat_axis=0, tiled=True)  6.25 us
    convert_element_type x1, local copies, waits for them, and re-layouts, local(): grad_q_all.astype(jnp.bfloat16)  6.2 us
  transfers between devices with their start and end apart: 7, of which 5 were waited for; matrix products, arithmetic and copies ran while one was open for 6% of the time, Pallas kernels for 0%

commit v1 on v0

v1 whole, which is shorter than its diff:
```python
import functools

import jax
import jax.numpy as jnp
from jax import lax
from jax.experimental import pallas as pl
from jax.experimental.pallas import tpu as pltpu
from jax.sharding import Mesh
from jax.sharding import PartitionSpec as P


QUERY_HEADS = 32
KEY_VALUE_HEADS = 8
HEAD_SIZE = 128
LOG2E = 1.4426950408889634
SCALE = HEAD_SIZE ** (-0.5)
RATIO = QUERY_HEADS // KEY_VALUE_HEADS


VMEM = pl.BlockSpec(memory_space=pltpu.VMEM)
SMEM = pl.BlockSpec(memory_space=pltpu.SMEM)


def sds(shape, dtype):
    return jax.ShapeDtypeStruct(shape, dtype)


def cost(flops, size):
    return pl.CostEstimate(flops=int(flops), bytes_accessed=int(size), transcendentals=0)


def near(x):
    return pltpu.with_memory_space_constraint(x, pltpu.VMEM)


def params(mib=16):
    return pltpu.CompilerParams(vmem_limit_bytes=mib << 20)


def pack_kernel(where, keys, values, *outs):
    core, z = where[1], where[2]
    for m, out in enumerate(outs):
        group = jnp.bitwise_xor(z, m)
        for j in range(2):
            col = (2 * group + jnp.bitwise_xor(core, j)) * HEAD_SIZE
            col = pl.multiple_of(col, HEAD_SIZE)
            out[j, 0] = keys[:, pl.ds(col, HEAD_SIZE)]
            out[j, 1] = values[:, pl.ds(col, HEAD_SIZE)]


def pack(where, keys, values, n_heads):
    shape = (2, 2, keys.shape[0], HEAD_SIZE)
    return pl.pallas_call(
        pack_kernel,
        in_specs=[SMEM, VMEM, VMEM],
        out_specs=[VMEM] * n_heads,
        out_shape=[pltpu.VMEM(shape, keys.dtype)] * n_heads,
        compiler_params=params(8),
        cost_estimate=cost(1e6, 4 * keys.size * 2),
        name="pack_kv",
    )(where, keys, values)


def prepare_kernel(where, q, do, o, lse, q_own, do_own, stats_own, q_send, do_send, stats_send):
    core = where[1]
    half = q.shape[0] // 2
    rows = []
    for h in range(lse.shape[0]):
        a = do[:, h * HEAD_SIZE : (h + 1) * HEAD_SIZE].astype(jnp.float32)
        b = o[:, h * HEAD_SIZE : (h + 1) * HEAD_SIZE].astype(jnp.float32)
        rows.append(jnp.sum((a * b).T, axis=0, keepdims=True))
    scaled = lse[...] * LOG2E
    low = jnp.concatenate([scaled[:RATIO]] + rows[:RATIO], 0)
    high = jnp.concatenate([scaled[RATIO:]] + rows[RATIO:], 0)
    stats_own[...] = jnp.where(core == 0, low, high)
    stats_send[...] = jnp.where(core == 0, high, low)

    def copy(first, q_out, do_out):
        for b in range(2):
            for h in range(RATIO):
                src = (slice(b * half, (b + 1) * half), slice((first + h) * HEAD_SIZE, (first + h + 1) * HEAD_SIZE))
                dst = slice((b * RATIO + h) * half, (b * RATIO + h + 1) * half)
                q_out[dst, :] = q[src]
                do_out[dst, :] = do[src]

    @pl.when(core == 0)
    def _():
        copy(0, q_own, do_own)
        copy(RATIO, q_send, do_send)

    @pl.when(core != 0)
    def _():
        copy(RATIO, q_own, do_own)
        copy(0, q_send, do_send)


def prepare(where, q, do, o, lse):
    tok = q.shape[0]
    part = pltpu.VMEM((tok * RATIO, HEAD_SIZE), q.dtype)
    stats = pltpu.VMEM((2 * RATIO, tok), jnp.float32)
    return pl.pallas_call(
        prepare_kernel,
        in_specs=[SMEM, VMEM, VMEM, VMEM, VMEM],
        out_specs=[VMEM] * 6,
        out_shape=[part, part, stats] * 2,
        compiler_params=params(16),
        cost_estimate=cost(1e7, 8 * q.size),
        name="prepare_q",
    )(where, q, do, o, lse)


def assemble_kernel(n_slots, *refs):
    out = refs[-1]
    for s in range(n_slots):
        out[s] = refs[s][0]
        out[n_slots + s] = refs[n_slots + s][1]


def assemble(mine, theirs):
    n_slots = len(mine)
    shape = (2 * n_slots,) + mine[0].shape[1:]
    return pl.pallas_call(
        functools.partial(assemble_kernel, n_slots),
        in_specs=[VMEM] * (2 * n_slots),
        out_specs=VMEM,
        out_shape=pltpu.VMEM(shape, mine[0].dtype),
        compiler_params=params(8),
        cost_estimate=cost(1e6, 1e6),
        name="assemble",
    )(*[near(x) for x in mine], *[near(x) for x in theirs])


def chunk_kernel(m, slots, first, where, order, q0, do0, stats0, q1, do1, stats1, kv, *rest):
    acc, dkv = rest[-2:]
    c, core, z = where[0], where[1], where[2]
    n_slots = len(slots)
    piece = kv.shape[2]
    half = stats0.shape[1] // 2
    width = RATIO * half
    per_block = half // piece
    other = jnp.bitwise_xor(c, m)
    starts = []
    for j in range(2):
        for slot in slots:
            source = jnp.bitwise_xor(z, slot)
            block = order[(other * 2 + jnp.bitwise_xor(core, j)) * 2 + source // per_block]
            starts.append(block * half + (source % per_block) * piece)
    row = lax.broadcasted_iota(jnp.int32, (piece, half), 0)
    lane = lax.broadcasted_iota(jnp.int32, (piece, half), 1)
    k = jnp.concatenate([kv[p, 0] for p in range(2 * n_slots)], 0)
    v = jnp.concatenate([kv[p, 1] for p in range(2 * n_slots)], 0)
    kt = k.T
    nt = (((1,), (1,)), ((), ()))
    dk = dv = None
    for b in range(4):
        q_ref, do_ref, stats = (q0, do0, stats0) if b < 2 else (q1, do1, stats1)
        i = b % 2
        lo = order[(c * 2 + jnp.bitwise_xor(core, b // 2)) * 2 + i] * half
        qs = q_ref[i * width : (i + 1) * width, :]
        dos = do_ref[i * width : (i + 1) * width, :]
        s = lax.dot_general(k, qs, nt, preferred_element_type=jnp.float32)
        dp = lax.dot_general(v, dos, nt, preferred_element_type=jnp.float32)
        visible = jnp.concatenate([row - lane for _ in starts], 0) <= jnp.concatenate(
            [jnp.full((piece, half), lo - start, jnp.int32) for start in starts], 0
        )
        probs, scores = [], []
        for h in range(RATIO):
            cols = slice(h * half, (h + 1) * half)
            lse = stats[h : h + 1, i * half : (i + 1) * half]
            delta = stats[RATIO + h : RATIO + h + 1, i * half : (i + 1) * half]
            p = jnp.where(visible, jnp.exp2(s[:, cols] * (SCALE * LOG2E) - lse), 0.0)
            probs.append(p.astype(jnp.bfloat16))
            scores.append((p * (dp[:, cols] - delta)).astype(jnp.bfloat16))
        prob = jnp.concatenate(probs, 1)
        score = jnp.concatenate(scores, 1)
        dv_b = jnp.dot(prob, dos, preferred_element_type=jnp.float32)
        dk_b = jnp.dot(score, qs, preferred_element_type=jnp.float32)
        dv = dv_b if dv is None else dv + dv_b
        dk = dk_b if dk is None else dk + dk_b
        dq = jnp.dot(kt, score, preferred_element_type=jnp.float32)
        if first:
            acc[:, b * width : (b + 1) * width] = dq
        else:
            acc[:, b * width : (b + 1) * width] = rest[0][:, b * width : (b + 1) * width] + dq
    for p in range(2 * n_slots):
        dkv[p, 0] = (dk[p * piece : (p + 1) * piece] * SCALE).astype(dkv.dtype)
        dkv[p, 1] = dv[p * piece : (p + 1) * piece].astype(dkv.dtype)


def chunk(m, slots, where, order, q_side, kv, acc, out_dtype):
    first = acc is None
    width = q_side[0].shape[0] * 2
    acc_out = pltpu.VMEM((HEAD_SIZE, width), jnp.float32)
    args = [near(x) for x in q_side] + [near(kv)] + ([] if first else [near(acc)])
    rows = kv.shape[0] * kv.shape[2]
    return pl.pallas_call(
        functools.partial(chunk_kernel, m, slots, first),
        in_specs=[SMEM, SMEM] + [VMEM] * len(args),
        out_specs=[VMEM] * 2,
        out_shape=[acc_out, pltpu.VMEM(kv.shape, out_dtype)],
        input_output_aliases={} if first else {len(args) + 1: 0},
        compiler_params=params(20),
        cost_estimate=cost(5 * 2 * rows * width * HEAD_SIZE * 2, 4 * kv.size),
        name="chunk",
    )(where, order, *args)


def finish_kernel(acc, dq_own, dq_send):
    half = dq_own.shape[0] // 2
    width = RATIO * half
    for b in range(4):
        out = dq_own if b < 2 else dq_send
        for h in range(RATIO):
            c = b * width + h * half
            block = (acc[:, c : c + half] * SCALE).T.astype(out.dtype)
            out[(b % 2) * half : (b % 2 + 1) * half, h * HEAD_SIZE : (h + 1) * HEAD_SIZE] = block


def finish(acc, tok, cols):
    out = pltpu.VMEM((tok, cols), jnp.bfloat16)
    return pl.pallas_call(
        finish_kernel,
        in_specs=[VMEM],
        out_specs=[VMEM] * 2,
        out_shape=[out, out],
        compiler_params=params(8),
        cost_estimate=cost(1e6, 6 * acc.size),
        name="finish_q",
    )(near(acc))


def place_kernel(where, mine, theirs, out):
    cols = mine.shape[1]

    @pl.when(where[1] == 0)
    def _():
        out[:, :cols] = mine[...]
        out[:, cols:] = theirs[...]

    @pl.when(where[1] != 0)
    def _():
        out[:, cols:] = mine[...]
        out[:, :cols] = theirs[...]


def place(where, mine, theirs):
    tok, cols = mine.shape
    return pl.pallas_call(
        place_kernel,
        in_specs=[SMEM, VMEM, VMEM],
        out_specs=VMEM,
        out_shape=sds((tok, 2 * cols), mine.dtype),
        compiler_params=params(8),
        cost_estimate=cost(1e6, 8 * mine.size),
        name="place_q",
    )(where, near(mine), near(theirs))


def collect_kernel(n_slots, own, *refs):
    received, outs = refs[: len(refs) - n_slots], refs[len(refs) - n_slots :]
    for s, out in enumerate(outs):
        for j in range(2):
            total = own[j * n_slots + s]
            for r in received:
                total = total + r[j * n_slots + s].astype(jnp.float32)
            out[j] = total.astype(out.dtype)


def collect(own, received):
    n_slots = own.shape[0] // 2
    shape = pltpu.VMEM((2,) + own.shape[1:], jnp.bfloat16)
    return pl.pallas_call(
        functools.partial(collect_kernel, n_slots),
        in_specs=[VMEM] * (1 + len(received)),
        out_specs=[VMEM] * n_slots,
        out_shape=[shape] * n_slots,
        compiler_params=params(8),
        cost_estimate=cost(1e6, 8 * own.size),
        name="collect",
    )(near(own), *[near(r) for r in received])


def unpack_kernel(n, where, *refs):
    core, z = where[1], where[2]
    mine, theirs, dk, dv = refs[:n], refs[n : 2 * n], refs[2 * n], refs[2 * n + 1]
    for m in range(n):
        group = jnp.bitwise_xor(z, m)
        for j, piece in enumerate((mine[m].at[0], theirs[m].at[1])):
            col = (2 * group + jnp.bitwise_xor(core, j)) * HEAD_SIZE
            col = pl.multiple_of(col, HEAD_SIZE)
            dk[:, pl.ds(col, HEAD_SIZE)] = piece[0]
            dv[:, pl.ds(col, HEAD_SIZE)] = piece[1]


def unpack(where, mine, theirs):
    n = len(mine)
    piece = mine[0].shape[2]
    out = sds((piece, KEY_VALUE_HEADS * HEAD_SIZE), jnp.bfloat16)
    return pl.pallas_call(
        functools.partial(unpack_kernel, n),
        in_specs=[SMEM] + [VMEM] * (2 * n),
        out_specs=[VMEM] * 2,
        out_shape=[out] * 2,
        compiler_params=params(8),
        cost_estimate=cost(1e6, 8 * piece * 1024),
        name="unpack_kv",
    )(where, *[near(x) for x in mine], *[near(x) for x in theirs])


def exchange(x, axis, size, m):
    return lax.ppermute(x, axis, [(i, i ^ m) for i in range(size)])


def local(n_chips, n_heads, queries, keys, values, outputs, out_grad, log_norm, block_order):
    where = jnp.stack([lax.axis_index("chip"), lax.axis_index("core"), lax.axis_index("head")])
    tok, cols = queries.shape
    halves = [tuple(m for m in range(n_heads) if m % 2 == a) for a in range(2)]

    zs = pack(where, keys, values, n_heads)
    order = [m for a in halves for m in a if m]
    zr = {0: zs[0]}
    for m in order:
        zr[m] = exchange(zs[m], "head", n_heads, m)
    own_side = prepare(where, queries, out_grad, outputs, log_norm)
    q_side = list(own_side[:3]) + [exchange(x, "core", 2, 1) for x in own_side[3:]]

    kvs = []
    for slots in halves:
        cr = [exchange(zr[m], "core", 2, 1) for m in slots]
        kv = assemble([zr[m] for m in slots], cr)
        kvs.append([kv] + [exchange(kv, "chip", n_chips, m) for m in range(1, n_chips)])

    acc = None
    back, theirs = {}, {}
    for slots, pieces in zip(halves, kvs):
        received = []
        for m in range(n_chips):
            acc, dkv = chunk(
                m, slots, where, block_order, q_side, pieces[m], acc,
                jnp.bfloat16 if m else jnp.float32,
            )
            if m:
                received.append(exchange(dkv, "chip", n_chips, m))
            else:
                own = dkv
        for m, x in zip(slots, collect(own, received)):
            back[m] = exchange(x, "head", n_heads, m) if m else x
            theirs[m] = exchange(back[m], "core", 2, 1)
    dq_own, dq_send = finish(acc, tok, cols // 2)
    dq = place(where, dq_own, exchange(dq_send, "core", 2, 1))
    dk, dv = unpack(where, [back[m] for m in range(n_heads)], [theirs[m] for m in range(n_heads)])
    return dq, dk, dv


def solution(mesh):
    n_seq, n_heads = mesh.shape["seq"], mesh.shape["head"]
    n_chips = n_seq // 2
    fine = Mesh(mesh.devices.reshape(n_chips, 2, n_heads), ("chip", "core", "head"))
    seq = ("chip", "core")
    rows, tokens = P(seq, "head"), P(("chip", "core", "head"), None)
    in_specs = (rows, tokens, tokens, rows, rows, P("head", seq), P())
    out_specs = (rows, tokens, tokens)

    def body(*args):
        return local(n_chips, n_heads, *args)

    return jax.shard_map(body, mesh=fine, in_specs=in_specs, out_specs=out_specs, check_vma=False)
```

time: 189 us -> 71.1 us (0.38)
  waiting for transfers between devices: 79.9 us -> 18.1 us
  local copies, waits for them, and re-layouts: 31.1 us -> 4.4 us
  Pallas kernels: 0 us -> 22.1 us
  blocking collectives: 20.6 us -> 0 us
  matrix products: 19.5 us -> 0 us
  between operations: 15.1 us -> 0.85 us
  starting transfers between devices: 19.4 us -> 25.4 us
    all_gather x2 -> x0, waiting for transfers between devices: 33.4 us -> none  [the longest x1 33.3 us: local(): dout_piece = lax.all_gather(out_grad, 'seq', axis=0, tiled=True)]
    reduce_scatter x1 -> x0, waiting for transfers between devices: 29.6 us -> none  [local(): lax.psum_scatter(grad_q_all.astype(jnp.bfloat16), 'seq', scatter_dimensio...]
    ppermute x0 -> x30, starting transfers between devices: none -> 25.4 us  [exchange(): return lax.ppermute(x, axis, [(i, i ^ m) for i in range(size)])]
    pallas_call x0 -> x17, Pallas kernels: none -> 22.1 us  [the longest x8 17.4 us: chunk(): pl.pallas_call(functools.partial(chunk_kernel, m, slots, first), in_specs...]
    all_gather x2 -> x0, blocking collectives: 20.6 us -> none  [the longest x1 12.3 us: local(): lax.all_gather(delta, 'seq', axis=0, tiled=True)]
    dot_general x10 -> x0, matrix products: 19.5 us -> none  [the longest x2 8.49 us: masked_terms(): jnp.einsum('tgrd,ngd->grtn', dout_blk, v_blk, preferred_element_type=jnp....]
    all_to_all x4 -> x0, starting transfers between devices: 19.3 us -> none  [the longest x1 6.35 us: local(): lax.all_to_all(keys, 'head', split_axis=1, concat_axis=0, tiled=True)]
    ppermute x0 -> x30, waiting for transfers between devices: none -> 18.1 us  [exchange(): return lax.ppermute(x, axis, [(i, i ^ m) for i in range(size)])]
  transfers between devices with their start and end apart: 7 -> 30, of which waited for: 5 -> 10; matrix products, arithmetic and copies ran while one was open for 6% -> 0% of each run, Pallas kernels for 0% -> 24%
where the time goes in v1:
time: 71.1 us; the launch traced here: 70.8 us
  starting transfers between devices  25.4 us (36%)
  Pallas kernels  22.1 us (31%)
  waiting for transfers between devices  18.1 us (25%)
  local copies, waits for them, and re-layouts  4.4 us (6%)
  between operations  0.85 us (1%)
    ppermute x30, starting transfers between devices, exchange(): return lax.ppermute(x, axis, [(i, i ^ m) for i in range(size)])  25.4 us
    ppermute x30, waiting for transfers between devices, exchange(): return lax.ppermute(x, axis, [(i, i ^ m) for i in range(size)])  18.1 us
    pallas_call x8, Pallas kernels, chunk(): pl.pallas_call(functools.partial(chunk_kernel, m, slots, first), in_specs...  17.4 us
    unnamed x14, local copies, waits for them, and re-layouts  4.4 us
  transfers between devices with their start and end apart: 30, of which 10 were waited for; matrix products, arithmetic and copies ran while one was open for 0% of the time, Pallas kernels for 24%

profile of v1, /device:TPU:0, one launch (start us, length us, event | category | flops | bytes accessed | tf_op | source)
XLA Modules:
  0.0 70.8 jit_solution(7656443519247794490)
XLA Ops:
  0.6 0.1 pad_add_fusion.where
  0.7 0.6 copy-done.5
  1.3 1.0 %copy-done = bf16[256,1024]{1,0:T(8,128)(2,1)S(1)} copy-done((bf16[256,1024]{1,0:T(8,128)(2,1)S(1)}, bf16[256,1024]{1,0:T(8,128)(2,1)}, u32[]{:S(2)}) %copy-start) | copy-done | bytes 524312
  2.4 1.0 %copy-done.1 = bf16[256,1024]{1,0:T(8,128)(2,1)S(1)} copy-done((bf16[256,1024]{1,0:T(8,128)(2,1)S(1)}, bf16[256,1024]{1,0:T(8,128)(2,1)}, u32[]{:S(2)}) %copy-start.1) | copy-done | bytes 524312
  3.4 1.0 %copy-done.2 = bf16[256,1024]{1,0:T(8,128)(2,1)S(1)} copy-done((bf16[256,1024]{1,0:T(8,128)(2,1)S(1)}, bf16[256,1024]{1,0:T(8,128)(2,1)}, u32[]{:S(2)}) %copy-start.2) | copy-done | bytes 524312
  4.5 1.0 %prepare_q.1 = (bf16[1024,128]{1,0:T(8,128)(2,1)S(1)}, bf16[1024,128]{1,0:T(8,128)(2,1)S(1)}, f32[8,256]{1,0:T(8,128)S(1)}, bf16[1024,128]{1,0:T(8,128)(2,1)S(1)...) custom-call(s32[3]{0:T(128)S(1)} %pad_add_fusion.where, bf16[256,1024]{1,0:T(8,128)(2,1)S(1)} %copy-done, ...), custom_call_target="tpu_custom_call" | custom-call | flops 10000000 | bytes 2097152 | tf_op jit(solution)/shard_map/prepare_q/pallas_call | solution.py:101
  5.5 0.6 collective-permute-start
  6.1 0.1 collective-permute-start.1
  6.2 0.6 pack_kv.1
  6.8 3.0 %collective-permute-start.3 = (bf16[2,2,64,128]{3,2,1,0:T(8,128)(2,1)S(1)}, bf16[2,2,64,128]{3,2,1,0:T(8,128)(2,1)S(1)}, u32[]{:S(2)}, u32[]{:S(2)}) collective-permute-start(bf16[2,2,64,128]{3,2,1,0:T(8,128)(2,1)S(1)} %get-tuple-element.43), channel_id=1, source_target_pairs={{0,1},{1,0},{2,3},{3,2},{4,5},{5,4},{6,7},{7,6},{8,9},{9,8},{10,11... | collective-permute-start | bytes 196616 | tf_op jit(solution)/shard_map/ppermute | solution.py:311
  9.8 2.6 %collective-permute-start.10 = (bf16[2,2,64,128]{3,2,1,0:T(8,128)(2,1)S(1)}, bf16[2,2,64,128]{3,2,1,0:T(8,128)(2,1)S(1)}, u32[]{:S(2)}, u32[]{:S(2)}) collective-permute-start(bf16[2,2,64,128]{3,2,1,0:T(8,128)(2,1)S(1)} %get-tuple-element.46), channel_id=1, source_target_pairs={{0,2},{1,3},{2,0},{3,1},{4,6},{5,7},{6,4},{7,5},{8,10},{9,11},{10,... | collective-permute-start | bytes 196616 | tf_op jit(solution)/shard_map/ppermute | solution.py:311
  12.4 0.0 collective-permute-start.4
  12.4 0.0 collective-permute-done.3.refs_0_
  12.4 0.0 collective-permute-start.11
  12.4 4.9 %collective-permute-done.10.refs_1_ = bf16[2,2,64,128]{3,2,1,0:T(8,128)(2,1)S(1)} collective-permute-done((bf16[2,2,64,128]{3,2,1,0:T(8,128)(2,1)S(1)}, bf16[2,2,64,128]{3,2,1,0:T(8,128)(2,1)S(1)}, u32[]{:S(2)}, u32[]{:S(2)}) %collective-permute-start.10) | collective-permute-done | bytes 65568 | tf_op jit(solution)/shard_map/ppermute | solution.py:311
  17.3 1.3 %collective-permute-done.4.refs_1_ = bf16[2,2,64,128]{3,2,1,0:T(8,128)(2,1)S(1)} collective-permute-done((bf16[2,2,64,128]{3,2,1,0:T(8,128)(2,1)S(1)}, bf16[2,2,64,128]{3,2,1,0:T(8,128)(2,1)S(1)}, u32[]{:S(2)}, u32[]{:S(2)}) %collective-permute-start.4) | collective-permute-done | bytes 65568 | tf_op jit(solution)/shard_map/ppermute | solution.py:311
  18.6 0.0 collective-permute-done.11.refs_2_
  18.6 0.5 collective-permute-start.6
  19.1 0.0 collective-permute-done.12.refs_3_
  19.1 0.1 collective-permute-start.2
  19.2 0.7 collective-permute-done.5.refs_2_
  19.9 1.5 %collective-permute-start.15 = (bf16[4,2,64,128]{3,2,1,0:T(8,128)(2,1)S(1)}, bf16[4,2,64,128]{3,2,1,0:T(8,128)(2,1)S(1)}, u32[]{:S(2)}, u32[]{:S(2)}) collective-permute-start(bf16[4,2,64,128]{3,2,1,0:T(8,128)(2,1)S(1)} %assemble.3.kv), channel_id=1, source_target_pairs={{0,8},{8,0},{16,24},{24,16},{1,9},{9,1},{17,25},{25,17},{2,10},{10... | collective-permute-start | bytes 393224 | tf_op jit(solution)/shard_map/ppermute | solution.py:311
  21.3 1.5 %collective-permute-start.14 = (bf16[4,2,64,128]{3,2,1,0:T(8,128)(2,1)S(1)}, bf16[4,2,64,128]{3,2,1,0:T(8,128)(2,1)S(1)}, u32[]{:S(2)}, u32[]{:S(2)}) collective-permute-start(bf16[4,2,64,128]{3,2,1,0:T(8,128)(2,1)S(1)} %assemble.3.kv), channel_id=1, source_target_pairs={{0,16},{8,24},{16,0},{24,8},{1,17},{9,25},{17,1},{25,9},{2,18},{10... | collective-permute-start | bytes 393224 | tf_op jit(solution)/shard_map/ppermute | solution.py:311
  22.9 0.0 collective-permute-done.2.stats1
  22.9 0.5 collective-permute-start.13
  23.4 1.5 %collective-permute-start.9 = (bf16[4,2,64,128]{3,2,1,0:T(8,128)(2,1)S(1)}, bf16[4,2,64,128]{3,2,1,0:T(8,128)(2,1)S(1)}, u32[]{:S(2)}, u32[]{:S(2)}) collective-permute-start(bf16[4,2,64,128]{3,2,1,0:T(8,128)(2,1)S(1)} %assemble.2.kv), channel_id=1, source_target_pairs={{0,8},{8,0},{16,24},{24,16},{1,9},{9,1},{17,25},{25,17},{2,10},{10... | collective-permute-start | bytes 393224 | tf_op jit(solution)/shard_map/ppermute | solution.py:311
  24.9 0.0 collective-permute-done.1.do1
  24.9 1.5 %collective-permute-start.8 = (bf16[4,2,64,128]{3,2,1,0:T(8,128)(2,1)S(1)}, bf16[4,2,64,128]{3,2,1,0:T(8,128)(2,1)S(1)}, u32[]{:S(2)}, u32[]{:S(2)}) collective-permute-start(bf16[4,2,64,128]{3,2,1,0:T(8,128)(2,1)S(1)} %assemble.2.kv), channel_id=1, source_target_pairs={{0,16},{8,24},{16,0},{24,8},{1,17},{9,25},{17,1},{25,9},{2,18},{10... | collective-permute-start | bytes 393224 | tf_op jit(solution)/shard_map/ppermute | solution.py:311
  26.5 0.7 copy-done.6
  27.1 2.1 %chunk.8 = (f32[128,2048]{1,0:T(8,128)S(1)}, f32[4,2,64,128]{3,2,1,0:T(8,128)S(1)}) custom-call(s32[3]{0:T(128)S(1)} %pad_add_fusion.where, s32[16]{0:T(128)S(1)} %copy-done.6, bf16[1024,128]{1,0:T(8,128)(2,1)S(1)} %get-tuple-element.37.q0, bf16[1024,128]{1,0:T(8,128)(2,1)S(1)} %get-tuple-element.38.do0, f32[8,256]{1,0:T(8,128)S(1)} %get-tuple-element.39.stats0, ...), custom_call_target="tpu_custom_call" | custom-call | flops 1342177280 | bytes 262144 | tf_op jit(solution)/shard_map/chunk/pallas_call | solution.py:196
  29.2 0.0 collective-permute-done.15.kv
  29.2 0.5 collective-permute-start.7
  29.8 2.2 %chunk.9 = (f32[128,2048]{1,0:T(8,128)S(1)}, bf16[4,2,64,128]{3,2,1,0:T(8,128)(2,1)S(1)}) custom-call(s32[3]{0:T(128)S(1)} %pad_add_fusion.where, s32[16]{0:T(128)S(1)} %copy-done.6, bf16[1024,128]{1,0:T(8,128)(2,1)S(1)} %get-tuple-element.37.q0, bf16[1024,128]{1,0:T(8,128)(2,1)S(1)} %get-tuple-element.38.do0, ...), custom_call_target="tpu_custom_call", output_to_operand_aliasing={{0}: (9, {})} | custom-call | flops 1342177280 | bytes 262144 | tf_op jit(solution)/shard_map/chunk/pallas_call | solution.py:196
  31.9 2.2 %chunk.10 = (f32[128,2048]{1,0:T(8,128)S(1)}, bf16[4,2,64,128]{3,2,1,0:T(8,128)(2,1)S(1)}) custom-call(s32[3]{0:T(128)S(1)} %pad_add_fusion.where, s32[16]{0:T(128)S(1)} %copy-done.6, bf16[1024,128]{1,0:T(8,128)(2,1)S(1)} %get-tuple-element.37.q0, bf16[1024,128]{1,0:T(8,128)(2,1)S(1)} %get-tuple-element.38.do0, ...), custom_call_target="tpu_custom_call", output_to_operand_aliasing={{0}: (9, {})} | custom-call | flops 1342177280 | bytes 262144 | tf_op jit(solution)/shard_map/chunk/pallas_call | solution.py:196
  34.1 0.0 collective-permute-done.13.kv
  34.1 2.2 %chunk.11 = (f32[128,2048]{1,0:T(8,128)S(1)}, bf16[4,2,64,128]{3,2,1,0:T(8,128)(2,1)S(1)}) custom-call(s32[3]{0:T(128)S(1)} %pad_add_fusion.where, s32[16]{0:T(128)S(1)} %copy-done.6, bf16[1024,128]{1,0:T(8,128)(2,1)S(1)} %get-tuple-element.37.q0, bf16[1024,128]{1,0:T(8,128)(2,1)S(1)} %get-tuple-element.38.do0, ...), custom_call_target="tpu_custom_call", output_to_operand_aliasing={{0}: (9, {})} | custom-call | flops 1342177280 | bytes 262144 | tf_op jit(solution)/shard_map/chunk/pallas_call | solution.py:196
  36.3 2.2 %chunk.12 = (f32[128,2048]{1,0:T(8,128)S(1)}, f32[4,2,64,128]{3,2,1,0:T(8,128)S(1)}) custom-call(s32[3]{0:T(128)S(1)} %pad_add_fusion.where, s32[16]{0:T(128)S(1)} %copy-done.6, bf16[1024,128]{1,0:T(8,128)(2,1)S(1)} %get-tuple-element.37.q0, bf16[1024,128]{1,0:T(8,128)(2,1)S(1)} %get-tuple-element.38.do0, ...), custom_call_target="tpu_custom_call", output_to_operand_aliasing={{0}: (9, {})} | custom-call | flops 1342177280 | bytes 262144 | tf_op jit(solution)/shard_map/chunk/pallas_call | solution.py:196
  38.5 0.0 collective-permute-done.9.kv
  38.5 2.2 %chunk.13 = (f32[128,2048]{1,0:T(8,128)S(1)}, bf16[4,2,64,128]{3,2,1,0:T(8,128)(2,1)S(1)}) custom-call(s32[3]{0:T(128)S(1)} %pad_add_fusion.where, s32[16]{0:T(128)S(1)} %copy-done.6, bf16[1024,128]{1,0:T(8,128)(2,1)S(1)} %get-tuple-element.37.q0, bf16[1024,128]{1,0:T(8,128)(2,1)S(1)} %get-tuple-element.38.do0, ...), custom_call_target="tpu_custom_call", output_to_operand_aliasing={{0}: (9, {})} | custom-call | flops 1342177280 | bytes 262144 | tf_op jit(solution)/shard_map/chunk/pallas_call | solution.py:196
  40.6 0.0 collective-permute-done.8.kv
  40.6 2.2 %chunk.14 = (f32[128,2048]{1,0:T(8,128)S(1)}, bf16[4,2,64,128]{3,2,1,0:T(8,128)(2,1)S(1)}) custom-call(s32[3]{0:T(128)S(1)} %pad_add_fusion.where, s32[16]{0:T(128)S(1)} %copy-done.6, bf16[1024,128]{1,0:T(8,128)(2,1)S(1)} %get-tuple-element.37.q0, bf16[1024,128]{1,0:T(8,128)(2,1)S(1)} %get-tuple-element.38.do0, ...), custom_call_target="tpu_custom_call", output_to_operand_aliasing={{0}: (9, {})} | custom-call | flops 1342177280 | bytes 262144 | tf_op jit(solution)/shard_map/chunk/pallas_call | solution.py:196
  42.8 2.4 %chunk.15 = (f32[128,2048]{1,0:T(8,128)S(1)}, bf16[4,2,64,128]{3,2,1,0:T(8,128)(2,1)S(1)}) custom-call(s32[3]{0:T(128)S(1)} %pad_add_fusion.where, s32[16]{0:T(128)S(1)} %copy-done.6, bf16[1024,128]{1,0:T(8,128)(2,1)S(1)} %get-tuple-element.37.q0, bf16[1024,128]{1,0:T(8,128)(2,1)S(1)} %get-tuple-element.38.do0, ...), custom_call_target="tpu_custom_call", output_to_operand_aliasing={{0}: (9, {})} | custom-call | flops 1342177280 | bytes 262144 | tf_op jit(solution)/shard_map/chunk/pallas_call | solution.py:196
  45.2 2.5 %collective-permute-start.22 = (bf16[4,2,64,128]{3,2,1,0:T(8,128)(2,1)S(1)}, bf16[4,2,64,128]{3,2,1,0:T(8,128)(2,1)S(1)}, u32[]{:S(2)}, u32[]{:S(2)}) collective-permute-start(bf16[4,2,64,128]{3,2,1,0:T(8,128)(2,1)S(1)} %get-tuple-element.65), channel_id=1, source_target_pairs={{0,24},{8,16},{16,8},{24,0},{1,25},{9,17},{17,9},{25,1},{2,26},{10... | collective-permute-start | bytes 393224 | tf_op jit(solution)/shard_map/ppermute | solution.py:311
  47.7 0.5 collective-permute-start.21
  48.2 0.5 collective-permute-start.20
  48.7 2.5 %collective-permute-start.19 = (bf16[4,2,64,128]{3,2,1,0:T(8,128)(2,1)S(1)}, bf16[4,2,64,128]{3,2,1,0:T(8,128)(2,1)S(1)}, u32[]{:S(2)}, u32[]{:S(2)}) collective-permute-start(bf16[4,2,64,128]{3,2,1,0:T(8,128)(2,1)S(1)} %get-tuple-element.60), channel_id=1, source_target_pairs={{0,24},{8,16},{16,8},{24,0},{1,25},{9,17},{17,9},{25,1},{2,26},{10... | collective-permute-start | bytes 393224 | tf_op jit(solution)/shard_map/ppermute | solution.py:311
  51.2 0.5 collective-permute-start.18
  51.7 0.9 %collective-permute-done.22.refs_2_ = bf16[4,2,64,128]{3,2,1,0:T(8,128)(2,1)S(1)} collective-permute-done((bf16[4,2,64,128]{3,2,1,0:T(8,128)(2,1)S(1)}, bf16[4,2,64,128]{3,2,1,0:T(8,128)(2,1)S(1)}, u32[]{:S(2)}, u32[]{:S(2)}) %collective-permute-start.22) | collective-permute-done | bytes 131104 | tf_op jit(solution)/shard_map/ppermute | solution.py:311
  52.6 1.5 %collective-permute-start.17 = (bf16[4,2,64,128]{3,2,1,0:T(8,128)(2,1)S(1)}, bf16[4,2,64,128]{3,2,1,0:T(8,128)(2,1)S(1)}, u32[]{:S(2)}, u32[]{:S(2)}) collective-permute-start(bf16[4,2,64,128]{3,2,1,0:T(8,128)(2,1)S(1)} %get-tuple-element.58), channel_id=1, source_target_pairs={{0,8},{8,0},{16,24},{24,16},{1,9},{9,1},{17,25},{25,17},{2,10},{10... | collective-permute-start | bytes 393224 | tf_op jit(solution)/shard_map/ppermute | solution.py:311
  54.1 0.2 finish_q.1
  54.3 2.2 %collective-permute-done.21.refs_1_ = bf16[4,2,64,128]{3,2,1,0:T(8,128)(2,1)S(1)} collective-permute-done((bf16[4,2,64,128]{3,2,1,0:T(8,128)(2,1)S(1)}, bf16[4,2,64,128]{3,2,1,0:T(8,128)(2,1)S(1)}, u32[]{:S(2)}, u32[]{:S(2)}) %collective-permute-start.21) | collective-permute-done | bytes 131104 | tf_op jit(solution)/shard_map/ppermute | solution.py:311
  56.5 0.1 collect.3
  56.6 0.9 %collective-permute-start.23 = (bf16[2,2,64,128]{3,2,1,0:T(8,128)(2,1)S(1)}, bf16[2,2,64,128]{3,2,1,0:T(8,128)(2,1)S(1)}, u32[]{:S(2)}, u32[]{:S(2)}) collective-permute-start(bf16[2,2,64,128]{3,2,1,0:T(8,128)(2,1)S(1)} %get-tuple-element.66), channel_id=1, source_target_pairs={{0,1},{1,0},{2,3},{3,2},{4,5},{5,4},{6,7},{7,6},{8,9},{9,8},{10,11... | collective-permute-start | bytes 196616 | tf_op jit(solution)/shard_map/ppermute | solution.py:311
  57.5 0.7 %collective-permute-done.19.refs_2_ = bf16[4,2,64,128]{3,2,1,0:T(8,128)(2,1)S(1)} collective-permute-done((bf16[4,2,64,128]{3,2,1,0:T(8,128)(2,1)S(1)}, bf16[4,2,64,128]{3,2,1,0:T(8,128)(2,1)S(1)}, u32[]{:S(2)}, u32[]{:S(2)}) %collective-permute-start.19) | collective-permute-done | bytes 131104 | tf_op jit(solution)/shard_map/ppermute | solution.py:311
  58.2 2.1 %collective-permute-start.25 = (bf16[2,2,64,128]{3,2,1,0:T(8,128)(2,1)S(1)}, bf16[2,2,64,128]{3,2,1,0:T(8,128)(2,1)S(1)}, u32[]{:S(2)}, u32[]{:S(2)}) collective-permute-start(bf16[2,2,64,128]{3,2,1,0:T(8,128)(2,1)S(1)} %get-tuple-element.68), channel_id=1, source_target_pairs={{0,3},{1,2},{2,1},{3,0},{4,7},{5,6},{6,5},{7,4},{8,11},{9,10},{10,... | collective-permute-start | bytes 196616 | tf_op jit(solution)/shard_map/ppermute | solution.py:311
  60.3 0.1 collect.2
  60.4 0.3 collective-permute-start.24
  60.7 0.5 collective-permute-done.23.refs_1_
  61.2 0.0 collective-permute-start.27
  61.2 3.3 %collective-permute-done.25.refs_3_ = bf16[2,2,64,128]{3,2,1,0:T(8,128)(2,1)S(1)} collective-permute-done((bf16[2,2,64,128]{3,2,1,0:T(8,128)(2,1)S(1)}, bf16[2,2,64,128]{3,2,1,0:T(8,128)(2,1)S(1)}, u32[]{:S(2)}, u32[]{:S(2)}) %collective-permute-start.25) | collective-permute-done | bytes 65568 | tf_op jit(solution)/shard_map/ppermute | solution.py:311
  64.6 2.3 %collective-permute-done.24.refs_2_ = bf16[2,2,64,128]{3,2,1,0:T(8,128)(2,1)S(1)} collective-permute-done((bf16[2,2,64,128]{3,2,1,0:T(8,128)(2,1)S(1)}, bf16[2,2,64,128]{3,2,1,0:T(8,128)(2,1)S(1)}, u32[]{:S(2)}, u32[]{:S(2)}) %collective-permute-start.24) | collective-permute-done | bytes 65568 | tf_op jit(solution)/shard_map/ppermute | solution.py:311
  66.9 1.2 %collective-permute-done.28.refs_6_ = bf16[2,2,64,128]{3,2,1,0:T(8,128)(2,1)S(1)} collective-permute-done((bf16[2,2,64,128]{3,2,1,0:T(8,128)(2,1)S(1)}, bf16[2,2,64,128]{3,2,1,0:T(8,128)(2,1)S(1)}, u32[]{:S(2)}, u32[]{:S(2)}) %collective-permute-start.28) | collective-permute-done | bytes 65568 | tf_op jit(solution)/shard_map/ppermute | solution.py:311
  68.2 1.3 %unpack_kv.1 = (bf16[64,1024]{1,0:T(8,128)(2,1)}, bf16[64,1024]{1,0:T(8,128)(2,1)}) custom-call(s32[3]{0:T(128)S(1)} %pad_add_fusion.where, bf16[2,2,64,128]{3,2,1,0:T(8,128)(2,1)S(1)} %get-tuple-element.61.refs_0_, bf16[2,2,64,128]{3,2,1,0:T(8,128)(2,1)S(1)} %collective-permute-done.23.refs_1_, bf16[2,2,64,128]{3,2,1,0:T(8,128)(2,1)S(1)} %collective-permute-done.24.refs_2_, ...), custom_call_target="tpu_custom_call" | custom-call | flops 1000000 | bytes 524288 | tf_op jit(solution)/shard_map/unpack_kv/pallas_call | solution.py:299
  69.5 1.4 %place_q.1 = bf16[256,1024]{1,0:T(8,128)(2,1)} custom-call(s32[3]{0:T(128)S(1)} %pad_add_fusion.where, bf16[256,512]{1,0:T(8,128)(2,1)S(1)} %get-tuple-element.55.mine, bf16[256,512]{1,0:T(8,128)(2,1)S(1)} %collective-permute-done.16.theirs), custom_call_target="tpu_custom_call" | custom-call | flops 1000000 | bytes 1048576 | tf_op jit(solution)/shard_map/place_q/pallas_call | solution.py:248
  (28 shorter events, 0.1 us)
Async XLA Ops:
  0.6 0.7 copy-start.5
  1.3 1.0 %copy-start = (bf16[256,1024]{1,0:T(8,128)(2,1)S(1)}, bf16[256,1024]{1,0:T(8,128)(2,1)}, u32[]{:S(2)}) copy-start(bf16[256,1024]{1,0:T(8,128)(2,1)} %q.1) | copy-start | bytes 1572868
  2.4 1.0 %copy-start.1 = (bf16[256,1024]{1,0:T(8,128)(2,1)S(1)}, bf16[256,1024]{1,0:T(8,128)(2,1)}, u32[]{:S(2)}) copy-start(bf16[256,1024]{1,0:T(8,128)(2,1)} %do.1) | copy-start | bytes 1572868
  3.4 1.0 %copy-start.2 = (bf16[256,1024]{1,0:T(8,128)(2,1)S(1)}, bf16[256,1024]{1,0:T(8,128)(2,1)}, u32[]{:S(2)}) copy-start(bf16[256,1024]{1,0:T(8,128)(2,1)} %o.1) | copy-start | bytes 1572868
  4.5 1.7 %copy-start.3 = (bf16[64,1024]{1,0:T(8,128)(2,1)S(1)}, bf16[64,1024]{1,0:T(8,128)(2,1)}, u32[]{:S(2)}) copy-start(bf16[64,1024]{1,0:T(8,128)(2,1)} %keys.1) | copy-start | bytes 393220
  4.5 1.7 %copy-start.4 = (bf16[64,1024]{1,0:T(8,128)(2,1)S(1)}, bf16[64,1024]{1,0:T(8,128)(2,1)}, u32[]{:S(2)}) copy-start(bf16[64,1024]{1,0:T(8,128)(2,1)} %values.1) | copy-start | bytes 393220
  5.5 17.9 %collective-permute-start = (bf16[1024,128]{1,0:T(8,128)(2,1)S(1)}, bf16[1024,128]{1,0:T(8,128)(2,1)S(1)}, u32[]{:S(2)}, u32[]{:S(2)}) collective-permute-start(bf16[1024,128]{1,0:T(8,128)(2,1)S(1)} %get-tuple-element.40), channel_id=1, source_target_pairs={{0,4},{4,0},{1,5},{5,1},{2,6},{6,2},{3,7},{7,3},{8,12},{12,8},{9,1... | collective-permute-start | bytes 786440 | tf_op jit(solution)/shard_map/ppermute | solution.py:311
  6.1 18.8 %collective-permute-start.1 = (bf16[1024,128]{1,0:T(8,128)(2,1)S(1)}, bf16[1024,128]{1,0:T(8,128)(2,1)S(1)}, u32[]{:S(2)}, u32[]{:S(2)}) collective-permute-start(bf16[1024,128]{1,0:T(8,128)(2,1)S(1)} %get-tuple-element.41), channel_id=1, source_target_pairs={{0,4},{4,0},{1,5},{5,1},{2,6},{6,2},{3,7},{7,3},{8,12},{12,8},{9,1... | collective-permute-start | bytes 786440 | tf_op jit(solution)/shard_map/ppermute | solution.py:311
  6.8 5.6 %collective-permute-start.3 = (bf16[2,2,64,128]{3,2,1,0:T(8,128)(2,1)S(1)}, bf16[2,2,64,128]{3,2,1,0:T(8,128)(2,1)S(1)}, u32[]{:S(2)}, u32[]{:S(2)}) collective-permute-start(bf16[2,2,64,128]{3,2,1,0:T(8,128)(2,1)S(1)} %get-tuple-element.43), channel_id=1, source_target_pairs={{0,1},{1,0},{2,3},{3,2},{4,5},{5,4},{6,7},{7,6},{8,9},{9,8},{10,11... | collective-permute-start | bytes 196616 | tf_op jit(solution)/shard_map/ppermute | solution.py:311
  9.8 7.5 %collective-permute-start.10 = (bf16[2,2,64,128]{3,2,1,0:T(8,128)(2,1)S(1)}, bf16[2,2,64,128]{3,2,1,0:T(8,128)(2,1)S(1)}, u32[]{:S(2)}, u32[]{:S(2)}) collective-permute-start(bf16[2,2,64,128]{3,2,1,0:T(8,128)(2,1)S(1)} %get-tuple-element.46), channel_id=1, source_target_pairs={{0,2},{1,3},{2,0},{3,1},{4,6},{5,7},{6,4},{7,5},{8,10},{9,11},{10,... | collective-permute-start | bytes 196616 | tf_op jit(solution)/shard_map/ppermute | solution.py:311
  12.4 6.2 %collective-permute-start.4 = (bf16[2,2,64,128]{3,2,1,0:T(8,128)(2,1)S(1)}, bf16[2,2,64,128]{3,2,1,0:T(8,128)(2,1)S(1)}, u32[]{:S(2)}, u32[]{:S(2)}) collective-permute-start(bf16[2,2,64,128]{3,2,1,0:T(8,128)(2,1)S(1)} %get-tuple-element.44), channel_id=1, source_target_pairs={{0,3},{1,2},{2,1},{3,0},{4,7},{5,6},{6,5},{7,4},{8,11},{9,10},{10,... | collective-permute-start | bytes 196616 | tf_op jit(solution)/shard_map/ppermute | solution.py:311
  12.4 6.2 %collective-permute-start.11 = (bf16[2,2,64,128]{3,2,1,0:T(8,128)(2,1)S(1)}, bf16[2,2,64,128]{3,2,1,0:T(8,128)(2,1)S(1)}, u32[]{:S(2)}, u32[]{:S(2)}) collective-permute-start(bf16[2,2,64,128]{3,2,1,0:T(8,128)(2,1)S(1)} %get-tuple-element.45.refs_0_), channel_id=1, source_target_pairs={{0,4},{4,0},{1,5},{5,1},{2,6},{6,2},{3,7},{7,3},{8,12},{12,8},{9,1... | collective-permute-start | bytes 196616 | tf_op jit(solution)/shard_map/ppermute | solution.py:311
  17.3 1.8 %collective-permute-start.12 = (bf16[2,2,64,128]{3,2,1,0:T(8,128)(2,1)S(1)}, bf16[2,2,64,128]{3,2,1,0:T(8,128)(2,1)S(1)}, u32[]{:S(2)}, u32[]{:S(2)}) collective-permute-start(bf16[2,2,64,128]{3,2,1,0:T(8,128)(2,1)S(1)} %collective-permute-done.10.refs_1_), channel_id=1, source_target_pairs={{0,4},{4,0},{1,5},{5,1},{2,6},{6,2},{3,7},{7,3},{8,12},{12,8},{9,1... | collective-permute-start | bytes 196616 | tf_op jit(solution)/shard_map/ppermute | solution.py:311
  18.6 1.3 %collective-permute-start.5 = (bf16[2,2,64,128]{3,2,1,0:T(8,128)(2,1)S(1)}, bf16[2,2,64,128]{3,2,1,0:T(8,128)(2,1)S(1)}, u32[]{:S(2)}, u32[]{:S(2)}) collective-permute-start(bf16[2,2,64,128]{3,2,1,0:T(8,128)(2,1)S(1)} %collective-permute-done.3.refs_0_), channel_id=1, source_target_pairs={{0,4},{4,0},{1,5},{5,1},{2,6},{6,2},{3,7},{7,3},{8,12},{12,8},{9,1... | collective-permute-start | bytes 196616 | tf_op jit(solution)/shard_map/ppermute | solution.py:311
  18.6 2.7 %collective-permute-start.6 = (bf16[2,2,64,128]{3,2,1,0:T(8,128)(2,1)S(1)}, bf16[2,2,64,128]{3,2,1,0:T(8,128)(2,1)S(1)}, u32[]{:S(2)}, u32[]{:S(2)}) collective-permute-start(bf16[2,2,64,128]{3,2,1,0:T(8,128)(2,1)S(1)} %collective-permute-done.4.refs_1_), channel_id=1, source_target_pairs={{0,4},{4,0},{1,5},{5,1},{2,6},{6,2},{3,7},{7,3},{8,12},{12,8},{9,1... | collective-permute-start | bytes 196616 | tf_op jit(solution)/shard_map/ppermute | solution.py:311
  19.1 3.8 %collective-permute-start.2 = (f32[8,256]{1,0:T(8,128)S(1)}, f32[8,256]{1,0:T(8,128)S(1)}, u32[]{:S(2)}, u32[]{:S(2)}) collective-permute-start(f32[8,256]{1,0:T(8,128)S(1)} %get-tuple-element.42), channel_id=1, source_target_pairs={{0,4},{4,0},{1,5},{5,1},{2,6},{6,2},{3,7},{7,3},{8,12},{12,8},{9,1... | collective-permute-start | bytes 24584 | tf_op jit(solution)/shard_map/ppermute | solution.py:311
  19.9 9.4 %collective-permute-start.15 = (bf16[4,2,64,128]{3,2,1,0:T(8,128)(2,1)S(1)}, bf16[4,2,64,128]{3,2,1,0:T(8,128)(2,1)S(1)}, u32[]{:S(2)}, u32[]{:S(2)}) collective-permute-start(bf16[4,2,64,128]{3,2,1,0:T(8,128)(2,1)S(1)} %assemble.3.kv), channel_id=1, source_target_pairs={{0,8},{8,0},{16,24},{24,16},{1,9},{9,1},{17,25},{25,17},{2,10},{10... | collective-permute-start | bytes 393224 | tf_op jit(solution)/shard_map/ppermute | solution.py:311
  21.3 10.6 %collective-permute-start.14 = (bf16[4,2,64,128]{3,2,1,0:T(8,128)(2,1)S(1)}, bf16[4,2,64,128]{3,2,1,0:T(8,128)(2,1)S(1)}, u32[]{:S(2)}, u32[]{:S(2)}) collective-permute-start(bf16[4,2,64,128]{3,2,1,0:T(8,128)(2,1)S(1)} %assemble.3.kv), channel_id=1, source_target_pairs={{0,16},{8,24},{16,0},{24,8},{1,17},{9,25},{17,1},{25,9},{2,18},{10... | collective-permute-start | bytes 393224 | tf_op jit(solution)/shard_map/ppermute | solution.py:311
  22.9 11.2 %collective-permute-start.13 = (bf16[4,2,64,128]{3,2,1,0:T(8,128)(2,1)S(1)}, bf16[4,2,64,128]{3,2,1,0:T(8,128)(2,1)S(1)}, u32[]{:S(2)}, u32[]{:S(2)}) collective-permute-start(bf16[4,2,64,128]{3,2,1,0:T(8,128)(2,1)S(1)} %assemble.3.kv), channel_id=1, source_target_pairs={{0,24},{8,16},{16,8},{24,0},{1,25},{9,17},{17,9},{25,1},{2,26},{10... | collective-permute-start | bytes 393224 | tf_op jit(solution)/shard_map/ppermute | solution.py:311
  23.4 15.0 %collective-permute-start.9 = (bf16[4,2,64,128]{3,2,1,0:T(8,128)(2,1)S(1)}, bf16[4,2,64,128]{3,2,1,0:T(8,128)(2,1)S(1)}, u32[]{:S(2)}, u32[]{:S(2)}) collective-permute-start(bf16[4,2,64,128]{3,2,1,0:T(8,128)(2,1)S(1)} %assemble.2.kv), channel_id=1, source_target_pairs={{0,8},{8,0},{16,24},{24,16},{1,9},{9,1},{17,25},{25,17},{2,10},{10... | collective-permute-start | bytes 393224 | tf_op jit(solution)/shard_map/ppermute | solution.py:311
  24.9 15.7 %collective-permute-start.8 = (bf16[4,2,64,128]{3,2,1,0:T(8,128)(2,1)S(1)}, bf16[4,2,64,128]{3,2,1,0:T(8,128)(2,1)S(1)}, u32[]{:S(2)}, u32[]{:S(2)}) collective-permute-start(bf16[4,2,64,128]{3,2,1,0:T(8,128)(2,1)S(1)} %assemble.2.kv), channel_id=1, source_target_pairs={{0,16},{8,24},{16,0},{24,8},{1,17},{9,25},{17,1},{25,9},{2,18},{10... | collective-permute-start | bytes 393224 | tf_op jit(solution)/shard_map/ppermute | solution.py:311
  26.5 0.7 copy-start.6
  29.2 13.6 %collective-permute-start.7 = (bf16[4,2,64,128]{3,2,1,0:T(8,128)(2,1)S(1)}, bf16[4,2,64,128]{3,2,1,0:T(8,128)(2,1)S(1)}, u32[]{:S(2)}, u32[]{:S(2)}) collective-permute-start(bf16[4,2,64,128]{3,2,1,0:T(8,128)(2,1)S(1)} %assemble.2.kv), channel_id=1, source_target_pairs={{0,24},{8,16},{16,8},{24,0},{1,25},{9,17},{17,9},{25,1},{2,26},{10... | collective-permute-start | bytes 393224 | tf_op jit(solution)/shard_map/ppermute | solution.py:311
  45.2 7.4 %collective-permute-start.22 = (bf16[4,2,64,128]{3,2,1,0:T(8,128)(2,1)S(1)}, bf16[4,2,64,128]{3,2,1,0:T(8,128)(2,1)S(1)}, u32[]{:S(2)}, u32[]{:S(2)}) collective-permute-start(bf16[4,2,64,128]{3,2,1,0:T(8,128)(2,1)S(1)} %get-tuple-element.65), channel_id=1, source_target_pairs={{0,24},{8,16},{16,8},{24,0},{1,25},{9,17},{17,9},{25,1},{2,26},{10... | collective-permute-start | bytes 393224 | tf_op jit(solution)/shard_map/ppermute | solution.py:311
  47.7 8.8 %collective-permute-start.21 = (bf16[4,2,64,128]{3,2,1,0:T(8,128)(2,1)S(1)}, bf16[4,2,64,128]{3,2,1,0:T(8,128)(2,1)S(1)}, u32[]{:S(2)}, u32[]{:S(2)}) collective-permute-start(bf16[4,2,64,128]{3,2,1,0:T(8,128)(2,1)S(1)} %get-tuple-element.64), channel_id=1, source_target_pairs={{0,16},{8,24},{16,0},{24,8},{1,17},{9,25},{17,1},{25,9},{2,18},{10... | collective-permute-start | bytes 393224 | tf_op jit(solution)/shard_map/ppermute | solution.py:311
  48.2 8.3 %collective-permute-start.20 = (bf16[4,2,64,128]{3,2,1,0:T(8,128)(2,1)S(1)}, bf16[4,2,64,128]{3,2,1,0:T(8,128)(2,1)S(1)}, u32[]{:S(2)}, u32[]{:S(2)}) collective-permute-start(bf16[4,2,64,128]{3,2,1,0:T(8,128)(2,1)S(1)} %get-tuple-element.63), channel_id=1, source_target_pairs={{0,8},{8,0},{16,24},{24,16},{1,9},{9,1},{17,25},{25,17},{2,10},{10... | collective-permute-start | bytes 393224 | tf_op jit(solution)/shard_map/ppermute | solution.py:311
  48.7 9.5 %collective-permute-start.19 = (bf16[4,2,64,128]{3,2,1,0:T(8,128)(2,1)S(1)}, bf16[4,2,64,128]{3,2,1,0:T(8,128)(2,1)S(1)}, u32[]{:S(2)}, u32[]{:S(2)}) collective-permute-start(bf16[4,2,64,128]{3,2,1,0:T(8,128)(2,1)S(1)} %get-tuple-element.60), channel_id=1, source_target_pairs={{0,24},{8,16},{16,8},{24,0},{1,25},{9,17},{17,9},{25,1},{2,26},{10... | collective-permute-start | bytes 393224 | tf_op jit(solution)/shard_map/ppermute | solution.py:311
  51.2 9.1 %collective-permute-start.18 = (bf16[4,2,64,128]{3,2,1,0:T(8,128)(2,1)S(1)}, bf16[4,2,64,128]{3,2,1,0:T(8,128)(2,1)S(1)}, u32[]{:S(2)}, u32[]{:S(2)}) collective-permute-start(bf16[4,2,64,128]{3,2,1,0:T(8,128)(2,1)S(1)} %get-tuple-element.59), channel_id=1, source_target_pairs={{0,16},{8,24},{16,0},{24,8},{1,17},{9,25},{17,1},{25,9},{2,18},{10... | collective-permute-start | bytes 393224 | tf_op jit(solution)/shard_map/ppermute | solution.py:311
  52.6 7.7 %collective-permute-start.17 = (bf16[4,2,64,128]{3,2,1,0:T(8,128)(2,1)S(1)}, bf16[4,2,64,128]{3,2,1,0:T(8,128)(2,1)S(1)}, u32[]{:S(2)}, u32[]{:S(2)}) collective-permute-start(bf16[4,2,64,128]{3,2,1,0:T(8,128)(2,1)S(1)} %get-tuple-element.58), channel_id=1, source_target_pairs={{0,8},{8,0},{16,24},{24,16},{1,9},{9,1},{17,25},{25,17},{2,10},{10... | collective-permute-start | bytes 393224 | tf_op jit(solution)/shard_map/ppermute | solution.py:311
  56.5 12.9 %collective-permute-start.16 = (bf16[256,512]{1,0:T(8,128)(2,1)S(1)}, bf16[256,512]{1,0:T(8,128)(2,1)S(1)}, u32[]{:S(2)}, u32[]{:S(2)}) collective-permute-start(bf16[256,512]{1,0:T(8,128)(2,1)S(1)} %get-tuple-element.56), channel_id=1, source_target_pairs={{0,4},{4,0},{1,5},{5,1},{2,6},{6,2},{3,7},{7,3},{8,12},{12,8},{9,1... | collective-permute-start | bytes 786440 | tf_op jit(solution)/shard_map/ppermute | solution.py:311
  56.6 4.6 %collective-permute-start.23 = (bf16[2,2,64,128]{3,2,1,0:T(8,128)(2,1)S(1)}, bf16[2,2,64,128]{3,2,1,0:T(8,128)(2,1)S(1)}, u32[]{:S(2)}, u32[]{:S(2)}) collective-permute-start(bf16[2,2,64,128]{3,2,1,0:T(8,128)(2,1)S(1)} %get-tuple-element.66), channel_id=1, source_target_pairs={{0,1},{1,0},{2,3},{3,2},{4,5},{5,4},{6,7},{7,6},{8,9},{9,8},{10,11... | collective-permute-start | bytes 196616 | tf_op jit(solution)/shard_map/ppermute | solution.py:311
  58.2 6.4 %collective-permute-start.25 = (bf16[2,2,64,128]{3,2,1,0:T(8,128)(2,1)S(1)}, bf16[2,2,64,128]{3,2,1,0:T(8,128)(2,1)S(1)}, u32[]{:S(2)}, u32[]{:S(2)}) collective-permute-start(bf16[2,2,64,128]{3,2,1,0:T(8,128)(2,1)S(1)} %get-tuple-element.68), channel_id=1, source_target_pairs={{0,3},{1,2},{2,1},{3,0},{4,7},{5,6},{6,5},{7,4},{8,11},{9,10},{10,... | collective-permute-start | bytes 196616 | tf_op jit(solution)/shard_map/ppermute | solution.py:311
  60.4 6.5 %collective-permute-start.24 = (bf16[2,2,64,128]{3,2,1,0:T(8,128)(2,1)S(1)}, bf16[2,2,64,128]{3,2,1,0:T(8,128)(2,1)S(1)}, u32[]{:S(2)}, u32[]{:S(2)}) collective-permute-start(bf16[2,2,64,128]{3,2,1,0:T(8,128)(2,1)S(1)} %get-tuple-element.67), channel_id=1, source_target_pairs={{0,2},{1,3},{2,0},{3,1},{4,6},{5,7},{6,4},{7,5},{8,10},{9,11},{10,... | collective-permute-start | bytes 196616 | tf_op jit(solution)/shard_map/ppermute | solution.py:311
  60.7 6.2 %collective-permute-start.26 = (bf16[2,2,64,128]{3,2,1,0:T(8,128)(2,1)S(1)}, bf16[2,2,64,128]{3,2,1,0:T(8,128)(2,1)S(1)}, u32[]{:S(2)}, u32[]{:S(2)}) collective-permute-start(bf16[2,2,64,128]{3,2,1,0:T(8,128)(2,1)S(1)} %get-tuple-element.61.refs_0_), channel_id=1, source_target_pairs={{0,4},{4,0},{1,5},{5,1},{2,6},{6,2},{3,7},{7,3},{8,12},{12,8},{9,1... | collective-permute-start | bytes 196616 | tf_op jit(solution)/shard_map/ppermute | solution.py:311
  61.2 5.7 %collective-permute-start.27 = (bf16[2,2,64,128]{3,2,1,0:T(8,128)(2,1)S(1)}, bf16[2,2,64,128]{3,2,1,0:T(8,128)(2,1)S(1)}, u32[]{:S(2)}, u32[]{:S(2)}) collective-permute-start(bf16[2,2,64,128]{3,2,1,0:T(8,128)(2,1)S(1)} %collective-permute-done.23.refs_1_), channel_id=1, source_target_pairs={{0,4},{4,0},{1,5},{5,1},{2,6},{6,2},{3,7},{7,3},{8,12},{12,8},{9,1... | collective-permute-start | bytes 196616 | tf_op jit(solution)/shard_map/ppermute | solution.py:311
  64.5 2.4 %collective-permute-start.29 = (bf16[2,2,64,128]{3,2,1,0:T(8,128)(2,1)S(1)}, bf16[2,2,64,128]{3,2,1,0:T(8,128)(2,1)S(1)}, u32[]{:S(2)}, u32[]{:S(2)}) collective-permute-start(bf16[2,2,64,128]{3,2,1,0:T(8,128)(2,1)S(1)} %collective-permute-done.25.refs_3_), channel_id=1, source_target_pairs={{0,4},{4,0},{1,5},{5,1},{2,6},{6,2},{3,7},{7,3},{8,12},{12,8},{9,1... | collective-permute-start | bytes 196616 | tf_op jit(solution)/shard_map/ppermute | solution.py:311
  66.9 1.3 %collective-permute-start.28 = (bf16[2,2,64,128]{3,2,1,0:T(8,128)(2,1)S(1)}, bf16[2,2,64,128]{3,2,1,0:T(8,128)(2,1)S(1)}, u32[]{:S(2)}, u32[]{:S(2)}) collective-permute-start(bf16[2,2,64,128]{3,2,1,0:T(8,128)(2,1)S(1)} %collective-permute-done.24.refs_2_), channel_id=1, source_target_pairs={{0,4},{4,0},{1,5},{5,1},{2,6},{6,2},{3,7},{7,3},{8,12},{12,8},{9,1... | collective-permute-start | bytes 196616 | tf_op jit(solution)/shard_map/ppermute | solution.py:311

commit v2 on v1

v2 whole, which is shorter than its diff:
```python
import functools

import jax
import jax.numpy as jnp
from jax import lax
from jax.experimental import pallas as pl
from jax.experimental.pallas import tpu as pltpu
from jax.sharding import Mesh
from jax.sharding import PartitionSpec as P


QUERY_HEADS = 32
KEY_VALUE_HEADS = 8
HEAD_SIZE = 128
LOG2E = 1.4426950408889634
SCALE = HEAD_SIZE ** (-0.5)
RATIO = QUERY_HEADS // KEY_VALUE_HEADS


VMEM = pl.BlockSpec(memory_space=pltpu.VMEM)
SMEM = pl.BlockSpec(memory_space=pltpu.SMEM)
ANY = pl.BlockSpec(memory_space=pl.ANY)


def sds(shape, dtype):
    return jax.ShapeDtypeStruct(shape, dtype)


def cost(flops, size):
    return pl.CostEstimate(flops=int(flops), bytes_accessed=int(size), transcendentals=0)


def near(x):
    return pltpu.with_memory_space_constraint(x, pltpu.VMEM)


def params(mib=16):
    return pltpu.CompilerParams(vmem_limit_bytes=mib << 20)


def far(x):
    return pltpu.with_memory_space_constraint(x, pltpu.HBM)


def columns(group):
    return pl.ds(pl.multiple_of(group * HEAD_SIZE, HEAD_SIZE), HEAD_SIZE)


def copy_all(copies, sems):
    started = [pltpu.make_async_copy(src, dst, sems.at[i]) for i, (src, dst) in enumerate(copies)]
    for copy in started:
        copy.start()
    return started


def pack_kernel(where, keys, values, *rest):
    outs, sems = rest[:-1], rest[-1]
    core, z = where[1], where[2]
    copies = []
    for m, out in enumerate(outs):
        group = jnp.bitwise_xor(z, m)
        for j in range(2):
            col = columns(2 * group + jnp.bitwise_xor(core, j))
            copies.append((keys.at[:, col], out.at[j, 0]))
            copies.append((values.at[:, col], out.at[j, 1]))
    for copy in copy_all(copies, sems):
        copy.wait()


def pack(where, keys, values, n_heads):
    shape = (2, 2, keys.shape[0], HEAD_SIZE)
    return pl.pallas_call(
        pack_kernel,
        in_specs=[SMEM, ANY, ANY],
        out_specs=[VMEM] * n_heads,
        out_shape=[pltpu.VMEM(shape, keys.dtype)] * n_heads,
        scratch_shapes=[pltpu.SemaphoreType.DMA((4 * n_heads,))],
        compiler_params=params(8),
        cost_estimate=cost(1e6, 4 * keys.size * 2),
        name="pack_kv",
    )(where, far(keys), far(values))


def prepare_kernel(where, q, do, o, lse, *rest):
    outs, (o_blocks, sems) = rest[:6], rest[6:]
    core = where[1]
    half = q.shape[0] // 2
    copies = []
    for side in range(2):
        first = jnp.bitwise_xor(core, side) * RATIO
        for b in range(2):
            for h in range(RATIO):
                src = (slice(b * half, (b + 1) * half), columns(first + h))
                i = b * RATIO + h
                dst = slice(i * half, (i + 1) * half)
                copies.append((do.at[src], outs[3 * side + 1].at[dst, :]))
                copies.append((o.at[src], o_blocks.at[side, dst, :]))
                copies.append((q.at[src], outs[3 * side].at[dst, :]))
    started = copy_all(copies, sems)
    scaled = lse[...] * LOG2E
    for side in range(2):
        own_low = jnp.bitwise_xor(core, side) == 0
        outs[3 * side + 2][:RATIO, :] = jnp.where(own_low, scaled[:RATIO], scaled[RATIO:])
    for copy in started:
        copy.wait()
    for side in range(2):
        do_ref, stats = outs[3 * side + 1], outs[3 * side + 2]
        for b in range(2):
            for h in range(RATIO):
                i = b * RATIO + h
                rows = slice(i * half, (i + 1) * half)
                prod = do_ref[rows, :].astype(jnp.float32) * o_blocks[side, rows, :].astype(jnp.float32)
                total = jnp.sum(prod.T, axis=0, keepdims=True)
                stats[RATIO + h : RATIO + h + 1, b * half : (b + 1) * half] = total


def prepare(where, q, do, o, lse):
    tok = q.shape[0]
    part = pltpu.VMEM((tok * RATIO, HEAD_SIZE), q.dtype)
    stats = pltpu.VMEM((2 * RATIO, tok), jnp.float32)
    return pl.pallas_call(
        prepare_kernel,
        in_specs=[SMEM, ANY, ANY, ANY, VMEM],
        out_specs=[VMEM] * 6,
        out_shape=[part, part, stats] * 2,
        scratch_shapes=[
            pltpu.VMEM((2, tok * RATIO, HEAD_SIZE), q.dtype),
            pltpu.SemaphoreType.DMA((12 * RATIO,)),
        ],
        compiler_params=params(8),
        cost_estimate=cost(1e7, 8 * q.size),
        name="prepare_q",
    )(where, far(q), far(do), far(o), lse)


def assemble_kernel(n_slots, *refs):
    out = refs[-1]
    for s in range(n_slots):
        out[s] = refs[s][0]
        out[n_slots + s] = refs[n_slots + s][1]


def assemble(mine, theirs):
    n_slots = len(mine)
    shape = (2 * n_slots,) + mine[0].shape[1:]
    return pl.pallas_call(
        functools.partial(assemble_kernel, n_slots),
        in_specs=[VMEM] * (2 * n_slots),
        out_specs=VMEM,
        out_shape=pltpu.VMEM(shape, mine[0].dtype),
        compiler_params=params(8),
        cost_estimate=cost(1e6, 1e6),
        name="assemble",
    )(*[near(x) for x in mine], *[near(x) for x in theirs])


def chunk_kernel(m, slots, n_heads, first, where, q0, do0, stats0, q1, do1, stats1, kv, *rest):
    acc, dkv = rest[-2:]
    c, core, z = where[0], where[1], where[2]
    piece = kv.shape[2]
    half = stats0.shape[1] // 2
    width = RATIO * half
    per_block = half // piece
    other = jnp.bitwise_xor(c, m)
    pieces = []
    for j in range(2):
        for slot in slots:
            source = jnp.bitwise_xor(z, slot)
            block = where[3 + (other * 2 + jnp.bitwise_xor(core, j)) * 2 + source // per_block]
            pieces.append((j * n_heads + slot, block * half + (source % per_block) * piece))
    per_tile = min(len(pieces), 256 // piece)
    tiles = [range(i, i + per_tile) for i in range(0, len(pieces), per_tile)]
    row = lax.broadcasted_iota(jnp.int32, (piece, half), 0)
    lane = lax.broadcasted_iota(jnp.int32, (piece, half), 1)
    offset = jnp.concatenate([row - lane] * per_tile, 0)
    ks = [jnp.concatenate([kv[pieces[p][0], 0] for p in t], 0) for t in tiles]
    vs = [jnp.concatenate([kv[pieces[p][0], 1] for p in t], 0) for t in tiles]
    kts = [k.T for k in ks]
    nt = (((1,), (1,)), ((), ()))
    dks, dvs = [None] * len(tiles), [None] * len(tiles)
    for b in range(4):
        q_ref, do_ref, stats = (q0, do0, stats0) if b < 2 else (q1, do1, stats1)
        i = b % 2
        lo = where[3 + (c * 2 + jnp.bitwise_xor(core, b // 2)) * 2 + i] * half
        qs = q_ref[i * width : (i + 1) * width, :]
        dos = do_ref[i * width : (i + 1) * width, :]
        dq = None if first else rest[0][:, b * width : (b + 1) * width]
        for t, tile in enumerate(tiles):
            s = lax.dot_general(ks[t], qs, nt, preferred_element_type=jnp.float32)
            dp = lax.dot_general(vs[t], dos, nt, preferred_element_type=jnp.float32)
            limits = [jnp.full((piece, half), lo - pieces[p][1], jnp.int32) for p in tile]
            visible = offset <= jnp.concatenate(limits, 0)
            probs, scores = [], []
            for h in range(RATIO):
                cols = slice(h * half, (h + 1) * half)
                lse = stats[h : h + 1, i * half : (i + 1) * half]
                delta = stats[RATIO + h : RATIO + h + 1, i * half : (i + 1) * half]
                p = jnp.where(visible, jnp.exp2(s[:, cols] * (SCALE * LOG2E) - lse), 0.0)
                probs.append(p.astype(jnp.bfloat16))
                scores.append((p * (dp[:, cols] - delta)).astype(jnp.bfloat16))
            prob = jnp.concatenate(probs, 1)
            score = jnp.concatenate(scores, 1)
            dv = jnp.dot(prob, dos, preferred_element_type=jnp.float32)
            dk = jnp.dot(score, qs, preferred_element_type=jnp.float32)
            dvs[t] = dv if dvs[t] is None else dvs[t] + dv
            dks[t] = dk if dks[t] is None else dks[t] + dk
            term = jnp.dot(kts[t], score, preferred_element_type=jnp.float32)
            dq = term if dq is None else dq + term
        acc[:, b * width : (b + 1) * width] = dq
    for t, tile in enumerate(tiles):
        for n, p in enumerate(tile):
            rows = slice(n * piece, (n + 1) * piece)
            dkv[p, 0] = (dks[t][rows] * SCALE).astype(dkv.dtype)
            dkv[p, 1] = dvs[t][rows].astype(dkv.dtype)


def chunk(m, slots, where, q_side, kv, acc, out_dtype):
    first = acc is None
    width = q_side[0].shape[0] * 2
    acc_out = pltpu.VMEM((HEAD_SIZE, width), jnp.float32)
    args = [near(x) for x in q_side] + [near(kv)] + ([] if first else [near(acc)])
    out = (2 * len(slots),) + kv.shape[1:]
    return pl.pallas_call(
        functools.partial(chunk_kernel, m, slots, kv.shape[0] // 2, first),
        in_specs=[SMEM] + [VMEM] * len(args),
        out_specs=[VMEM] * 2,
        out_shape=[acc_out, pltpu.VMEM(out, out_dtype)],
        input_output_aliases={} if first else {len(args): 0},
        compiler_params=params(20),
        cost_estimate=cost(5 * 2 * out[0] * out[2] * width * HEAD_SIZE * 2, 4 * kv.size),
        name="chunk",
    )(where, *args)


def finish_kernel(acc, dq_own, dq_send):
    half = dq_own.shape[0] // 2
    width = RATIO * half
    for b in range(4):
        out = dq_own if b < 2 else dq_send
        for h in range(RATIO):
            c = b * width + h * half
            block = (acc[:, c : c + half] * SCALE).T.astype(out.dtype)
            out[(b % 2) * half : (b % 2 + 1) * half, h * HEAD_SIZE : (h + 1) * HEAD_SIZE] = block


def finish(acc, tok, cols):
    out = pltpu.VMEM((tok, cols), jnp.bfloat16)
    return pl.pallas_call(
        finish_kernel,
        in_specs=[VMEM],
        out_specs=[VMEM] * 2,
        out_shape=[out, out],
        compiler_params=params(8),
        cost_estimate=cost(1e6, 6 * acc.size),
        name="finish_q",
    )(near(acc))


def place_kernel(where, mine, theirs, out):
    cols = mine.shape[1]

    @pl.when(where[1] == 0)
    def _():
        out[:, :cols] = mine[...]
        out[:, cols:] = theirs[...]

    @pl.when(where[1] != 0)
    def _():
        out[:, cols:] = mine[...]
        out[:, :cols] = theirs[...]


def place(where, mine, theirs):
    tok, cols = mine.shape
    return pl.pallas_call(
        place_kernel,
        in_specs=[SMEM, VMEM, VMEM],
        out_specs=VMEM,
        out_shape=sds((tok, 2 * cols), mine.dtype),
        compiler_params=params(8),
        cost_estimate=cost(1e6, 8 * mine.size),
        name="place_q",
    )(where, near(mine), near(theirs))


def collect_kernel(picks, own, *refs):
    n = len(picks[0]) // 2
    received, outs = refs[: len(refs) - n], refs[len(refs) - n :]
    for s, out in enumerate(outs):
        for j in range(2):
            total = own[picks[0][j * n + s]]
            for pick, r in zip(picks[1:], received):
                total = total + r[pick[j * n + s]].astype(jnp.float32)
            out[j] = total.astype(out.dtype)


def collect(picks, own, received):
    n = len(picks[0]) // 2
    shape = pltpu.VMEM((2,) + own.shape[1:], jnp.bfloat16)
    return pl.pallas_call(
        functools.partial(collect_kernel, picks),
        in_specs=[VMEM] * (1 + len(received)),
        out_specs=[VMEM] * n,
        out_shape=[shape] * n,
        compiler_params=params(8),
        cost_estimate=cost(1e6, 8 * own.size),
        name="collect",
    )(near(own), *[near(r) for r in received])


def unpack_kernel(n, where, *refs):
    core, z = where[1], where[2]
    mine, theirs, dk, dv = refs[:n], refs[n : 2 * n], refs[2 * n], refs[2 * n + 1]
    for m in range(n):
        group = jnp.bitwise_xor(z, m)
        for j, piece in enumerate((mine[m].at[0], theirs[m].at[1])):
            col = (2 * group + jnp.bitwise_xor(core, j)) * HEAD_SIZE
            col = pl.multiple_of(col, HEAD_SIZE)
            dk[:, pl.ds(col, HEAD_SIZE)] = piece[0]
            dv[:, pl.ds(col, HEAD_SIZE)] = piece[1]


def unpack(where, mine, theirs):
    n = len(mine)
    piece = mine[0].shape[2]
    out = sds((piece, KEY_VALUE_HEADS * HEAD_SIZE), jnp.bfloat16)
    return pl.pallas_call(
        functools.partial(unpack_kernel, n),
        in_specs=[SMEM] + [VMEM] * (2 * n),
        out_specs=[VMEM] * 2,
        out_shape=[out] * 2,
        compiler_params=params(8),
        cost_estimate=cost(1e6, 8 * piece * 1024),
        name="unpack_kv",
    )(where, *[near(x) for x in mine], *[near(x) for x in theirs])


def exchange(x, axis, size, m):
    return lax.ppermute(x, axis, [(i, i ^ m) for i in range(size)])


def slot_halves(n_heads):
    slots = sorted(range(n_heads), key=lambda m: (m % 2, m))
    return tuple(slots[: n_heads // 2]), tuple(slots[n_heads // 2 :])


def local(n_chips, n_heads, queries, keys, values, outputs, out_grad, log_norm, block_order):
    where = jnp.stack([lax.axis_index("chip"), lax.axis_index("core"), lax.axis_index("head")])
    tok, cols = queries.shape
    info = jnp.concatenate([where, block_order])
    every = tuple(range(n_heads))
    halves = slot_halves(n_heads)

    zs = pack(where, keys, values, n_heads)
    zr = {0: zs[0]}
    for m in range(1, n_heads):
        zr[m] = exchange(zs[m], "head", n_heads, m)
    own_side = prepare(where, queries, out_grad, outputs, log_norm)
    q_side = list(own_side[:3]) + [exchange(x, "core", 2, 1) for x in own_side[3:]]

    kv = assemble([zr[m] for m in every], [exchange(zr[m], "core", 2, 1) for m in every])
    kvs = [kv]
    for m in range(1, n_chips):
        kvs.append(exchange(kv, "chip", n_chips, m))

    acc = None
    received = []
    for m in range(n_chips - 1):
        acc, dkv = chunk(
            m, every, info, q_side, kvs[m], acc,
            jnp.bfloat16 if m else jnp.float32,
        )
        if m:
            received.append(exchange(dkv, "chip", n_chips, m))
        else:
            own = dkv
    late = []
    m = n_chips - 1
    for slots in halves:
        acc, dkv = chunk(m, slots, info, q_side, kvs[m], acc, jnp.bfloat16)
        late.append(exchange(dkv, "chip", n_chips, m))

    dq_own, dq_send = finish(acc, tok, cols // 2)
    dq_other = exchange(dq_send, "core", 2, 1)
    dq = place(where, dq_own, dq_other)

    back, theirs = {}, {}
    for a, slots in enumerate(halves):
        full = [j * n_heads + slot for j in range(2) for slot in slots]
        picks = [full] * (n_chips - 1) + [list(range(len(full)))]
        sums = collect(picks, own, received + [late[a]])
        for slot, x in zip(slots, sums):
            back[slot] = exchange(x, "head", n_heads, slot) if slot else x
            theirs[slot] = exchange(back[slot], "core", 2, 1)
    dk, dv = unpack(where, [back[m] for m in every], [theirs[m] for m in every])
    return dq, dk, dv


def solution(mesh):
    n_seq, n_heads = mesh.shape["seq"], mesh.shape["head"]
    n_chips = n_seq // 2
    fine = Mesh(mesh.devices.reshape(n_chips, 2, n_heads), ("chip", "core", "head"))
    seq = ("chip", "core")
    rows, tokens = P(seq, "head"), P(("chip", "core", "head"), None)
    in_specs = (rows, tokens, tokens, rows, rows, P("head", seq), P())
    out_specs = (rows, tokens, tokens)

    def body(*args):
        return local(n_chips, n_heads, *args)

    return jax.shard_map(body, mesh=fine, in_specs=in_specs, out_specs=out_specs, check_vma=False)
```

time: 71.1 us -> 63 us (0.89)
  starting transfers between devices: 25.4 us -> 20.9 us
  local copies, waits for them, and re-layouts: 4.4 us -> 0.01 us
    ppermute x30 -> x25, starting transfers between devices: 25.4 us -> 20.9 us  [exchange(): return lax.ppermute(x, axis, [(i, i ^ m) for i in range(size)])]
    unnamed x14 -> x4, local copies, waits for them, and re-layouts: 4.4 us -> 0.01 us
    ppermute x30 -> x25, waiting for transfers between devices: 18.1 us -> 18.7 us  [exchange(): return lax.ppermute(x, axis, [(i, i ^ m) for i in range(size)])]
    pallas_call x12 -> x9, Pallas kernels: 19.2 us -> 19.2 us  [the longest x5 14.8 us: chunk(): pl.pallas_call(functools.partial(chunk_kernel, m, slots, kv.shape[0] // 2...]
  transfers between devices with their start and end apart: 30 -> 25, of which waited for: 10 -> 9; matrix products, arithmetic and copies ran while one was open for 0% -> 0% of each run, Pallas kernels for 24% -> 31%
where the time goes in v2:
time: 63 us; the launch traced here: 62.7 us
  Pallas kernels  22.1 us (35%)
  starting transfers between devices  20.9 us (33%)
  waiting for transfers between devices  18.7 us (30%)
  between operations  0.76 us (1%)
    ppermute x25, starting transfers between devices, exchange(): return lax.ppermute(x, axis, [(i, i ^ m) for i in range(size)])  20.9 us
    ppermute x25, waiting for transfers between devices, exchange(): return lax.ppermute(x, axis, [(i, i ^ m) for i in range(size)])  18.7 us
    pallas_call x5, Pallas kernels, chunk(): pl.pallas_call(functools.partial(chunk_kernel, m, slots, kv.shape[0] // 2...  14.8 us
    pallas_call x1, Pallas kernels, prepare(): pl.pallas_call(prepare_kernel, in_specs=[SMEM, ANY, ANY, ANY, VMEM], out_...  2.68 us
    pallas_call x1, Pallas kernels, pack(): pl.pallas_call(pack_kernel, in_specs=[SMEM, ANY, ANY], out_specs=[VMEM] *...  1.58 us
    pallas_call x1, Pallas kernels, place(): pl.pallas_call(place_kernel, in_specs=[SMEM, VMEM, VMEM], out_specs=VMEM,...  1.38 us
    pallas_call x1, Pallas kernels, unpack(): pl.pallas_call(functools.partial(unpack_kernel, n), in_specs=[SMEM] + [VM...  1.3 us
  transfers between devices with their start and end apart: 25, of which 9 were waited for; matrix products, arithmetic and copies ran while one was open for 0% of the time, Pallas kernels for 31%

profile of v2, /device:TPU:0, one launch (start us, length us, event | category | flops | bytes accessed | tf_op | source)
XLA Modules:
  0.0 62.7 jit_solution(10776043616921027968)
XLA Ops:
  0.6 0.1 pad_add_fusion.where
  0.7 1.6 %pack_kv.1 = (bf16[2,2,64,128]{3,2,1,0:T(8,128)(2,1)S(1)}, bf16[2,2,64,128]{3,2,1,0:T(8,128)(2,1)S(1)}, bf16[2,2,64,128]{3,2,1,0:T(8,128)(2,1)S(1)}, bf16[2,2,64,128]{3,2,1,0:T(8,128)(2,1)S(1)}) custom-call(s32[3]{0:T(128)S(1)} %pad_add_fusion.where, bf16[64,1024]{1,0:T(8,128)(2,1)} %keys.1, bf16[64,1024]{1,0:T(8,128)(2,1)} %values.1), custom_call_target="tpu_custom_call" | custom-call | flops 1000000 | bytes 524288 | tf_op jit(solution)/shard_map/pack_kv/pallas_call | solution.py:72
  2.3 3.1 %collective-permute-start.3 = (bf16[2,2,64,128]{3,2,1,0:T(8,128)(2,1)S(1)}, bf16[2,2,64,128]{3,2,1,0:T(8,128)(2,1)S(1)}, u32[]{:S(2)}, u32[]{:S(2)}) collective-permute-start(bf16[2,2,64,128]{3,2,1,0:T(8,128)(2,1)S(1)} %get-tuple-element.38), channel_id=1, source_target_pairs={{0,1},{1,0},{2,3},{3,2},{4,5},{5,4},{6,7},{7,6},{8,9},{9,8},{10,11... | collective-permute-start | bytes 196616 | tf_op jit(solution)/shard_map/ppermute | solution.py:339
  5.4 2.7 %prepare_q.1 = (bf16[1024,128]{1,0:T(8,128)(2,1)S(1)}, bf16[1024,128]{1,0:T(8,128)(2,1)S(1)}, f32[8,256]{1,0:T(8,128)S(1)}, bf16[1024,128]{1,0:T(8,128)(2,1)S(1)...) custom-call(s32[3]{0:T(128)S(1)} %pad_add_fusion.where, bf16[256,1024]{1,0:T(8,128)(2,1)} %q.1, ...), custom_call_target="tpu_custom_call" | custom-call | flops 10000000 | bytes 2097152 | tf_op jit(solution)/shard_map/prepare_q/pallas_call | solution.py:121
  8.1 0.1 collective-permute-start
  8.2 0.5 collective-permute-start.1
  8.7 2.6 %collective-permute-start.4 = (bf16[2,2,64,128]{3,2,1,0:T(8,128)(2,1)S(1)}, bf16[2,2,64,128]{3,2,1,0:T(8,128)(2,1)S(1)}, u32[]{:S(2)}, u32[]{:S(2)}) collective-permute-start(bf16[2,2,64,128]{3,2,1,0:T(8,128)(2,1)S(1)} %get-tuple-element.39), channel_id=1, source_target_pairs={{0,2},{1,3},{2,0},{3,1},{4,6},{5,7},{6,4},{7,5},{8,10},{9,11},{10,... | collective-permute-start | bytes 196616 | tf_op jit(solution)/shard_map/ppermute | solution.py:339
  11.3 0.0 collective-permute-start.5
  11.3 0.0 collective-permute-done.3.refs_1_
  11.3 0.0 collective-permute-start.6
  11.3 3.7 %collective-permute-done.4.refs_2_ = bf16[2,2,64,128]{3,2,1,0:T(8,128)(2,1)S(1)} collective-permute-done((bf16[2,2,64,128]{3,2,1,0:T(8,128)(2,1)S(1)}, bf16[2,2,64,128]{3,2,1,0:T(8,128)(2,1)S(1)}, u32[]{:S(2)}, u32[]{:S(2)}) %collective-permute-start.4) | collective-permute-done | bytes 65568 | tf_op jit(solution)/shard_map/ppermute | solution.py:339
  15.0 0.0 collective-permute-start.7
  15.0 2.4 %collective-permute-done.5.refs_3_ = bf16[2,2,64,128]{3,2,1,0:T(8,128)(2,1)S(1)} collective-permute-done((bf16[2,2,64,128]{3,2,1,0:T(8,128)(2,1)S(1)}, bf16[2,2,64,128]{3,2,1,0:T(8,128)(2,1)S(1)}, u32[]{:S(2)}, u32[]{:S(2)}) %collective-permute-start.5) | collective-permute-done | bytes 65568 | tf_op jit(solution)/shard_map/ppermute | solution.py:339
  17.3 0.0 collective-permute-start.8
  17.4 0.0 collective-permute-done.6.refs_4_
  17.4 0.5 collective-permute-start.9
  17.9 0.0 collective-permute-done.7.refs_5_
  17.9 0.1 collective-permute-start.2
  17.9 0.7 %collective-permute-done.8.refs_6_ = bf16[2,2,64,128]{3,2,1,0:T(8,128)(2,1)S(1)} collective-permute-done((bf16[2,2,64,128]{3,2,1,0:T(8,128)(2,1)S(1)}, bf16[2,2,64,128]{3,2,1,0:T(8,128)(2,1)S(1)}, u32[]{:S(2)}, u32[]{:S(2)}) %collective-permute-start.8) | collective-permute-done | bytes 65568 | tf_op jit(solution)/shard_map/ppermute | solution.py:339
  18.6 0.2 collective-permute-done.9.refs_7_
  18.8 1.6 %collective-permute-start.12 = (bf16[8,2,64,128]{3,2,1,0:T(8,128)(2,1)S(1)}, bf16[8,2,64,128]{3,2,1,0:T(8,128)(2,1)S(1)}, u32[]{:S(2)}, u32[]{:S(2)}) collective-permute-start(bf16[8,2,64,128]{3,2,1,0:T(8,128)(2,1)S(1)} %assemble.1.kv), channel_id=1, source_target_pairs={{0,8},{8,0},{16,24},{24,16},{1,9},{9,1},{17,25},{25,17},{2,10},{10... | collective-permute-start | bytes 786440 | tf_op jit(solution)/shard_map/ppermute | solution.py:339
  20.4 0.1 pad_add_fusion.1.where
  20.4 1.5 %collective-permute-start.11 = (bf16[8,2,64,128]{3,2,1,0:T(8,128)(2,1)S(1)}, bf16[8,2,64,128]{3,2,1,0:T(8,128)(2,1)S(1)}, u32[]{:S(2)}, u32[]{:S(2)}) collective-permute-start(bf16[8,2,64,128]{3,2,1,0:T(8,128)(2,1)S(1)} %assemble.1.kv), channel_id=1, source_target_pairs={{0,16},{8,24},{16,0},{24,8},{1,17},{9,25},{17,1},{25,9},{2,18},{10... | collective-permute-start | bytes 786440 | tf_op jit(solution)/shard_map/ppermute | solution.py:339
  21.9 0.0 collective-permute-done.2.stats1
  22.0 0.5 collective-permute-start.10
  22.4 0.0 collective-permute-done.q1
  22.4 0.0 collective-permute-done.1.do1
  22.4 3.4 %chunk.5 = (f32[128,2048]{1,0:T(8,128)S(1)}, f32[8,2,64,128]{3,2,1,0:T(8,128)S(1)}) custom-call(s32[19]{0:T(128)S(1)} %pad_add_fusion.1.where, bf16[1024,128]{1,0:T(8,128)(2,1)S(1)} %get-tuple-element.31.q0, bf16[1024,128]{1,0:T(8,128)(2,1)S(1)} %get-tuple-element.32.do0, f32[8,256]{1,0:T(8,128)S(1)} %get-tuple-element.33.stats0, ...), custom_call_target="tpu_custom_call" | custom-call | flops 2684354560 | bytes 524288 | tf_op jit(solution)/shard_map/chunk/pallas_call | solution.py:223
  25.8 2.2 %collective-permute-done.12.kv = bf16[8,2,64,128]{3,2,1,0:T(8,128)(2,1)S(1)} collective-permute-done((bf16[8,2,64,128]{3,2,1,0:T(8,128)(2,1)S(1)}, bf16[8,2,64,128]{3,2,1,0:T(8,128)(2,1)S(1)}, u32[]{:S(2)}, u32[]{:S(2)}) %collective-permute-start.12) | collective-permute-done | bytes 262176 | tf_op jit(solution)/shard_map/ppermute | solution.py:339
  28.0 3.6 %chunk.6 = (f32[128,2048]{1,0:T(8,128)S(1)}, bf16[8,2,64,128]{3,2,1,0:T(8,128)(2,1)S(1)}) custom-call(s32[19]{0:T(128)S(1)} %pad_add_fusion.1.where, bf16[1024,128]{1,0:T(8,128)(2,1)S(1)} %get-tuple-element.31.q0, bf16[1024,128]{1,0:T(8,128)(2,1)S(1)} %get-tuple-element.32.do0, ...), custom_call_target="tpu_custom_call", output_to_operand_aliasing={{0}: (8, {})} | custom-call | flops 2684354560 | bytes 524288 | tf_op jit(solution)/shard_map/chunk/pallas_call | solution.py:223
  31.6 2.7 %collective-permute-done.11.kv = bf16[8,2,64,128]{3,2,1,0:T(8,128)(2,1)S(1)} collective-permute-done((bf16[8,2,64,128]{3,2,1,0:T(8,128)(2,1)S(1)}, bf16[8,2,64,128]{3,2,1,0:T(8,128)(2,1)S(1)}, u32[]{:S(2)}, u32[]{:S(2)}) %collective-permute-start.11) | collective-permute-done | bytes 262176 | tf_op jit(solution)/shard_map/ppermute | solution.py:339
  34.3 3.6 %chunk.7 = (f32[128,2048]{1,0:T(8,128)S(1)}, bf16[8,2,64,128]{3,2,1,0:T(8,128)(2,1)S(1)}) custom-call(s32[19]{0:T(128)S(1)} %pad_add_fusion.1.where, bf16[1024,128]{1,0:T(8,128)(2,1)S(1)} %get-tuple-element.31.q0, bf16[1024,128]{1,0:T(8,128)(2,1)S(1)} %get-tuple-element.32.do0, ...), custom_call_target="tpu_custom_call", output_to_operand_aliasing={{0}: (8, {})} | custom-call | flops 2684354560 | bytes 524288 | tf_op jit(solution)/shard_map/chunk/pallas_call | solution.py:223
  37.9 1.6 %collective-permute-start.15 = (bf16[8,2,64,128]{3,2,1,0:T(8,128)(2,1)S(1)}, bf16[8,2,64,128]{3,2,1,0:T(8,128)(2,1)S(1)}, u32[]{:S(2)}, u32[]{:S(2)}) collective-permute-start(bf16[8,2,64,128]{3,2,1,0:T(8,128)(2,1)S(1)} %get-tuple-element.50), channel_id=1, source_target_pairs={{0,16},{8,24},{16,0},{24,8},{1,17},{9,25},{17,1},{25,9},{2,18},{10... | collective-permute-start | bytes 786440 | tf_op jit(solution)/shard_map/ppermute | solution.py:339
  39.5 0.5 collective-permute-start.14
  40.0 0.0 collective-permute-done.10.kv
  40.0 2.2 %chunk.8 = (f32[128,2048]{1,0:T(8,128)S(1)}, bf16[4,2,64,128]{3,2,1,0:T(8,128)(2,1)S(1)}) custom-call(s32[19]{0:T(128)S(1)} %pad_add_fusion.1.where, bf16[1024,128]{1,0:T(8,128)(2,1)S(1)} %get-tuple-element.31.q0, bf16[1024,128]{1,0:T(8,128)(2,1)S(1)} %get-tuple-element.32.do0, ...), custom_call_target="tpu_custom_call", output_to_operand_aliasing={{0}: (8, {})} | custom-call | flops 1342177280 | bytes 524288 | tf_op jit(solution)/shard_map/chunk/pallas_call | solution.py:223
  42.2 2.2 %chunk.9 = (f32[128,2048]{1,0:T(8,128)S(1)}, bf16[4,2,64,128]{3,2,1,0:T(8,128)(2,1)S(1)}) custom-call(s32[19]{0:T(128)S(1)} %pad_add_fusion.1.where, bf16[1024,128]{1,0:T(8,128)(2,1)S(1)} %get-tuple-element.31.q0, bf16[1024,128]{1,0:T(8,128)(2,1)S(1)} %get-tuple-element.32.do0, ...), custom_call_target="tpu_custom_call", output_to_operand_aliasing={{0}: (8, {})} | custom-call | flops 1342177280 | bytes 524288 | tf_op jit(solution)/shard_map/chunk/pallas_call | solution.py:223
  44.4 1.5 %collective-permute-start.17 = (bf16[4,2,64,128]{3,2,1,0:T(8,128)(2,1)S(1)}, bf16[4,2,64,128]{3,2,1,0:T(8,128)(2,1)S(1)}, u32[]{:S(2)}, u32[]{:S(2)}) collective-permute-start(bf16[4,2,64,128]{3,2,1,0:T(8,128)(2,1)S(1)} %get-tuple-element.53), channel_id=1, source_target_pairs={{0,24},{8,16},{16,8},{24,0},{1,25},{9,17},{17,9},{25,1},{2,26},{10... | collective-permute-start | bytes 393224 | tf_op jit(solution)/shard_map/ppermute | solution.py:339
  45.9 0.2 finish_q.1
  46.1 0.1 collective-permute-start.13
  46.2 1.6 %collective-permute-start.16 = (bf16[4,2,64,128]{3,2,1,0:T(8,128)(2,1)S(1)}, bf16[4,2,64,128]{3,2,1,0:T(8,128)(2,1)S(1)}, u32[]{:S(2)}, u32[]{:S(2)}) collective-permute-start(bf16[4,2,64,128]{3,2,1,0:T(8,128)(2,1)S(1)} %get-tuple-element.51), channel_id=1, source_target_pairs={{0,24},{8,16},{16,8},{24,0},{1,25},{9,17},{17,9},{25,1},{2,26},{10... | collective-permute-start | bytes 393224 | tf_op jit(solution)/shard_map/ppermute | solution.py:339
  47.7 2.7 %collective-permute-done.17.refs_2_ = bf16[4,2,64,128]{3,2,1,0:T(8,128)(2,1)S(1)} collective-permute-done((bf16[4,2,64,128]{3,2,1,0:T(8,128)(2,1)S(1)}, bf16[4,2,64,128]{3,2,1,0:T(8,128)(2,1)S(1)}, u32[]{:S(2)}, u32[]{:S(2)}) %collective-permute-start.17) | collective-permute-done | bytes 131104 | tf_op jit(solution)/shard_map/ppermute | solution.py:339
  50.4 0.0 collective-permute-done.15.refs_1_
  50.4 0.0 collective-permute-done.14.refs_0_
  50.4 0.1 collect.3
  50.5 1.0 %collective-permute-start.18 = (bf16[2,2,64,128]{3,2,1,0:T(8,128)(2,1)S(1)}, bf16[2,2,64,128]{3,2,1,0:T(8,128)(2,1)S(1)}, u32[]{:S(2)}, u32[]{:S(2)}) collective-permute-start(bf16[2,2,64,128]{3,2,1,0:T(8,128)(2,1)S(1)} %get-tuple-element.54), channel_id=1, source_target_pairs={{0,1},{1,0},{2,3},{3,2},{4,5},{5,4},{6,7},{7,6},{8,9},{9,8},{10,11... | collective-permute-start | bytes 196616 | tf_op jit(solution)/shard_map/ppermute | solution.py:339
  51.5 2.6 %collective-permute-start.20 = (bf16[2,2,64,128]{3,2,1,0:T(8,128)(2,1)S(1)}, bf16[2,2,64,128]{3,2,1,0:T(8,128)(2,1)S(1)}, u32[]{:S(2)}, u32[]{:S(2)}) collective-permute-start(bf16[2,2,64,128]{3,2,1,0:T(8,128)(2,1)S(1)} %get-tuple-element.56), channel_id=1, source_target_pairs={{0,3},{1,2},{2,1},{3,0},{4,7},{5,6},{6,5},{7,4},{8,11},{9,10},{10,... | collective-permute-start | bytes 196616 | tf_op jit(solution)/shard_map/ppermute | solution.py:339
  54.2 0.0 collective-permute-done.16.refs_2_
  54.2 0.1 collect.2
  54.2 1.1 %collective-permute-start.19 = (bf16[2,2,64,128]{3,2,1,0:T(8,128)(2,1)S(1)}, bf16[2,2,64,128]{3,2,1,0:T(8,128)(2,1)S(1)}, u32[]{:S(2)}, u32[]{:S(2)}) collective-permute-start(bf16[2,2,64,128]{3,2,1,0:T(8,128)(2,1)S(1)} %get-tuple-element.55), channel_id=1, source_target_pairs={{0,2},{1,3},{2,0},{3,1},{4,6},{5,7},{6,4},{7,5},{8,10},{9,11},{10,... | collective-permute-start | bytes 196616 | tf_op jit(solution)/shard_map/ppermute | solution.py:339
  55.3 0.0 collective-permute-start.21
  55.3 0.0 collective-permute-done.18.refs_1_
  55.3 0.5 collective-permute-start.22
  55.9 2.5 %collective-permute-done.20.refs_3_ = bf16[2,2,64,128]{3,2,1,0:T(8,128)(2,1)S(1)} collective-permute-done((bf16[2,2,64,128]{3,2,1,0:T(8,128)(2,1)S(1)}, bf16[2,2,64,128]{3,2,1,0:T(8,128)(2,1)S(1)}, u32[]{:S(2)}, u32[]{:S(2)}) %collective-permute-start.20) | collective-permute-done | bytes 65568 | tf_op jit(solution)/shard_map/ppermute | solution.py:339
  58.4 0.0 collective-permute-start.24
  58.4 1.6 %collective-permute-done.19.refs_2_ = bf16[2,2,64,128]{3,2,1,0:T(8,128)(2,1)S(1)} collective-permute-done((bf16[2,2,64,128]{3,2,1,0:T(8,128)(2,1)S(1)}, bf16[2,2,64,128]{3,2,1,0:T(8,128)(2,1)S(1)}, u32[]{:S(2)}, u32[]{:S(2)}) %collective-permute-start.19) | collective-permute-done | bytes 65568 | tf_op jit(solution)/shard_map/ppermute | solution.py:339
  60.0 0.0 collective-permute-start.23
  60.0 0.0 collective-permute-done.13.theirs
  60.0 1.4 %place_q.1 = bf16[256,1024]{1,0:T(8,128)(2,1)} custom-call(s32[3]{0:T(128)S(1)} %pad_add_fusion.where, bf16[256,512]{1,0:T(8,128)(2,1)S(1)} %get-tuple-element.46.mine, bf16[256,512]{1,0:T(8,128)(2,1)S(1)} %collective-permute-done.13.theirs), custom_call_target="tpu_custom_call" | custom-call | flops 1000000 | bytes 1048576 | tf_op jit(solution)/shard_map/place_q/pallas_call | solution.py:275
  61.3 0.0 collective-permute-done.21.refs_4_
  61.3 0.0 collective-permute-done.22.refs_5_
  61.4 0.0 collective-permute-done.24.refs_7_
  61.4 0.0 collective-permute-done.23.refs_6_
  61.4 1.3 %unpack_kv.1 = (bf16[64,1024]{1,0:T(8,128)(2,1)}, bf16[64,1024]{1,0:T(8,128)(2,1)}) custom-call(s32[3]{0:T(128)S(1)} %pad_add_fusion.where, bf16[2,2,64,128]{3,2,1,0:T(8,128)(2,1)S(1)} %get-tuple-element.52.refs_0_, bf16[2,2,64,128]{3,2,1,0:T(8,128)(2,1)S(1)} %collective-permute-done.18.refs_1_, bf16[2,2,64,128]{3,2,1,0:T(8,128)(2,1)S(1)} %collective-permute-done.19.refs_2_, ...), custom_call_target="tpu_custom_call" | custom-call | flops 1000000 | bytes 524288 | tf_op jit(solution)/shard_map/unpack_kv/pallas_call | solution.py:327
  (5 shorter events, 0.0 us)
Async XLA Ops:
  0.7 4.7 %copy-start = (f32[8,256]{1,0:T(8,128)S(1)}, f32[8,256]{1,0:T(8,128)}, u32[]{:S(2)}) copy-start(f32[8,256]{1,0:T(8,128)} %lse.1) | copy-start | bytes 24580
  2.3 9.0 %collective-permute-start.3 = (bf16[2,2,64,128]{3,2,1,0:T(8,128)(2,1)S(1)}, bf16[2,2,64,128]{3,2,1,0:T(8,128)(2,1)S(1)}, u32[]{:S(2)}, u32[]{:S(2)}) collective-permute-start(bf16[2,2,64,128]{3,2,1,0:T(8,128)(2,1)S(1)} %get-tuple-element.38), channel_id=1, source_target_pairs={{0,1},{1,0},{2,3},{3,2},{4,5},{5,4},{6,7},{7,6},{8,9},{9,8},{10,11... | collective-permute-start | bytes 196616 | tf_op jit(solution)/shard_map/ppermute | solution.py:339
  8.1 14.3 %collective-permute-start = (bf16[1024,128]{1,0:T(8,128)(2,1)S(1)}, bf16[1024,128]{1,0:T(8,128)(2,1)S(1)}, u32[]{:S(2)}, u32[]{:S(2)}) collective-permute-start(bf16[1024,128]{1,0:T(8,128)(2,1)S(1)} %get-tuple-element.34), channel_id=1, source_target_pairs={{0,4},{4,0},{1,5},{5,1},{2,6},{6,2},{3,7},{7,3},{8,12},{12,8},{9,1... | collective-permute-start | bytes 786440 | tf_op jit(solution)/shard_map/ppermute | solution.py:339
  8.2 14.2 %collective-permute-start.1 = (bf16[1024,128]{1,0:T(8,128)(2,1)S(1)}, bf16[1024,128]{1,0:T(8,128)(2,1)S(1)}, u32[]{:S(2)}, u32[]{:S(2)}) collective-permute-start(bf16[1024,128]{1,0:T(8,128)(2,1)S(1)} %get-tuple-element.35), channel_id=1, source_target_pairs={{0,4},{4,0},{1,5},{5,1},{2,6},{6,2},{3,7},{7,3},{8,12},{12,8},{9,1... | collective-permute-start | bytes 786440 | tf_op jit(solution)/shard_map/ppermute | solution.py:339
  8.7 6.3 %collective-permute-start.4 = (bf16[2,2,64,128]{3,2,1,0:T(8,128)(2,1)S(1)}, bf16[2,2,64,128]{3,2,1,0:T(8,128)(2,1)S(1)}, u32[]{:S(2)}, u32[]{:S(2)}) collective-permute-start(bf16[2,2,64,128]{3,2,1,0:T(8,128)(2,1)S(1)} %get-tuple-element.39), channel_id=1, source_target_pairs={{0,2},{1,3},{2,0},{3,1},{4,6},{5,7},{6,4},{7,5},{8,10},{9,11},{10,... | collective-permute-start | bytes 196616 | tf_op jit(solution)/shard_map/ppermute | solution.py:339
  11.3 6.1 %collective-permute-start.5 = (bf16[2,2,64,128]{3,2,1,0:T(8,128)(2,1)S(1)}, bf16[2,2,64,128]{3,2,1,0:T(8,128)(2,1)S(1)}, u32[]{:S(2)}, u32[]{:S(2)}) collective-permute-start(bf16[2,2,64,128]{3,2,1,0:T(8,128)(2,1)S(1)} %get-tuple-element.40), channel_id=1, source_target_pairs={{0,3},{1,2},{2,1},{3,0},{4,7},{5,6},{6,5},{7,4},{8,11},{9,10},{10,... | collective-permute-start | bytes 196616 | tf_op jit(solution)/shard_map/ppermute | solution.py:339
  11.3 6.1 %collective-permute-start.6 = (bf16[2,2,64,128]{3,2,1,0:T(8,128)(2,1)S(1)}, bf16[2,2,64,128]{3,2,1,0:T(8,128)(2,1)S(1)}, u32[]{:S(2)}, u32[]{:S(2)}) collective-permute-start(bf16[2,2,64,128]{3,2,1,0:T(8,128)(2,1)S(1)} %get-tuple-element.37.refs_0_), channel_id=1, source_target_pairs={{0,4},{4,0},{1,5},{5,1},{2,6},{6,2},{3,7},{7,3},{8,12},{12,8},{9,1... | collective-permute-start | bytes 196616 | tf_op jit(solution)/shard_map/ppermute | solution.py:339
  15.0 2.9 %collective-permute-start.7 = (bf16[2,2,64,128]{3,2,1,0:T(8,128)(2,1)S(1)}, bf16[2,2,64,128]{3,2,1,0:T(8,128)(2,1)S(1)}, u32[]{:S(2)}, u32[]{:S(2)}) collective-permute-start(bf16[2,2,64,128]{3,2,1,0:T(8,128)(2,1)S(1)} %collective-permute-done.3.refs_1_), channel_id=1, source_target_pairs={{0,4},{4,0},{1,5},{5,1},{2,6},{6,2},{3,7},{7,3},{8,12},{12,8},{9,1... | collective-permute-start | bytes 196616 | tf_op jit(solution)/shard_map/ppermute | solution.py:339
  17.3 1.3 %collective-permute-start.8 = (bf16[2,2,64,128]{3,2,1,0:T(8,128)(2,1)S(1)}, bf16[2,2,64,128]{3,2,1,0:T(8,128)(2,1)S(1)}, u32[]{:S(2)}, u32[]{:S(2)}) collective-permute-start(bf16[2,2,64,128]{3,2,1,0:T(8,128)(2,1)S(1)} %collective-permute-done.4.refs_2_), channel_id=1, source_target_pairs={{0,4},{4,0},{1,5},{5,1},{2,6},{6,2},{3,7},{7,3},{8,12},{12,8},{9,1... | collective-permute-start | bytes 196616 | tf_op jit(solution)/shard_map/ppermute | solution.py:339
  17.4 1.4 %collective-permute-start.9 = (bf16[2,2,64,128]{3,2,1,0:T(8,128)(2,1)S(1)}, bf16[2,2,64,128]{3,2,1,0:T(8,128)(2,1)S(1)}, u32[]{:S(2)}, u32[]{:S(2)}) collective-permute-start(bf16[2,2,64,128]{3,2,1,0:T(8,128)(2,1)S(1)} %collective-permute-done.5.refs_3_), channel_id=1, source_target_pairs={{0,4},{4,0},{1,5},{5,1},{2,6},{6,2},{3,7},{7,3},{8,12},{12,8},{9,1... | collective-permute-start | bytes 196616 | tf_op jit(solution)/shard_map/ppermute | solution.py:339
  17.9 2.5 %copy-start.1 = (s32[16]{0:T(128)S(1)}, s32[16]{0:T(128)}, u32[]{:S(2)}) copy-start(s32[16]{0:T(128)} %param.13) | copy-start | bytes 196
  17.9 4.1 %collective-permute-start.2 = (f32[8,256]{1,0:T(8,128)S(1)}, f32[8,256]{1,0:T(8,128)S(1)}, u32[]{:S(2)}, u32[]{:S(2)}) collective-permute-start(f32[8,256]{1,0:T(8,128)S(1)} %get-tuple-element.36), channel_id=1, source_target_pairs={{0,4},{4,0},{1,5},{5,1},{2,6},{6,2},{3,7},{7,3},{8,12},{12,8},{9,1... | collective-permute-start | bytes 24584 | tf_op jit(solution)/shard_map/ppermute | solution.py:339
  18.8 9.2 %collective-permute-start.12 = (bf16[8,2,64,128]{3,2,1,0:T(8,128)(2,1)S(1)}, bf16[8,2,64,128]{3,2,1,0:T(8,128)(2,1)S(1)}, u32[]{:S(2)}, u32[]{:S(2)}) collective-permute-start(bf16[8,2,64,128]{3,2,1,0:T(8,128)(2,1)S(1)} %assemble.1.kv), channel_id=1, source_target_pairs={{0,8},{8,0},{16,24},{24,16},{1,9},{9,1},{17,25},{25,17},{2,10},{10... | collective-permute-start | bytes 786440 | tf_op jit(solution)/shard_map/ppermute | solution.py:339
  20.4 13.9 %collective-permute-start.11 = (bf16[8,2,64,128]{3,2,1,0:T(8,128)(2,1)S(1)}, bf16[8,2,64,128]{3,2,1,0:T(8,128)(2,1)S(1)}, u32[]{:S(2)}, u32[]{:S(2)}) collective-permute-start(bf16[8,2,64,128]{3,2,1,0:T(8,128)(2,1)S(1)} %assemble.1.kv), channel_id=1, source_target_pairs={{0,16},{8,24},{16,0},{24,8},{1,17},{9,25},{17,1},{25,9},{2,18},{10... | collective-permute-start | bytes 786440 | tf_op jit(solution)/shard_map/ppermute | solution.py:339
  22.0 18.1 %collective-permute-start.10 = (bf16[8,2,64,128]{3,2,1,0:T(8,128)(2,1)S(1)}, bf16[8,2,64,128]{3,2,1,0:T(8,128)(2,1)S(1)}, u32[]{:S(2)}, u32[]{:S(2)}) collective-permute-start(bf16[8,2,64,128]{3,2,1,0:T(8,128)(2,1)S(1)} %assemble.1.kv), channel_id=1, source_target_pairs={{0,24},{8,16},{16,8},{24,0},{1,25},{9,17},{17,9},{25,1},{2,26},{10... | collective-permute-start | bytes 786440 | tf_op jit(solution)/shard_map/ppermute | solution.py:339
  37.9 12.5 %collective-permute-start.15 = (bf16[8,2,64,128]{3,2,1,0:T(8,128)(2,1)S(1)}, bf16[8,2,64,128]{3,2,1,0:T(8,128)(2,1)S(1)}, u32[]{:S(2)}, u32[]{:S(2)}) collective-permute-start(bf16[8,2,64,128]{3,2,1,0:T(8,128)(2,1)S(1)} %get-tuple-element.50), channel_id=1, source_target_pairs={{0,16},{8,24},{16,0},{24,8},{1,17},{9,25},{17,1},{25,9},{2,18},{10... | collective-permute-start | bytes 786440 | tf_op jit(solution)/shard_map/ppermute | solution.py:339
  39.5 10.9 %collective-permute-start.14 = (bf16[8,2,64,128]{3,2,1,0:T(8,128)(2,1)S(1)}, bf16[8,2,64,128]{3,2,1,0:T(8,128)(2,1)S(1)}, u32[]{:S(2)}, u32[]{:S(2)}) collective-permute-start(bf16[8,2,64,128]{3,2,1,0:T(8,128)(2,1)S(1)} %get-tuple-element.49), channel_id=1, source_target_pairs={{0,8},{8,0},{16,24},{24,16},{1,9},{9,1},{17,25},{25,17},{2,10},{10... | collective-permute-start | bytes 786440 | tf_op jit(solution)/shard_map/ppermute | solution.py:339
  44.4 6.1 %collective-permute-start.17 = (bf16[4,2,64,128]{3,2,1,0:T(8,128)(2,1)S(1)}, bf16[4,2,64,128]{3,2,1,0:T(8,128)(2,1)S(1)}, u32[]{:S(2)}, u32[]{:S(2)}) collective-permute-start(bf16[4,2,64,128]{3,2,1,0:T(8,128)(2,1)S(1)} %get-tuple-element.53), channel_id=1, source_target_pairs={{0,24},{8,16},{16,8},{24,0},{1,25},{9,17},{17,9},{25,1},{2,26},{10... | collective-permute-start | bytes 393224 | tf_op jit(solution)/shard_map/ppermute | solution.py:339
  46.1 13.9 %collective-permute-start.13 = (bf16[256,512]{1,0:T(8,128)(2,1)S(1)}, bf16[256,512]{1,0:T(8,128)(2,1)S(1)}, u32[]{:S(2)}, u32[]{:S(2)}) collective-permute-start(bf16[256,512]{1,0:T(8,128)(2,1)S(1)} %get-tuple-element.47), channel_id=1, source_target_pairs={{0,4},{4,0},{1,5},{5,1},{2,6},{6,2},{3,7},{7,3},{8,12},{12,8},{9,1... | collective-permute-start | bytes 786440 | tf_op jit(solution)/shard_map/ppermute | solution.py:339
  46.2 8.0 %collective-permute-start.16 = (bf16[4,2,64,128]{3,2,1,0:T(8,128)(2,1)S(1)}, bf16[4,2,64,128]{3,2,1,0:T(8,128)(2,1)S(1)}, u32[]{:S(2)}, u32[]{:S(2)}) collective-permute-start(bf16[4,2,64,128]{3,2,1,0:T(8,128)(2,1)S(1)} %get-tuple-element.51), channel_id=1, source_target_pairs={{0,24},{8,16},{16,8},{24,0},{1,25},{9,17},{17,9},{25,1},{2,26},{10... | collective-permute-start | bytes 393224 | tf_op jit(solution)/shard_map/ppermute | solution.py:339
  50.5 4.8 %collective-permute-start.18 = (bf16[2,2,64,128]{3,2,1,0:T(8,128)(2,1)S(1)}, bf16[2,2,64,128]{3,2,1,0:T(8,128)(2,1)S(1)}, u32[]{:S(2)}, u32[]{:S(2)}) collective-permute-start(bf16[2,2,64,128]{3,2,1,0:T(8,128)(2,1)S(1)} %get-tuple-element.54), channel_id=1, source_target_pairs={{0,1},{1,0},{2,3},{3,2},{4,5},{5,4},{6,7},{7,6},{8,9},{9,8},{10,11... | collective-permute-start | bytes 196616 | tf_op jit(solution)/shard_map/ppermute | solution.py:339
  51.5 6.8 %collective-permute-start.20 = (bf16[2,2,64,128]{3,2,1,0:T(8,128)(2,1)S(1)}, bf16[2,2,64,128]{3,2,1,0:T(8,128)(2,1)S(1)}, u32[]{:S(2)}, u32[]{:S(2)}) collective-permute-start(bf16[2,2,64,128]{3,2,1,0:T(8,128)(2,1)S(1)} %get-tuple-element.56), channel_id=1, source_target_pairs={{0,3},{1,2},{2,1},{3,0},{4,7},{5,6},{6,5},{7,4},{8,11},{9,10},{10,... | collective-permute-start | bytes 196616 | tf_op jit(solution)/shard_map/ppermute | solution.py:339
  54.2 5.7 %collective-permute-start.19 = (bf16[2,2,64,128]{3,2,1,0:T(8,128)(2,1)S(1)}, bf16[2,2,64,128]{3,2,1,0:T(8,128)(2,1)S(1)}, u32[]{:S(2)}, u32[]{:S(2)}) collective-permute-start(bf16[2,2,64,128]{3,2,1,0:T(8,128)(2,1)S(1)} %get-tuple-element.55), channel_id=1, source_target_pairs={{0,2},{1,3},{2,0},{3,1},{4,6},{5,7},{6,4},{7,5},{8,10},{9,11},{10,... | collective-permute-start | bytes 196616 | tf_op jit(solution)/shard_map/ppermute | solution.py:339
  55.3 6.0 %collective-permute-start.21 = (bf16[2,2,64,128]{3,2,1,0:T(8,128)(2,1)S(1)}, bf16[2,2,64,128]{3,2,1,0:T(8,128)(2,1)S(1)}, u32[]{:S(2)}, u32[]{:S(2)}) collective-permute-start(bf16[2,2,64,128]{3,2,1,0:T(8,128)(2,1)S(1)} %get-tuple-element.52.refs_0_), channel_id=1, source_target_pairs={{0,4},{4,0},{1,5},{5,1},{2,6},{6,2},{3,7},{7,3},{8,12},{12,8},{9,1... | collective-permute-start | bytes 196616 | tf_op jit(solution)/shard_map/ppermute | solution.py:339
  55.3 6.0 %collective-permute-start.22 = (bf16[2,2,64,128]{3,2,1,0:T(8,128)(2,1)S(1)}, bf16[2,2,64,128]{3,2,1,0:T(8,128)(2,1)S(1)}, u32[]{:S(2)}, u32[]{:S(2)}) collective-permute-start(bf16[2,2,64,128]{3,2,1,0:T(8,128)(2,1)S(1)} %collective-permute-done.18.refs_1_), channel_id=1, source_target_pairs={{0,4},{4,0},{1,5},{5,1},{2,6},{6,2},{3,7},{7,3},{8,12},{12,8},{9,1... | collective-permute-start | bytes 196616 | tf_op jit(solution)/shard_map/ppermute | solution.py:339
  58.4 3.0 %collective-permute-start.24 = (bf16[2,2,64,128]{3,2,1,0:T(8,128)(2,1)S(1)}, bf16[2,2,64,128]{3,2,1,0:T(8,128)(2,1)S(1)}, u32[]{:S(2)}, u32[]{:S(2)}) collective-permute-start(bf16[2,2,64,128]{3,2,1,0:T(8,128)(2,1)S(1)} %collective-permute-done.20.refs_3_), channel_id=1, source_target_pairs={{0,4},{4,0},{1,5},{5,1},{2,6},{6,2},{3,7},{7,3},{8,12},{12,8},{9,1... | collective-permute-start | bytes 196616 | tf_op jit(solution)/shard_map/ppermute | solution.py:339
  60.0 1.4 %collective-permute-start.23 = (bf16[2,2,64,128]{3,2,1,0:T(8,128)(2,1)S(1)}, bf16[2,2,64,128]{3,2,1,0:T(8,128)(2,1)S(1)}, u32[]{:S(2)}, u32[]{:S(2)}) collective-permute-start(bf16[2,2,64,128]{3,2,1,0:T(8,128)(2,1)S(1)} %collective-permute-done.19.refs_2_), channel_id=1, source_target_pairs={{0,4},{4,0},{1,5},{5,1},{2,6},{6,2},{3,7},{7,3},{8,12},{12,8},{9,1... | collective-permute-start | bytes 196616 | tf_op jit(solution)/shard_map/ppermute | solution.py:339

commit v3 on v2

--- a/solution.py
+++ b/solution.py
@@ -133,19 +133,19 @@
     )(where, far(q), far(do), far(o), lse)
 
 
-def assemble_kernel(n_slots, *refs):
-    out = refs[-1]
-    for s in range(n_slots):
-        out[s] = refs[s][0]
-        out[n_slots + s] = refs[n_slots + s][1]
+def assemble_kernel(n, refs):
+    mine, theirs, out = refs[:n], refs[n : 2 * n], refs[2 * n]
+    for s in range(n):
+        out[s] = mine[s][0]
+        out[n + s] = theirs[s][1]
 
 
 def assemble(mine, theirs):
-    n_slots = len(mine)
-    shape = (2 * n_slots,) + mine[0].shape[1:]
-    return pl.pallas_call(
-        functools.partial(assemble_kernel, n_slots),
-        in_specs=[VMEM] * (2 * n_slots),
+    n = len(mine)
+    shape = (2 * n,) + mine[0].shape[1:]
+    return pl.pallas_call(
+        lambda *refs: assemble_kernel(n, refs),
+        in_specs=[VMEM] * (2 * n),
         out_specs=VMEM,
         out_shape=pltpu.VMEM(shape, mine[0].dtype),
         compiler_params=params(8),
@@ -154,27 +154,28 @@
     )(*[near(x) for x in mine], *[near(x) for x in theirs])
 
 
-def chunk_kernel(m, slots, n_heads, first, where, q0, do0, stats0, q1, do1, stats1, kv, *rest):
+def chunk_kernel(m, picks, first, where, q0, do0, stats0, q1, do1, stats1, *rest):
     acc, dkv = rest[-2:]
+    n_kv = max(p[0] for p in picks) + 1
+    kvs, rest = rest[:n_kv], rest[n_kv:]
     c, core, z = where[0], where[1], where[2]
-    piece = kv.shape[2]
+    piece = kvs[0].shape[2]
     half = stats0.shape[1] // 2
     width = RATIO * half
     per_block = half // piece
     other = jnp.bitwise_xor(c, m)
     pieces = []
-    for j in range(2):
-        for slot in slots:
-            source = jnp.bitwise_xor(z, slot)
-            block = where[3 + (other * 2 + jnp.bitwise_xor(core, j)) * 2 + source // per_block]
-            pieces.append((j * n_heads + slot, block * half + (source % per_block) * piece))
+    for array, place, j, slot in picks:
+        source = jnp.bitwise_xor(z, slot)
+        block = where[3 + (other * 2 + jnp.bitwise_xor(core, j)) * 2 + source // per_block]
+        pieces.append((kvs[array].at[place], block * half + (source % per_block) * piece))
     per_tile = min(len(pieces), 256 // piece)
     tiles = [range(i, i + per_tile) for i in range(0, len(pieces), per_tile)]
     row = lax.broadcasted_iota(jnp.int32, (piece, half), 0)
     lane = lax.broadcasted_iota(jnp.int32, (piece, half), 1)
     offset = jnp.concatenate([row - lane] * per_tile, 0)
-    ks = [jnp.concatenate([kv[pieces[p][0], 0] for p in t], 0) for t in tiles]
-    vs = [jnp.concatenate([kv[pieces[p][0], 1] for p in t], 0) for t in tiles]
+    ks = [jnp.concatenate([pieces[p][0][0] for p in t], 0) for t in tiles]
+    vs = [jnp.concatenate([pieces[p][0][1] for p in t], 0) for t in tiles]
     kts = [k.T for k in ks]
     nt = (((1,), (1,)), ((), ()))
     dks, dvs = [None] * len(tiles), [None] * len(tiles)
@@ -214,20 +215,20 @@
             dkv[p, 1] = dvs[t][rows].astype(dkv.dtype)
 
 
-def chunk(m, slots, where, q_side, kv, acc, out_dtype):
+def chunk(m, picks, where, q_side, kvs, acc, out_dtype):
     first = acc is None
     width = q_side[0].shape[0] * 2
     acc_out = pltpu.VMEM((HEAD_SIZE, width), jnp.float32)
-    args = [near(x) for x in q_side] + [near(kv)] + ([] if first else [near(acc)])
-    out = (2 * len(slots),) + kv.shape[1:]
-    return pl.pallas_call(
-        functools.partial(chunk_kernel, m, slots, kv.shape[0] // 2, first),
+    args = [near(x) for x in q_side] + [near(kv) for kv in kvs] + ([] if first else [near(acc)])
+    out = (len(picks),) + kvs[0].shape[1:]
+    return pl.pallas_call(
+        functools.partial(chunk_kernel, m, picks, first),
         in_specs=[SMEM] + [VMEM] * len(args),
         out_specs=[VMEM] * 2,
         out_shape=[acc_out, pltpu.VMEM(out, out_dtype)],
         input_output_aliases={} if first else {len(args): 0},
         compiler_params=params(20),
-        cost_estimate=cost(5 * 2 * out[0] * out[2] * width * HEAD_SIZE * 2, 4 * kv.size),
+        cost_estimate=cost(5 * 2 * out[0] * out[2] * width * HEAD_SIZE * 2, 4 * kvs[0].size),
         name="chunk",
     )(where, *args)
 
@@ -358,27 +359,38 @@
     own_side = prepare(where, queries, out_grad, outputs, log_norm)
     q_side = list(own_side[:3]) + [exchange(x, "core", 2, 1) for x in own_side[3:]]
 
-    kv = assemble([zr[m] for m in every], [exchange(zr[m], "core", 2, 1) for m in every])
-    kvs = [kv]
-    for m in range(1, n_chips):
-        kvs.append(exchange(kv, "chip", n_chips, m))
-
+    other = {}
+    for m in every:
+        other[m] = exchange(zr[m], "core", 2, 1)
+    last = n_chips - 1
+    own, sent = [], [[] for _ in range(n_chips)]
+    for a, slots in enumerate(halves):
+        own.append(assemble([zr[m] for m in slots], [other[m] for m in slots]))
+        for m in range(1, last):
+            sent[m].append(exchange(own[a], "chip", n_chips, m))
+    full = [m for slots in halves for m in slots]
+    whole = assemble([zr[m] for m in full], [other[m] for m in full])
+    far_kv = exchange(whole, "chip", n_chips, last)
+
+    half_picks = [
+        (a, j * len(slots) + i, j, slot)
+        for a, slots in enumerate(halves)
+        for j in range(2)
+        for i, slot in enumerate(slots)
+    ]
+    far_picks = [
+        [(0, j * n_heads + full.index(slot), j, slot) for j in range(2) for slot in slots]
+        for slots in halves
+    ]
     acc = None
-    received = []
-    for m in range(n_chips - 1):
-        acc, dkv = chunk(
-            m, every, info, q_side, kvs[m], acc,
-            jnp.bfloat16 if m else jnp.float32,
-        )
-        if m:
-            received.append(exchange(dkv, "chip", n_chips, m))
-        else:
-            own = dkv
-    late = []
-    m = n_chips - 1
-    for slots in halves:
-        acc, dkv = chunk(m, slots, info, q_side, kvs[m], acc, jnp.bfloat16)
-        late.append(exchange(dkv, "chip", n_chips, m))
+    received, late = [], []
+    for m in range(1, last):
+        acc, dkv = chunk(m, half_picks, info, q_side, sent[m], acc, jnp.bfloat16)
+        received.append(exchange(dkv, "chip", n_chips, m))
+    for a in range(2):
+        acc, dkv = chunk(last, far_picks[a], info, q_side, [far_kv], acc, jnp.bfloat16)
+        late.append(exchange(dkv, "chip", n_chips, last))
+    acc, total = chunk(0, half_picks, info, q_side, own, acc, jnp.float32)
 
     dq_own, dq_send = finish(acc, tok, cols // 2)
     dq_other = exchange(dq_send, "core", 2, 1)
@@ -386,9 +398,9 @@
 
     back, theirs = {}, {}
     for a, slots in enumerate(halves):
-        full = [j * n_heads + slot for j in range(2) for slot in slots]
-        picks = [full] * (n_chips - 1) + [list(range(len(full)))]
-        sums = collect(picks, own, received + [late[a]])
+        n = 2 * len(slots)
+        picks = [[i for i, p in enumerate(half_picks) if p[0] == a]] * last + [list(range(n))]
+        sums = collect(picks, total, received + [late[a]])
         for slot, x in zip(slots, sums):
             back[slot] = exchange(x, "head", n_heads, slot) if slot else x
             theirs[slot] = exchange(back[slot], "core", 2, 1)

time: 63 us -> 65.1 us (1.033)
  starting transfers between devices: 20.9 us -> 24.3 us
  waiting for transfers between devices: 18.7 us -> 17.1 us
    ppermute x25 -> x27, starting transfers between devices: 20.9 us -> 24.3 us  [exchange(): return lax.ppermute(x, axis, [(i, i ^ m) for i in range(size)])]
    ppermute x25 -> x27, waiting for transfers between devices: 18.7 us -> 17.1 us  [exchange(): return lax.ppermute(x, axis, [(i, i ^ m) for i in range(size)])]
    pallas_call x6 -> x8, Pallas kernels: 14.8 us -> 15.1 us  [the longest x5 15 us: chunk(): pl.pallas_call(functools.partial(chunk_kernel, m, picks, first), in_specs...]
  transfers between devices with their start and end apart: 25 -> 27, of which waited for: 9 -> 10; matrix products, arithmetic and copies ran while one was open for 0% -> 0% of each run, Pallas kernels for 31% -> 30%
where the time goes in v3:
time: 65.1 us; the launch traced here: 64.8 us
  starting transfers between devices  24.3 us (37%)
  Pallas kernels  22.4 us (34%)
  waiting for transfers between devices  17.1 us (26%)
  between operations  0.82 us (1%)
    ppermute x27, starting transfers between devices, exchange(): return lax.ppermute(x, axis, [(i, i ^ m) for i in range(size)])  24.3 us
    ppermute x27, waiting for transfers between devices, exchange(): return lax.ppermute(x, axis, [(i, i ^ m) for i in range(size)])  17.1 us
    pallas_call x5, Pallas kernels, chunk(): pl.pallas_call(functools.partial(chunk_kernel, m, picks, first), in_specs...  15 us
    pallas_call x1, Pallas kernels, prepare(): pl.pallas_call(prepare_kernel, in_specs=[SMEM, ANY, ANY, ANY, VMEM], out_...  2.69 us
    pallas_call x1, Pallas kernels, pack(): pl.pallas_call(pack_kernel, in_specs=[SMEM, ANY, ANY], out_specs=[VMEM] *...  1.58 us
    pallas_call x1, Pallas kernels, place(): pl.pallas_call(place_kernel, in_specs=[SMEM, VMEM, VMEM], out_specs=VMEM,...  1.38 us
  transfers between devices with their start and end apart: 27, of which 10 were waited for; matrix products, arithmetic and copies ran while one was open for 0% of the time, Pallas kernels for 30%

profile of v3, /device:TPU:0, one launch (start us, length us, event | category | flops | bytes accessed | tf_op | source)
XLA Modules:
  0.0 64.8 jit_solution(4646616620964544362)
XLA Ops:
  0.6 0.1 pad_add_fusion.where
  0.7 1.6 %pack_kv.1 = (bf16[2,2,64,128]{3,2,1,0:T(8,128)(2,1)S(1)}, bf16[2,2,64,128]{3,2,1,0:T(8,128)(2,1)S(1)}, bf16[2,2,64,128]{3,2,1,0:T(8,128)(2,1)S(1)}, bf16[2,2,64,128]{3,2,1,0:T(8,128)(2,1)S(1)}) custom-call(s32[3]{0:T(128)S(1)} %pad_add_fusion.where, bf16[64,1024]{1,0:T(8,128)(2,1)} %keys.1, bf16[64,1024]{1,0:T(8,128)(2,1)} %values.1), custom_call_target="tpu_custom_call" | custom-call | flops 1000000 | bytes 524288 | tf_op jit(solution)/shard_map/pack_kv/pallas_call | solution.py:72
  2.3 3.1 %collective-permute-start.6 = (bf16[2,2,64,128]{3,2,1,0:T(8,128)(2,1)S(1)}, bf16[2,2,64,128]{3,2,1,0:T(8,128)(2,1)S(1)}, u32[]{:S(2)}, u32[]{:S(2)}) collective-permute-start(bf16[2,2,64,128]{3,2,1,0:T(8,128)(2,1)S(1)} %get-tuple-element.39), channel_id=1, source_target_pairs={{0,1},{1,0},{2,3},{3,2},{4,5},{5,4},{6,7},{7,6},{8,9},{9,8},{10,11... | collective-permute-start | bytes 196616 | tf_op jit(solution)/shard_map/ppermute | solution.py:340
  5.4 2.6 %collective-permute-start.3 = (bf16[2,2,64,128]{3,2,1,0:T(8,128)(2,1)S(1)}, bf16[2,2,64,128]{3,2,1,0:T(8,128)(2,1)S(1)}, u32[]{:S(2)}, u32[]{:S(2)}) collective-permute-start(bf16[2,2,64,128]{3,2,1,0:T(8,128)(2,1)S(1)} %get-tuple-element.38), channel_id=1, source_target_pairs={{0,2},{1,3},{2,0},{3,1},{4,6},{5,7},{6,4},{7,5},{8,10},{9,11},{10,... | collective-permute-start | bytes 196616 | tf_op jit(solution)/shard_map/ppermute | solution.py:340
  8.0 0.0 collective-permute-done.6.refs_0_.refs_2_
  8.0 0.0 collective-permute-start.8
  8.0 2.7 %prepare_q.1 = (bf16[1024,128]{1,0:T(8,128)(2,1)S(1)}, bf16[1024,128]{1,0:T(8,128)(2,1)S(1)}, f32[8,256]{1,0:T(8,128)S(1)}, bf16[1024,128]{1,0:T(8,128)(2,1)S(1)...) custom-call(s32[3]{0:T(128)S(1)} %pad_add_fusion.where, bf16[256,1024]{1,0:T(8,128)(2,1)} %q.1, ...), custom_call_target="tpu_custom_call" | custom-call | flops 10000000 | bytes 2097152 | tf_op jit(solution)/shard_map/prepare_q/pallas_call | solution.py:121
  10.7 0.6 collective-permute-start
  11.3 0.1 collective-permute-start.1
  11.4 2.7 %collective-permute-done.7.refs_1_.refs_3_ = bf16[2,2,64,128]{3,2,1,0:T(8,128)(2,1)S(1)} collective-permute-done((bf16[2,2,64,128]{3,2,1,0:T(8,128)(2,1)S(1)}, bf16[2,2,64,128]{3,2,1,0:T(8,128)(2,1)S(1)}, u32[]{:S(2)}, u32[]{:S(2)}) %collective-permute-start.7) | collective-permute-done | bytes 65568 | tf_op jit(solution)/shard_map/ppermute | solution.py:340
  14.1 0.0 collective-permute-start.9
  14.1 0.0 collective-permute-done.3.refs_1_
  14.1 0.5 collective-permute-start.4
  14.6 0.1 collective-permute-start.5
  14.7 0.7 %collective-permute-done.9.refs_3_.refs_7_ = bf16[2,2,64,128]{3,2,1,0:T(8,128)(2,1)S(1)} collective-permute-done((bf16[2,2,64,128]{3,2,1,0:T(8,128)(2,1)S(1)}, bf16[2,2,64,128]{3,2,1,0:T(8,128)(2,1)S(1)}, u32[]{:S(2)}, u32[]{:S(2)}) %collective-permute-start.9) | collective-permute-done | bytes 65568 | tf_op jit(solution)/shard_map/ppermute | solution.py:340
  15.4 1.6 %collective-permute-start.14 = (bf16[4,2,64,128]{3,2,1,0:T(8,128)(2,1)S(1)}, bf16[4,2,64,128]{3,2,1,0:T(8,128)(2,1)S(1)}, u32[]{:S(2)}, u32[]{:S(2)}) collective-permute-start(bf16[4,2,64,128]{3,2,1,0:T(8,128)(2,1)S(1)} %assemble.4.rest_1_), channel_id=1, source_target_pairs={{0,8},{8,0},{16,24},{24,16},{1,9},{9,1},{17,25},{25,17},{2,10},{10... | collective-permute-start | bytes 393224 | tf_op jit(solution)/shard_map/ppermute | solution.py:340
  16.9 0.0 collective-permute-done.4.refs_2_.refs_4_
  16.9 0.0 collective-permute-done.5.refs_3_.refs_5_
  16.9 0.0 copy-start.1
  16.9 0.6 collective-permute-start.13
  17.5 0.0 collective-permute-start.2
  17.6 0.0 copy-done.1
  17.6 0.1 pad_add_fusion.1.where
  17.7 1.0 %collective-permute-done.2.stats1 = f32[8,256]{1,0:T(8,128)S(1)} collective-permute-done((f32[8,256]{1,0:T(8,128)S(1)}, f32[8,256]{1,0:T(8,128)S(1)}, u32[]{:S(2)}, u32[]{:S(2)}) %collective-permute-start.2) | collective-permute-done | bytes 8224 | tf_op jit(solution)/shard_map/ppermute | solution.py:340
  18.7 1.5 %collective-permute-start.12 = (bf16[4,2,64,128]{3,2,1,0:T(8,128)(2,1)S(1)}, bf16[4,2,64,128]{3,2,1,0:T(8,128)(2,1)S(1)}, u32[]{:S(2)}, u32[]{:S(2)}) collective-permute-start(bf16[4,2,64,128]{3,2,1,0:T(8,128)(2,1)S(1)} %assemble.4.rest_1_), channel_id=1, source_target_pairs={{0,16},{8,24},{16,0},{24,8},{1,17},{9,25},{17,1},{25,9},{2,18},{10... | collective-permute-start | bytes 393224 | tf_op jit(solution)/shard_map/ppermute | solution.py:340
  20.2 1.6 %collective-permute-done.14.rest_1_ = bf16[4,2,64,128]{3,2,1,0:T(8,128)(2,1)S(1)} collective-permute-done((bf16[4,2,64,128]{3,2,1,0:T(8,128)(2,1)S(1)}, bf16[4,2,64,128]{3,2,1,0:T(8,128)(2,1)S(1)}, u32[]{:S(2)}, u32[]{:S(2)}) %collective-permute-start.14) | collective-permute-done | bytes 131104 | tf_op jit(solution)/shard_map/ppermute | solution.py:340
  21.8 1.5 %collective-permute-start.11 = (bf16[4,2,64,128]{3,2,1,0:T(8,128)(2,1)S(1)}, bf16[4,2,64,128]{3,2,1,0:T(8,128)(2,1)S(1)}, u32[]{:S(2)}, u32[]{:S(2)}) collective-permute-start(bf16[4,2,64,128]{3,2,1,0:T(8,128)(2,1)S(1)} %assemble.3.rest_0_), channel_id=1, source_target_pairs={{0,16},{8,24},{16,0},{24,8},{1,17},{9,25},{17,1},{25,9},{2,18},{10... | collective-permute-start | bytes 393224 | tf_op jit(solution)/shard_map/ppermute | solution.py:340
  23.3 0.5 collective-permute-done.13.rest_0_
  23.8 2.4 %collective-permute-start.10 = (bf16[8,2,64,128]{3,2,1,0:T(8,128)(2,1)S(1)}, bf16[8,2,64,128]{3,2,1,0:T(8,128)(2,1)S(1)}, u32[]{:S(2)}, u32[]{:S(2)}) collective-permute-start(bf16[8,2,64,128]{3,2,1,0:T(8,128)(2,1)S(1)} %assemble.5), channel_id=1, source_target_pairs={{0,24},{8,16},{16,8},{24,0},{1,25},{9,17},{17,9},{25,1},{2,26},{10... | collective-permute-start | bytes 786440 | tf_op jit(solution)/shard_map/ppermute | solution.py:340
  26.2 0.0 collective-permute-done.q1
  26.2 0.0 collective-permute-done.1.do1
  26.2 3.4 %chunk.5 = (f32[128,2048]{1,0:T(8,128)S(1)}, bf16[8,2,64,128]{3,2,1,0:T(8,128)(2,1)S(1)}) custom-call(s32[19]{0:T(128)S(1)} %pad_add_fusion.1.where, bf16[1024,128]{1,0:T(8,128)(2,1)S(1)} %get-tuple-element.31.q0, bf16[1024,128]{1,0:T(8,128)(2,1)S(1)} %get-tuple-element.32.do0, f32[8,256]{1,0:T(8,128)S(1)} %get-tuple-element.33.stats0, ...), custom_call_target="tpu_custom_call" | custom-call | flops 2684354560 | bytes 262144 | tf_op jit(solution)/shard_map/chunk/pallas_call | solution.py:224
  29.6 0.0 collective-permute-done.12.rest_1_
  29.6 3.1 %collective-permute-done.11.rest_0_ = bf16[4,2,64,128]{3,2,1,0:T(8,128)(2,1)S(1)} collective-permute-done((bf16[4,2,64,128]{3,2,1,0:T(8,128)(2,1)S(1)}, bf16[4,2,64,128]{3,2,1,0:T(8,128)(2,1)S(1)}, u32[]{:S(2)}, u32[]{:S(2)}) %collective-permute-start.11) | collective-permute-done | bytes 131104 | tf_op jit(solution)/shard_map/ppermute | solution.py:340
  32.7 3.6 %chunk.6 = (f32[128,2048]{1,0:T(8,128)S(1)}, bf16[8,2,64,128]{3,2,1,0:T(8,128)(2,1)S(1)}) custom-call(s32[19]{0:T(128)S(1)} %pad_add_fusion.1.where, bf16[1024,128]{1,0:T(8,128)(2,1)S(1)} %get-tuple-element.31.q0, bf16[1024,128]{1,0:T(8,128)(2,1)S(1)} %get-tuple-element.32.do0, ...), custom_call_target="tpu_custom_call", output_to_operand_aliasing={{0}: (9, {})} | custom-call | flops 2684354560 | bytes 262144 | tf_op jit(solution)/shard_map/chunk/pallas_call | solution.py:224
  36.3 1.6 %collective-permute-start.17 = (bf16[8,2,64,128]{3,2,1,0:T(8,128)(2,1)S(1)}, bf16[8,2,64,128]{3,2,1,0:T(8,128)(2,1)S(1)}, u32[]{:S(2)}, u32[]{:S(2)}) collective-permute-start(bf16[8,2,64,128]{3,2,1,0:T(8,128)(2,1)S(1)} %get-tuple-element.50), channel_id=1, source_target_pairs={{0,16},{8,24},{16,0},{24,8},{1,17},{9,25},{17,1},{25,9},{2,18},{10... | collective-permute-start | bytes 786440 | tf_op jit(solution)/shard_map/ppermute | solution.py:340
  37.9 1.5 %collective-permute-start.16 = (bf16[8,2,64,128]{3,2,1,0:T(8,128)(2,1)S(1)}, bf16[8,2,64,128]{3,2,1,0:T(8,128)(2,1)S(1)}, u32[]{:S(2)}, u32[]{:S(2)}) collective-permute-start(bf16[8,2,64,128]{3,2,1,0:T(8,128)(2,1)S(1)} %get-tuple-element.49), channel_id=1, source_target_pairs={{0,8},{8,0},{16,24},{24,16},{1,9},{9,1},{17,25},{25,17},{2,10},{10... | collective-permute-start | bytes 786440 | tf_op jit(solution)/shard_map/ppermute | solution.py:340
  39.4 0.0 collective-permute-done.10.rest_0_
  39.4 2.2 %chunk.7 = (f32[128,2048]{1,0:T(8,128)S(1)}, bf16[4,2,64,128]{3,2,1,0:T(8,128)(2,1)S(1)}) custom-call(s32[19]{0:T(128)S(1)} %pad_add_fusion.1.where, bf16[1024,128]{1,0:T(8,128)(2,1)S(1)} %get-tuple-element.31.q0, bf16[1024,128]{1,0:T(8,128)(2,1)S(1)} %get-tuple-element.32.do0, ...), custom_call_target="tpu_custom_call", output_to_operand_aliasing={{0}: (8, {})} | custom-call | flops 1342177280 | bytes 524288 | tf_op jit(solution)/shard_map/chunk/pallas_call | solution.py:224
  41.5 2.2 %chunk.8 = (f32[128,2048]{1,0:T(8,128)S(1)}, bf16[4,2,64,128]{3,2,1,0:T(8,128)(2,1)S(1)}) custom-call(s32[19]{0:T(128)S(1)} %pad_add_fusion.1.where, bf16[1024,128]{1,0:T(8,128)(2,1)S(1)} %get-tuple-element.31.q0, bf16[1024,128]{1,0:T(8,128)(2,1)S(1)} %get-tuple-element.32.do0, ...), custom_call_target="tpu_custom_call", output_to_operand_aliasing={{0}: (8, {})} | custom-call | flops 1342177280 | bytes 524288 | tf_op jit(solution)/shard_map/chunk/pallas_call | solution.py:224
  43.7 0.5 collective-permute-start.19
  44.2 2.5 %collective-permute-start.18 = (bf16[4,2,64,128]{3,2,1,0:T(8,128)(2,1)S(1)}, bf16[4,2,64,128]{3,2,1,0:T(8,128)(2,1)S(1)}, u32[]{:S(2)}, u32[]{:S(2)}) collective-permute-start(bf16[4,2,64,128]{3,2,1,0:T(8,128)(2,1)S(1)} %get-tuple-element.51), channel_id=1, source_target_pairs={{0,24},{8,16},{16,8},{24,0},{1,25},{9,17},{17,9},{25,1},{2,26},{10... | collective-permute-start | bytes 393224 | tf_op jit(solution)/shard_map/ppermute | solution.py:340
  46.7 3.8 %chunk.9 = (f32[128,2048]{1,0:T(8,128)S(1)}, f32[8,2,64,128]{3,2,1,0:T(8,128)S(1)}) custom-call(s32[19]{0:T(128)S(1)} %pad_add_fusion.1.where, bf16[1024,128]{1,0:T(8,128)(2,1)S(1)} %get-tuple-element.31.q0, bf16[1024,128]{1,0:T(8,128)(2,1)S(1)} %get-tuple-element.32.do0, f32[8,256]{1,0:T(8,128)S(1)} %get-tuple-element.33.stats0, ...), custom_call_target="tpu_custom_call", output_to_operand_aliasing={{0}: (9, {})} | custom-call | flops 2684354560 | bytes 262144 | tf_op jit(solution)/shard_map/chunk/pallas_call | solution.py:224
  50.5 0.2 finish_q.1
  50.7 0.1 collective-permute-start.15
  50.8 0.0 collective-permute-done.19.refs_2_
  50.8 0.0 collective-permute-done.17.refs_1_
  50.8 0.1 collect.3
  50.9 0.1 collective-permute-start.20
  51.0 3.0 %collective-permute-start.22 = (bf16[2,2,64,128]{3,2,1,0:T(8,128)(2,1)S(1)}, bf16[2,2,64,128]{3,2,1,0:T(8,128)(2,1)S(1)}, u32[]{:S(2)}, u32[]{:S(2)}) collective-permute-start(bf16[2,2,64,128]{3,2,1,0:T(8,128)(2,1)S(1)} %get-tuple-element.56), channel_id=1, source_target_pairs={{0,3},{1,2},{2,1},{3,0},{4,7},{5,6},{6,5},{7,4},{8,11},{9,10},{10,... | collective-permute-start | bytes 196616 | tf_op jit(solution)/shard_map/ppermute | solution.py:340
  54.0 0.1 collect.2
  54.1 0.5 collective-permute-start.21
  54.6 0.0 collective-permute-start.23
  54.6 0.8 %collective-permute-done.20.refs_1_ = bf16[2,2,64,128]{3,2,1,0:T(8,128)(2,1)S(1)} collective-permute-done((bf16[2,2,64,128]{3,2,1,0:T(8,128)(2,1)S(1)}, bf16[2,2,64,128]{3,2,1,0:T(8,128)(2,1)S(1)}, u32[]{:S(2)}, u32[]{:S(2)}) %collective-permute-start.20) | collective-permute-done | bytes 65568 | tf_op jit(solution)/shard_map/ppermute | solution.py:340
  55.4 0.0 collective-permute-start.24
  55.4 3.0 %collective-permute-done.22.refs_3_ = bf16[2,2,64,128]{3,2,1,0:T(8,128)(2,1)S(1)} collective-permute-done((bf16[2,2,64,128]{3,2,1,0:T(8,128)(2,1)S(1)}, bf16[2,2,64,128]{3,2,1,0:T(8,128)(2,1)S(1)}, u32[]{:S(2)}, u32[]{:S(2)}) %collective-permute-start.22) | collective-permute-done | bytes 65568 | tf_op jit(solution)/shard_map/ppermute | solution.py:340
  58.4 0.0 collective-permute-start.26
  58.4 2.4 %collective-permute-done.21.refs_2_ = bf16[2,2,64,128]{3,2,1,0:T(8,128)(2,1)S(1)} collective-permute-done((bf16[2,2,64,128]{3,2,1,0:T(8,128)(2,1)S(1)}, bf16[2,2,64,128]{3,2,1,0:T(8,128)(2,1)S(1)}, u32[]{:S(2)}, u32[]{:S(2)}) %collective-permute-start.21) | collective-permute-done | bytes 65568 | tf_op jit(solution)/shard_map/ppermute | solution.py:340
  60.9 0.0 collective-permute-start.25
  60.9 0.0 collective-permute-done.23.refs_4_
  60.9 0.0 collective-permute-done.24.refs_5_
  60.9 1.2 %collective-permute-done.25.refs_6_ = bf16[2,2,64,128]{3,2,1,0:T(8,128)(2,1)S(1)} collective-permute-done((bf16[2,2,64,128]{3,2,1,0:T(8,128)(2,1)S(1)}, bf16[2,2,64,128]{3,2,1,0:T(8,128)(2,1)S(1)}, u32[]{:S(2)}, u32[]{:S(2)}) %collective-permute-start.25) | collective-permute-done | bytes 65568 | tf_op jit(solution)/shard_map/ppermute | solution.py:340
  62.1 1.3 %unpack_kv.1 = (bf16[64,1024]{1,0:T(8,128)(2,1)}, bf16[64,1024]{1,0:T(8,128)(2,1)}) custom-call(s32[3]{0:T(128)S(1)} %pad_add_fusion.where, bf16[2,2,64,128]{3,2,1,0:T(8,128)(2,1)S(1)} %get-tuple-element.52.refs_0_, bf16[2,2,64,128]{3,2,1,0:T(8,128)(2,1)S(1)} %collective-permute-done.20.refs_1_, bf16[2,2,64,128]{3,2,1,0:T(8,128)(2,1)S(1)} %collective-permute-done.21.refs_2_, ...), custom_call_target="tpu_custom_call" | custom-call | flops 1000000 | bytes 524288 | tf_op jit(solution)/shard_map/unpack_kv/pallas_call | solution.py:328
  63.4 1.4 %place_q.1 = bf16[256,1024]{1,0:T(8,128)(2,1)} custom-call(s32[3]{0:T(128)S(1)} %pad_add_fusion.where, bf16[256,512]{1,0:T(8,128)(2,1)S(1)} %get-tuple-element.46.mine, bf16[256,512]{1,0:T(8,128)(2,1)S(1)} %collective-permute-done.15.theirs), custom_call_target="tpu_custom_call" | custom-call | flops 1000000 | bytes 1048576 | tf_op jit(solution)/shard_map/place_q/pallas_call | solution.py:276
  (11 shorter events, 0.1 us)
Async XLA Ops:
  0.7 7.3 %copy-start = (f32[8,256]{1,0:T(8,128)S(1)}, f32[8,256]{1,0:T(8,128)}, u32[]{:S(2)}) copy-start(f32[8,256]{1,0:T(8,128)} %lse.1) | copy-start | bytes 24580
  2.3 5.7 %collective-permute-start.6 = (bf16[2,2,64,128]{3,2,1,0:T(8,128)(2,1)S(1)}, bf16[2,2,64,128]{3,2,1,0:T(8,128)(2,1)S(1)}, u32[]{:S(2)}, u32[]{:S(2)}) collective-permute-start(bf16[2,2,64,128]{3,2,1,0:T(8,128)(2,1)S(1)} %get-tuple-element.39), channel_id=1, source_target_pairs={{0,1},{1,0},{2,3},{3,2},{4,5},{5,4},{6,7},{7,6},{8,9},{9,8},{10,11... | collective-permute-start | bytes 196616 | tf_op jit(solution)/shard_map/ppermute | solution.py:340
  5.4 8.7 %collective-permute-start.3 = (bf16[2,2,64,128]{3,2,1,0:T(8,128)(2,1)S(1)}, bf16[2,2,64,128]{3,2,1,0:T(8,128)(2,1)S(1)}, u32[]{:S(2)}, u32[]{:S(2)}) collective-permute-start(bf16[2,2,64,128]{3,2,1,0:T(8,128)(2,1)S(1)} %get-tuple-element.38), channel_id=1, source_target_pairs={{0,2},{1,3},{2,0},{3,1},{4,6},{5,7},{6,4},{7,5},{8,10},{9,11},{10,... | collective-permute-start | bytes 196616 | tf_op jit(solution)/shard_map/ppermute | solution.py:340
  8.0 6.1 %collective-permute-start.7 = (bf16[2,2,64,128]{3,2,1,0:T(8,128)(2,1)S(1)}, bf16[2,2,64,128]{3,2,1,0:T(8,128)(2,1)S(1)}, u32[]{:S(2)}, u32[]{:S(2)}) collective-permute-start(bf16[2,2,64,128]{3,2,1,0:T(8,128)(2,1)S(1)} %get-tuple-element.40), channel_id=1, source_target_pairs={{0,3},{1,2},{2,1},{3,0},{4,7},{5,6},{6,5},{7,4},{8,11},{9,10},{10,... | collective-permute-start | bytes 196616 | tf_op jit(solution)/shard_map/ppermute | solution.py:340
  8.0 6.6 %collective-permute-start.8 = (bf16[2,2,64,128]{3,2,1,0:T(8,128)(2,1)S(1)}, bf16[2,2,64,128]{3,2,1,0:T(8,128)(2,1)S(1)}, u32[]{:S(2)}, u32[]{:S(2)}) collective-permute-start(bf16[2,2,64,128]{3,2,1,0:T(8,128)(2,1)S(1)} %collective-permute-done.6.refs_0_.refs_2_), channel_id=1, source_target_pairs={{0,4},{4,0},{1,5},{5,1},{2,6},{6,2},{3,7},{7,3},{8,12},{12,8},{9,1... | collective-permute-start | bytes 196616 | tf_op jit(solution)/shard_map/ppermute | solution.py:340
  10.7 15.5 %collective-permute-start = (bf16[1024,128]{1,0:T(8,128)(2,1)S(1)}, bf16[1024,128]{1,0:T(8,128)(2,1)S(1)}, u32[]{:S(2)}, u32[]{:S(2)}) collective-permute-start(bf16[1024,128]{1,0:T(8,128)(2,1)S(1)} %get-tuple-element.34), channel_id=1, source_target_pairs={{0,4},{4,0},{1,5},{5,1},{2,6},{6,2},{3,7},{7,3},{8,12},{12,8},{9,1... | collective-permute-start | bytes 786440 | tf_op jit(solution)/shard_map/ppermute | solution.py:340
  11.3 15.0 %collective-permute-start.1 = (bf16[1024,128]{1,0:T(8,128)(2,1)S(1)}, bf16[1024,128]{1,0:T(8,128)(2,1)S(1)}, u32[]{:S(2)}, u32[]{:S(2)}) collective-permute-start(bf16[1024,128]{1,0:T(8,128)(2,1)S(1)} %get-tuple-element.35), channel_id=1, source_target_pairs={{0,4},{4,0},{1,5},{5,1},{2,6},{6,2},{3,7},{7,3},{8,12},{12,8},{9,1... | collective-permute-start | bytes 786440 | tf_op jit(solution)/shard_map/ppermute | solution.py:340
  14.1 1.3 %collective-permute-start.9 = (bf16[2,2,64,128]{3,2,1,0:T(8,128)(2,1)S(1)}, bf16[2,2,64,128]{3,2,1,0:T(8,128)(2,1)S(1)}, u32[]{:S(2)}, u32[]{:S(2)}) collective-permute-start(bf16[2,2,64,128]{3,2,1,0:T(8,128)(2,1)S(1)} %collective-permute-done.7.refs_1_.refs_3_), channel_id=1, source_target_pairs={{0,4},{4,0},{1,5},{5,1},{2,6},{6,2},{3,7},{7,3},{8,12},{12,8},{9,1... | collective-permute-start | bytes 196616 | tf_op jit(solution)/shard_map/ppermute | solution.py:340
  14.1 2.8 %collective-permute-start.4 = (bf16[2,2,64,128]{3,2,1,0:T(8,128)(2,1)S(1)}, bf16[2,2,64,128]{3,2,1,0:T(8,128)(2,1)S(1)}, u32[]{:S(2)}, u32[]{:S(2)}) collective-permute-start(bf16[2,2,64,128]{3,2,1,0:T(8,128)(2,1)S(1)} %get-tuple-element.37.refs_0_), channel_id=1, source_target_pairs={{0,4},{4,0},{1,5},{5,1},{2,6},{6,2},{3,7},{7,3},{8,12},{12,8},{9,1... | collective-permute-start | bytes 196616 | tf_op jit(solution)/shard_map/ppermute | solution.py:340
  14.6 2.3 %collective-permute-start.5 = (bf16[2,2,64,128]{3,2,1,0:T(8,128)(2,1)S(1)}, bf16[2,2,64,128]{3,2,1,0:T(8,128)(2,1)S(1)}, u32[]{:S(2)}, u32[]{:S(2)}) collective-permute-start(bf16[2,2,64,128]{3,2,1,0:T(8,128)(2,1)S(1)} %collective-permute-done.3.refs_1_), channel_id=1, source_target_pairs={{0,4},{4,0},{1,5},{5,1},{2,6},{6,2},{3,7},{7,3},{8,12},{12,8},{9,1... | collective-permute-start | bytes 196616 | tf_op jit(solution)/shard_map/ppermute | solution.py:340
  15.4 6.4 %collective-permute-start.14 = (bf16[4,2,64,128]{3,2,1,0:T(8,128)(2,1)S(1)}, bf16[4,2,64,128]{3,2,1,0:T(8,128)(2,1)S(1)}, u32[]{:S(2)}, u32[]{:S(2)}) collective-permute-start(bf16[4,2,64,128]{3,2,1,0:T(8,128)(2,1)S(1)} %assemble.4.rest_1_), channel_id=1, source_target_pairs={{0,8},{8,0},{16,24},{24,16},{1,9},{9,1},{17,25},{25,17},{2,10},{10... | collective-permute-start | bytes 393224 | tf_op jit(solution)/shard_map/ppermute | solution.py:340
  16.9 0.7 %copy-start.1 = (s32[16]{0:T(128)S(1)}, s32[16]{0:T(128)}, u32[]{:S(2)}) copy-start(s32[16]{0:T(128)} %param.13) | copy-start | bytes 196
  16.9 6.8 %collective-permute-start.13 = (bf16[4,2,64,128]{3,2,1,0:T(8,128)(2,1)S(1)}, bf16[4,2,64,128]{3,2,1,0:T(8,128)(2,1)S(1)}, u32[]{:S(2)}, u32[]{:S(2)}) collective-permute-start(bf16[4,2,64,128]{3,2,1,0:T(8,128)(2,1)S(1)} %assemble.3.rest_0_), channel_id=1, source_target_pairs={{0,8},{8,0},{16,24},{24,16},{1,9},{9,1},{17,25},{25,17},{2,10},{10... | collective-permute-start | bytes 393224 | tf_op jit(solution)/shard_map/ppermute | solution.py:340
  17.5 1.2 %collective-permute-start.2 = (f32[8,256]{1,0:T(8,128)S(1)}, f32[8,256]{1,0:T(8,128)S(1)}, u32[]{:S(2)}, u32[]{:S(2)}) collective-permute-start(f32[8,256]{1,0:T(8,128)S(1)} %get-tuple-element.36), channel_id=1, source_target_pairs={{0,4},{4,0},{1,5},{5,1},{2,6},{6,2},{3,7},{7,3},{8,12},{12,8},{9,1... | collective-permute-start | bytes 24584 | tf_op jit(solution)/shard_map/ppermute | solution.py:340
  18.7 10.9 %collective-permute-start.12 = (bf16[4,2,64,128]{3,2,1,0:T(8,128)(2,1)S(1)}, bf16[4,2,64,128]{3,2,1,0:T(8,128)(2,1)S(1)}, u32[]{:S(2)}, u32[]{:S(2)}) collective-permute-start(bf16[4,2,64,128]{3,2,1,0:T(8,128)(2,1)S(1)} %assemble.4.rest_1_), channel_id=1, source_target_pairs={{0,16},{8,24},{16,0},{24,8},{1,17},{9,25},{17,1},{25,9},{2,18},{10... | collective-permute-start | bytes 393224 | tf_op jit(solution)/shard_map/ppermute | solution.py:340
  21.8 10.9 %collective-permute-start.11 = (bf16[4,2,64,128]{3,2,1,0:T(8,128)(2,1)S(1)}, bf16[4,2,64,128]{3,2,1,0:T(8,128)(2,1)S(1)}, u32[]{:S(2)}, u32[]{:S(2)}) collective-permute-start(bf16[4,2,64,128]{3,2,1,0:T(8,128)(2,1)S(1)} %assemble.3.rest_0_), channel_id=1, source_target_pairs={{0,16},{8,24},{16,0},{24,8},{1,17},{9,25},{17,1},{25,9},{2,18},{10... | collective-permute-start | bytes 393224 | tf_op jit(solution)/shard_map/ppermute | solution.py:340
  23.8 15.6 %collective-permute-start.10 = (bf16[8,2,64,128]{3,2,1,0:T(8,128)(2,1)S(1)}, bf16[8,2,64,128]{3,2,1,0:T(8,128)(2,1)S(1)}, u32[]{:S(2)}, u32[]{:S(2)}) collective-permute-start(bf16[8,2,64,128]{3,2,1,0:T(8,128)(2,1)S(1)} %assemble.5), channel_id=1, source_target_pairs={{0,24},{8,16},{16,8},{24,0},{1,25},{9,17},{17,9},{25,1},{2,26},{10... | collective-permute-start | bytes 786440 | tf_op jit(solution)/shard_map/ppermute | solution.py:340
  36.3 14.5 %collective-permute-start.17 = (bf16[8,2,64,128]{3,2,1,0:T(8,128)(2,1)S(1)}, bf16[8,2,64,128]{3,2,1,0:T(8,128)(2,1)S(1)}, u32[]{:S(2)}, u32[]{:S(2)}) collective-permute-start(bf16[8,2,64,128]{3,2,1,0:T(8,128)(2,1)S(1)} %get-tuple-element.50), channel_id=1, source_target_pairs={{0,16},{8,24},{16,0},{24,8},{1,17},{9,25},{17,1},{25,9},{2,18},{10... | collective-permute-start | bytes 786440 | tf_op jit(solution)/shard_map/ppermute | solution.py:340
  37.9 12.9 %collective-permute-start.16 = (bf16[8,2,64,128]{3,2,1,0:T(8,128)(2,1)S(1)}, bf16[8,2,64,128]{3,2,1,0:T(8,128)(2,1)S(1)}, u32[]{:S(2)}, u32[]{:S(2)}) collective-permute-start(bf16[8,2,64,128]{3,2,1,0:T(8,128)(2,1)S(1)} %get-tuple-element.49), channel_id=1, source_target_pairs={{0,8},{8,0},{16,24},{24,16},{1,9},{9,1},{17,25},{25,17},{2,10},{10... | collective-permute-start | bytes 786440 | tf_op jit(solution)/shard_map/ppermute | solution.py:340
  43.7 7.1 %collective-permute-start.19 = (bf16[4,2,64,128]{3,2,1,0:T(8,128)(2,1)S(1)}, bf16[4,2,64,128]{3,2,1,0:T(8,128)(2,1)S(1)}, u32[]{:S(2)}, u32[]{:S(2)}) collective-permute-start(bf16[4,2,64,128]{3,2,1,0:T(8,128)(2,1)S(1)} %get-tuple-element.53), channel_id=1, source_target_pairs={{0,24},{8,16},{16,8},{24,0},{1,25},{9,17},{17,9},{25,1},{2,26},{10... | collective-permute-start | bytes 393224 | tf_op jit(solution)/shard_map/ppermute | solution.py:340
  44.2 9.7 %collective-permute-start.18 = (bf16[4,2,64,128]{3,2,1,0:T(8,128)(2,1)S(1)}, bf16[4,2,64,128]{3,2,1,0:T(8,128)(2,1)S(1)}, u32[]{:S(2)}, u32[]{:S(2)}) collective-permute-start(bf16[4,2,64,128]{3,2,1,0:T(8,128)(2,1)S(1)} %get-tuple-element.51), channel_id=1, source_target_pairs={{0,24},{8,16},{16,8},{24,0},{1,25},{9,17},{17,9},{25,1},{2,26},{10... | collective-permute-start | bytes 393224 | tf_op jit(solution)/shard_map/ppermute | solution.py:340
  50.7 12.7 %collective-permute-start.15 = (bf16[256,512]{1,0:T(8,128)(2,1)S(1)}, bf16[256,512]{1,0:T(8,128)(2,1)S(1)}, u32[]{:S(2)}, u32[]{:S(2)}) collective-permute-start(bf16[256,512]{1,0:T(8,128)(2,1)S(1)} %get-tuple-element.47), channel_id=1, source_target_pairs={{0,4},{4,0},{1,5},{5,1},{2,6},{6,2},{3,7},{7,3},{8,12},{12,8},{9,1... | collective-permute-start | bytes 786440 | tf_op jit(solution)/shard_map/ppermute | solution.py:340
  50.9 4.5 %collective-permute-start.20 = (bf16[2,2,64,128]{3,2,1,0:T(8,128)(2,1)S(1)}, bf16[2,2,64,128]{3,2,1,0:T(8,128)(2,1)S(1)}, u32[]{:S(2)}, u32[]{:S(2)}) collective-permute-start(bf16[2,2,64,128]{3,2,1,0:T(8,128)(2,1)S(1)} %get-tuple-element.54), channel_id=1, source_target_pairs={{0,1},{1,0},{2,3},{3,2},{4,5},{5,4},{6,7},{7,6},{8,9},{9,8},{10,11... | collective-permute-start | bytes 196616 | tf_op jit(solution)/shard_map/ppermute | solution.py:340
  51.0 7.5 %collective-permute-start.22 = (bf16[2,2,64,128]{3,2,1,0:T(8,128)(2,1)S(1)}, bf16[2,2,64,128]{3,2,1,0:T(8,128)(2,1)S(1)}, u32[]{:S(2)}, u32[]{:S(2)}) collective-permute-start(bf16[2,2,64,128]{3,2,1,0:T(8,128)(2,1)S(1)} %get-tuple-element.56), channel_id=1, source_target_pairs={{0,3},{1,2},{2,1},{3,0},{4,7},{5,6},{6,5},{7,4},{8,11},{9,10},{10,... | collective-permute-start | bytes 196616 | tf_op jit(solution)/shard_map/ppermute | solution.py:340
  54.1 6.8 %collective-permute-start.21 = (bf16[2,2,64,128]{3,2,1,0:T(8,128)(2,1)S(1)}, bf16[2,2,64,128]{3,2,1,0:T(8,128)(2,1)S(1)}, u32[]{:S(2)}, u32[]{:S(2)}) collective-permute-start(bf16[2,2,64,128]{3,2,1,0:T(8,128)(2,1)S(1)} %get-tuple-element.55), channel_id=1, source_target_pairs={{0,2},{1,3},{2,0},{3,1},{4,6},{5,7},{6,4},{7,5},{8,10},{9,11},{10,... | collective-permute-start | bytes 196616 | tf_op jit(solution)/shard_map/ppermute | solution.py:340
  54.6 6.3 %collective-permute-start.23 = (bf16[2,2,64,128]{3,2,1,0:T(8,128)(2,1)S(1)}, bf16[2,2,64,128]{3,2,1,0:T(8,128)(2,1)S(1)}, u32[]{:S(2)}, u32[]{:S(2)}) collective-permute-start(bf16[2,2,64,128]{3,2,1,0:T(8,128)(2,1)S(1)} %get-tuple-element.52.refs_0_), channel_id=1, source_target_pairs={{0,4},{4,0},{1,5},{5,1},{2,6},{6,2},{3,7},{7,3},{8,12},{12,8},{9,1... | collective-permute-start | bytes 196616 | tf_op jit(solution)/shard_map/ppermute | solution.py:340
  55.4 5.5 %collective-permute-start.24 = (bf16[2,2,64,128]{3,2,1,0:T(8,128)(2,1)S(1)}, bf16[2,2,64,128]{3,2,1,0:T(8,128)(2,1)S(1)}, u32[]{:S(2)}, u32[]{:S(2)}) collective-permute-start(bf16[2,2,64,128]{3,2,1,0:T(8,128)(2,1)S(1)} %collective-permute-done.20.refs_1_), channel_id=1, source_target_pairs={{0,4},{4,0},{1,5},{5,1},{2,6},{6,2},{3,7},{7,3},{8,12},{12,8},{9,1... | collective-permute-start | bytes 196616 | tf_op jit(solution)/shard_map/ppermute | solution.py:340
  58.4 2.5 %collective-permute-start.26 = (bf16[2,2,64,128]{3,2,1,0:T(8,128)(2,1)S(1)}, bf16[2,2,64,128]{3,2,1,0:T(8,128)(2,1)S(1)}, u32[]{:S(2)}, u32[]{:S(2)}) collective-permute-start(bf16[2,2,64,128]{3,2,1,0:T(8,128)(2,1)S(1)} %collective-permute-done.22.refs_3_), channel_id=1, source_target_pairs={{0,4},{4,0},{1,5},{5,1},{2,6},{6,2},{3,7},{7,3},{8,12},{12,8},{9,1... | collective-permute-start | bytes 196616 | tf_op jit(solution)/shard_map/ppermute | solution.py:340
  60.9 1.3 %collective-permute-start.25 = (bf16[2,2,64,128]{3,2,1,0:T(8,128)(2,1)S(1)}, bf16[2,2,64,128]{3,2,1,0:T(8,128)(2,1)S(1)}, u32[]{:S(2)}, u32[]{:S(2)}) collective-permute-start(bf16[2,2,64,128]{3,2,1,0:T(8,128)(2,1)S(1)} %collective-permute-done.21.refs_2_), channel_id=1, source_target_pairs={{0,4},{4,0},{1,5},{5,1},{2,6},{6,2},{3,7},{7,3},{8,12},{12,8},{9,1... | collective-permute-start | bytes 196616 | tf_op jit(solution)/shard_map/ppermute | solution.py:340

commit v4 on v3

--- a/solution.py
+++ b/solution.py
@@ -154,8 +154,9 @@
     )(*[near(x) for x in mine], *[near(x) for x in theirs])
 
 
-def chunk_kernel(m, picks, first, where, q0, do0, stats0, q1, do1, stats1, *rest):
-    acc, dkv = rest[-2:]
+def chunk_kernel(m, groups, first, where, q0, do0, stats0, q1, do1, stats1, *rest):
+    acc, dkvs = rest[-1 - len(groups)], rest[-len(groups) :]
+    picks = [p for group in groups for p in group]
     n_kv = max(p[0] for p in picks) + 1
     kvs, rest = rest[:n_kv], rest[n_kv:]
     c, core, z = where[0], where[1], where[2]
@@ -208,27 +209,29 @@
             term = jnp.dot(kts[t], score, preferred_element_type=jnp.float32)
             dq = term if dq is None else dq + term
         acc[:, b * width : (b + 1) * width] = dq
+    targets = [dkv.at[i] for dkv, group in zip(dkvs, groups) for i in range(len(group))]
     for t, tile in enumerate(tiles):
         for n, p in enumerate(tile):
             rows = slice(n * piece, (n + 1) * piece)
-            dkv[p, 0] = (dks[t][rows] * SCALE).astype(dkv.dtype)
-            dkv[p, 1] = dvs[t][rows].astype(dkv.dtype)
-
-
-def chunk(m, picks, where, q_side, kvs, acc, out_dtype):
+            targets[p][0] = (dks[t][rows] * SCALE).astype(targets[p].dtype)
+            targets[p][1] = dvs[t][rows].astype(targets[p].dtype)
+
+
+def chunk(m, groups, where, q_side, kvs, acc, out_dtype):
     first = acc is None
     width = q_side[0].shape[0] * 2
     acc_out = pltpu.VMEM((HEAD_SIZE, width), jnp.float32)
     args = [near(x) for x in q_side] + [near(kv) for kv in kvs] + ([] if first else [near(acc)])
-    out = (len(picks),) + kvs[0].shape[1:]
-    return pl.pallas_call(
-        functools.partial(chunk_kernel, m, picks, first),
+    outs = [pltpu.VMEM((len(g),) + kvs[0].shape[1:], out_dtype) for g in groups]
+    rows = sum(len(g) for g in groups) * kvs[0].shape[2]
+    return pl.pallas_call(
+        functools.partial(chunk_kernel, m, groups, first),
         in_specs=[SMEM] + [VMEM] * len(args),
-        out_specs=[VMEM] * 2,
-        out_shape=[acc_out, pltpu.VMEM(out, out_dtype)],
+        out_specs=[VMEM] * (1 + len(outs)),
+        out_shape=[acc_out] + outs,
         input_output_aliases={} if first else {len(args): 0},
         compiler_params=params(20),
-        cost_estimate=cost(5 * 2 * out[0] * out[2] * width * HEAD_SIZE * 2, 4 * kvs[0].size),
+        cost_estimate=cost(5 * 2 * rows * width * HEAD_SIZE * 2, 4 * kvs[0].size),
         name="chunk",
     )(where, *args)
 
@@ -345,6 +348,10 @@
     return tuple(slots[: n_heads // 2]), tuple(slots[n_heads // 2 :])
 
 
+def home_halves(n_heads):
+    return tuple(range(n_heads // 2, n_heads)), tuple(range(n_heads // 2))
+
+
 def local(n_chips, n_heads, queries, keys, values, outputs, out_grad, log_norm, block_order):
     where = jnp.stack([lax.axis_index("chip"), lax.axis_index("core"), lax.axis_index("head")])
     tok, cols = queries.shape
@@ -368,9 +375,8 @@
         own.append(assemble([zr[m] for m in slots], [other[m] for m in slots]))
         for m in range(1, last):
             sent[m].append(exchange(own[a], "chip", n_chips, m))
-    full = [m for slots in halves for m in slots]
-    whole = assemble([zr[m] for m in full], [other[m] for m in full])
-    far_kv = exchange(whole, "chip", n_chips, last)
+    for a, (first, second) in enumerate(((1, last ^ 1), (last ^ 1, 1))):
+        sent[last].append(exchange(sent[first][a], "chip", n_chips, second))
 
     half_picks = [
         (a, j * len(slots) + i, j, slot)
@@ -378,29 +384,32 @@
         for j in range(2)
         for i, slot in enumerate(slots)
     ]
-    far_picks = [
-        [(0, j * n_heads + full.index(slot), j, slot) for j in range(2) for slot in slots]
-        for slots in halves
-    ]
+    home = home_halves(n_heads)
+    home_picks = [[p for p in half_picks if p[3] in slots] for slots in home]
     acc = None
-    received, late = [], []
-    for m in range(1, last):
-        acc, dkv = chunk(m, half_picks, info, q_side, sent[m], acc, jnp.bfloat16)
-        received.append(exchange(dkv, "chip", n_chips, m))
-    for a in range(2):
-        acc, dkv = chunk(last, far_picks[a], info, q_side, [far_kv], acc, jnp.bfloat16)
-        late.append(exchange(dkv, "chip", n_chips, last))
-    acc, total = chunk(0, half_picks, info, q_side, own, acc, jnp.float32)
+    total, received, late = [], [], [[], []]
+    acc, dkv = chunk(0, home_picks[:1], info, q_side, own, acc, jnp.float32)
+    total.append(dkv)
+    for m in range(1, n_chips):
+        groups = [half_picks] if m < last - 1 else home_picks
+        acc, *parts = chunk(m, groups, info, q_side, sent[m], acc, jnp.bfloat16)
+        for a, dkv in enumerate(parts):
+            dkv = exchange(dkv, "chip", n_chips, m)
+            (received if m < last - 1 else late[a]).append(dkv)
+    acc, dkv = chunk(0, home_picks[1:], info, q_side, own, acc, jnp.float32)
+    total.append(dkv)
 
     dq_own, dq_send = finish(acc, tok, cols // 2)
     dq_other = exchange(dq_send, "core", 2, 1)
     dq = place(where, dq_own, dq_other)
 
     back, theirs = {}, {}
-    for a, slots in enumerate(halves):
-        n = 2 * len(slots)
-        picks = [[i for i, p in enumerate(half_picks) if p[0] == a]] * last + [list(range(n))]
-        sums = collect(picks, total, received + [late[a]])
+    for a, slots in enumerate(home):
+        wanted = [(j, slot) for j in range(2) for slot in slots]
+        part = [[p[2:] for p in home_picks[a]].index(w) for w in wanted]
+        full = [[p[2:] for p in half_picks].index(w) for w in wanted]
+        picks = [part] + [full] * len(received) + [part] * len(late[a])
+        sums = collect(picks, total[a], received + late[a])
         for slot, x in zip(slots, sums):
             back[slot] = exchange(x, "head", n_heads, slot) if slot else x
             theirs[slot] = exchange(back[slot], "core", 2, 1)

time: 65.1 us -> 60.6 us (0.931)
  waiting for transfers between devices: 17.1 us -> 12 us
  starting transfers between devices: 24.3 us -> 25 us
    ppermute x27 -> x29, waiting for transfers between devices: 17.1 us -> 12 us  [exchange(): return lax.ppermute(x, axis, [(i, i ^ m) for i in range(size)])]
    ppermute x27 -> x29, starting transfers between devices: 24.3 us -> 25 us  [exchange(): return lax.ppermute(x, axis, [(i, i ^ m) for i in range(size)])]
  transfers between devices with their start and end apart: 27 -> 29, of which waited for: 10 -> 9; matrix products, arithmetic and copies ran while one was open for 0% -> 0% of each run, Pallas kernels for 30% -> 32%
where the time goes in v4:
time: 60.6 us; the launch traced here: 60.3 us
  starting transfers between devices  25 us (41%)
  Pallas kernels  22.3 us (37%)
  waiting for transfers between devices  12 us (20%)
  between operations  0.79 us (1%)
    ppermute x29, starting transfers between devices, exchange(): return lax.ppermute(x, axis, [(i, i ^ m) for i in range(size)])  25 us
    pallas_call x5, Pallas kernels, chunk(): pl.pallas_call(functools.partial(chunk_kernel, m, groups, first), in_spec...  15 us
    ppermute x29, waiting for transfers between devices, exchange(): return lax.ppermute(x, axis, [(i, i ^ m) for i in range(size)])  12 us
    pallas_call x1, Pallas kernels, prepare(): pl.pallas_call(prepare_kernel, in_specs=[SMEM, ANY, ANY, ANY, VMEM], out_...  2.69 us
    pallas_call x1, Pallas kernels, pack(): pl.pallas_call(pack_kernel, in_specs=[SMEM, ANY, ANY], out_specs=[VMEM] *...  1.58 us
    pallas_call x1, Pallas kernels, place(): pl.pallas_call(place_kernel, in_specs=[SMEM, VMEM, VMEM], out_specs=VMEM,...  1.38 us
    pallas_call x1, Pallas kernels, unpack(): pl.pallas_call(functools.partial(unpack_kernel, n), in_specs=[SMEM] + [VM...  1.3 us
  transfers between devices with their start and end apart: 29, of which 9 were waited for; matrix products, arithmetic and copies ran while one was open for 0% of the time, Pallas kernels for 32%

profile of v4, /device:TPU:0, one launch (start us, length us, event | category | flops | bytes accessed | tf_op | source)
XLA Modules:
  0.0 60.3 jit_solution(1265702086872287791)
XLA Ops:
  0.6 0.1 pad_add_fusion.where
  0.7 1.6 %pack_kv.1 = (bf16[2,2,64,128]{3,2,1,0:T(8,128)(2,1)S(1)}, bf16[2,2,64,128]{3,2,1,0:T(8,128)(2,1)S(1)}, bf16[2,2,64,128]{3,2,1,0:T(8,128)(2,1)S(1)}, bf16[2,2,64,128]{3,2,1,0:T(8,128)(2,1)S(1)}) custom-call(s32[3]{0:T(128)S(1)} %pad_add_fusion.where, bf16[64,1024]{1,0:T(8,128)(2,1)} %keys.1, bf16[64,1024]{1,0:T(8,128)(2,1)} %values.1), custom_call_target="tpu_custom_call" | custom-call | flops 1000000 | bytes 524288 | tf_op jit(solution)/shard_map/pack_kv/pallas_call | solution.py:72
  2.3 4.1 %collective-permute-start.3 = (bf16[2,2,64,128]{3,2,1,0:T(8,128)(2,1)S(1)}, bf16[2,2,64,128]{3,2,1,0:T(8,128)(2,1)S(1)}, u32[]{:S(2)}, u32[]{:S(2)}) collective-permute-start(bf16[2,2,64,128]{3,2,1,0:T(8,128)(2,1)S(1)} %get-tuple-element.40), channel_id=1, source_target_pairs={{0,2},{1,3},{2,0},{3,1},{4,6},{5,7},{6,4},{7,5},{8,10},{9,11},{10,... | collective-permute-start | bytes 196616 | tf_op jit(solution)/shard_map/ppermute | solution.py:343
  6.4 1.6 %collective-permute-start.6 = (bf16[2,2,64,128]{3,2,1,0:T(8,128)(2,1)S(1)}, bf16[2,2,64,128]{3,2,1,0:T(8,128)(2,1)S(1)}, u32[]{:S(2)}, u32[]{:S(2)}) collective-permute-start(bf16[2,2,64,128]{3,2,1,0:T(8,128)(2,1)S(1)} %get-tuple-element.41), channel_id=1, source_target_pairs={{0,1},{1,0},{2,3},{3,2},{4,5},{5,4},{6,7},{7,6},{8,9},{9,8},{10,11... | collective-permute-start | bytes 196616 | tf_op jit(solution)/shard_map/ppermute | solution.py:343
  8.0 0.0 collective-permute-start.7
  8.0 0.0 collective-permute-start.4
  8.0 2.7 %prepare_q.1 = (bf16[1024,128]{1,0:T(8,128)(2,1)S(1)}, bf16[1024,128]{1,0:T(8,128)(2,1)S(1)}, f32[8,256]{1,0:T(8,128)S(1)}, bf16[1024,128]{1,0:T(8,128)(2,1)S(1)...) custom-call(s32[3]{0:T(128)S(1)} %pad_add_fusion.where, bf16[256,1024]{1,0:T(8,128)(2,1)} %q.1, ...), custom_call_target="tpu_custom_call" | custom-call | flops 10000000 | bytes 2097152 | tf_op jit(solution)/shard_map/prepare_q/pallas_call | solution.py:121
  10.7 0.6 collective-permute-start
  11.3 0.0 collective-permute-done.3.refs_1_
  11.3 0.1 collective-permute-start.1
  11.4 0.0 collective-permute-done.6.refs_0_
  11.4 0.4 collective-permute-start.5
  11.8 2.3 %collective-permute-done.7.refs_1_ = bf16[2,2,64,128]{3,2,1,0:T(8,128)(2,1)S(1)} collective-permute-done((bf16[2,2,64,128]{3,2,1,0:T(8,128)(2,1)S(1)}, bf16[2,2,64,128]{3,2,1,0:T(8,128)(2,1)S(1)}, u32[]{:S(2)}, u32[]{:S(2)}) %collective-permute-start.7) | collective-permute-done | bytes 65568 | tf_op jit(solution)/shard_map/ppermute | solution.py:343
  14.1 0.0 collective-permute-start.8
  14.1 0.0 collective-permute-done.4.refs_2_
  14.1 0.5 collective-permute-start.9
  14.6 0.0 collective-permute-done.5.refs_3_
  14.6 1.6 %collective-permute-start.10 = (bf16[4,2,64,128]{3,2,1,0:T(8,128)(2,1)S(1)}, bf16[4,2,64,128]{3,2,1,0:T(8,128)(2,1)S(1)}, u32[]{:S(2)}, u32[]{:S(2)}) collective-permute-start(bf16[4,2,64,128]{3,2,1,0:T(8,128)(2,1)S(1)} %assemble.2.rest_0_), channel_id=1, source_target_pairs={{0,8},{8,0},{16,24},{24,16},{1,9},{9,1},{17,25},{25,17},{2,10},{10... | collective-permute-start | bytes 393224 | tf_op jit(solution)/shard_map/ppermute | solution.py:343
  16.2 0.0 collective-permute-done.8.refs_2_
  16.2 0.0 collective-permute-done.9.refs_3_
  16.2 0.0 copy-start.1
  16.2 1.6 %collective-permute-start.12 = (bf16[4,2,64,128]{3,2,1,0:T(8,128)(2,1)S(1)}, bf16[4,2,64,128]{3,2,1,0:T(8,128)(2,1)S(1)}, u32[]{:S(2)}, u32[]{:S(2)}) collective-permute-start(bf16[4,2,64,128]{3,2,1,0:T(8,128)(2,1)S(1)} %assemble.3.rest_1_), channel_id=1, source_target_pairs={{0,16},{8,24},{16,0},{24,8},{1,17},{9,25},{17,1},{25,9},{2,18},{10... | collective-permute-start | bytes 393224 | tf_op jit(solution)/shard_map/ppermute | solution.py:343
  17.8 0.0 collective-permute-start.2
  17.8 1.2 %collective-permute-done.2.stats1 = f32[8,256]{1,0:T(8,128)S(1)} collective-permute-done((f32[8,256]{1,0:T(8,128)S(1)}, f32[8,256]{1,0:T(8,128)S(1)}, u32[]{:S(2)}, u32[]{:S(2)}) %collective-permute-start.2) | collective-permute-done | bytes 8224 | tf_op jit(solution)/shard_map/ppermute | solution.py:343
  19.0 0.8 %collective-permute-start.15 = (bf16[4,2,64,128]{3,2,1,0:T(8,128)(2,1)S(1)}, bf16[4,2,64,128]{3,2,1,0:T(8,128)(2,1)S(1)}, u32[]{:S(2)}, u32[]{:S(2)}) collective-permute-start(bf16[4,2,64,128]{3,2,1,0:T(8,128)(2,1)S(1)} %assemble.3.rest_1_), channel_id=1, source_target_pairs={{0,8},{8,0},{16,24},{24,16},{1,9},{9,1},{17,25},{25,17},{2,10},{10... | collective-permute-start | bytes 393224 | tf_op jit(solution)/shard_map/ppermute | solution.py:343
  19.8 0.1 pad_add_fusion.1.where
  19.9 0.2 collective-permute-done.10.rest_0_
  20.1 1.5 %collective-permute-start.14 = (bf16[4,2,64,128]{3,2,1,0:T(8,128)(2,1)S(1)}, bf16[4,2,64,128]{3,2,1,0:T(8,128)(2,1)S(1)}, u32[]{:S(2)}, u32[]{:S(2)}) collective-permute-start(bf16[4,2,64,128]{3,2,1,0:T(8,128)(2,1)S(1)} %assemble.2.rest_0_), channel_id=1, source_target_pairs={{0,16},{8,24},{16,0},{24,8},{1,17},{9,25},{17,1},{25,9},{2,18},{10... | collective-permute-start | bytes 393224 | tf_op jit(solution)/shard_map/ppermute | solution.py:343
  21.6 0.0 collective-permute-done.12.rest_1_
  21.6 1.3 %collective-permute-start.11 = (bf16[4,2,64,128]{3,2,1,0:T(8,128)(2,1)S(1)}, bf16[4,2,64,128]{3,2,1,0:T(8,128)(2,1)S(1)}, u32[]{:S(2)}, u32[]{:S(2)}) collective-permute-start(bf16[4,2,64,128]{3,2,1,0:T(8,128)(2,1)S(1)} %collective-permute-done.10.rest_0_), channel_id=1, source_target_pairs={{0,16},{8,24},{16,0},{24,8},{1,17},{9,25},{17,1},{25,9},{2,18},{10... | collective-permute-start | bytes 393224 | tf_op jit(solution)/shard_map/ppermute | solution.py:343
  22.9 0.0 collective-permute-done.q1
  22.9 1.4 %collective-permute-start.13 = (bf16[4,2,64,128]{3,2,1,0:T(8,128)(2,1)S(1)}, bf16[4,2,64,128]{3,2,1,0:T(8,128)(2,1)S(1)}, u32[]{:S(2)}, u32[]{:S(2)}) collective-permute-start(bf16[4,2,64,128]{3,2,1,0:T(8,128)(2,1)S(1)} %collective-permute-done.12.rest_1_), channel_id=1, source_target_pairs={{0,8},{8,0},{16,24},{24,16},{1,9},{9,1},{17,25},{25,17},{2,10},{10... | collective-permute-start | bytes 393224 | tf_op jit(solution)/shard_map/ppermute | solution.py:343
  24.4 0.0 collective-permute-done.1.do1
  24.4 2.1 %chunk.5 = (f32[128,2048]{1,0:T(8,128)S(1)}, f32[4,2,64,128]{3,2,1,0:T(8,128)S(1)}) custom-call(s32[19]{0:T(128)S(1)} %pad_add_fusion.1.where, bf16[1024,128]{1,0:T(8,128)(2,1)S(1)} %get-tuple-element.33.q0, bf16[1024,128]{1,0:T(8,128)(2,1)S(1)} %get-tuple-element.34.do0, f32[8,256]{1,0:T(8,128)S(1)} %get-tuple-element.35.stats0, ...), custom_call_target="tpu_custom_call" | custom-call | flops 1342177280 | bytes 262144 | tf_op jit(solution)/shard_map/chunk/pallas_call | solution.py:227
  26.5 0.0 collective-permute-done.15.rest_1_
  26.5 3.6 %chunk.6 = (f32[128,2048]{1,0:T(8,128)S(1)}, bf16[8,2,64,128]{3,2,1,0:T(8,128)(2,1)S(1)}) custom-call(s32[19]{0:T(128)S(1)} %pad_add_fusion.1.where, bf16[1024,128]{1,0:T(8,128)(2,1)S(1)} %get-tuple-element.33.q0, bf16[1024,128]{1,0:T(8,128)(2,1)S(1)} %get-tuple-element.34.do0, ...), custom_call_target="tpu_custom_call", output_to_operand_aliasing={{0}: (9, {})} | custom-call | flops 2684354560 | bytes 262144 | tf_op jit(solution)/shard_map/chunk/pallas_call | solution.py:227
  30.1 0.0 collective-permute-done.14.rest_0_
  30.1 3.6 %chunk.7 = (f32[128,2048]{1,0:T(8,128)S(1)}, bf16[4,2,64,128]{3,2,1,0:T(8,128)(2,1)S(1)}, bf16[4,2,64,128]{3,2,1,0:T(8,128)(2,1)S(1)}) custom-call(s32[19]{0:T(128)S(1)} %pad_add_fusion.1.where, bf16[1024,128]{1,0:T(8,128)(2,1)S(1)} %get-tuple-element.33.q0, bf16[1024,128]{1,0:T(8,128)(2,1)S(1)} %get-tuple-element.34.do0, ...), custom_call_target="tpu_custom_call", output_to_operand_aliasing={{0}: (9, {})} | custom-call | flops 2684354560 | bytes 262144 | tf_op jit(solution)/shard_map/chunk/pallas_call | solution.py:227
  33.7 0.9 %collective-permute-start.18 = (bf16[4,2,64,128]{3,2,1,0:T(8,128)(2,1)S(1)}, bf16[4,2,64,128]{3,2,1,0:T(8,128)(2,1)S(1)}, u32[]{:S(2)}, u32[]{:S(2)}) collective-permute-start(bf16[4,2,64,128]{3,2,1,0:T(8,128)(2,1)S(1)} %get-tuple-element.52), channel_id=1, source_target_pairs={{0,16},{8,24},{16,0},{24,8},{1,17},{9,25},{17,1},{25,9},{2,18},{10... | collective-permute-start | bytes 393224 | tf_op jit(solution)/shard_map/ppermute | solution.py:343
  34.6 1.2 %collective-permute-start.21 = (bf16[4,2,64,128]{3,2,1,0:T(8,128)(2,1)S(1)}, bf16[4,2,64,128]{3,2,1,0:T(8,128)(2,1)S(1)}, u32[]{:S(2)}, u32[]{:S(2)}) collective-permute-start(bf16[4,2,64,128]{3,2,1,0:T(8,128)(2,1)S(1)} %get-tuple-element.57), channel_id=1, source_target_pairs={{0,16},{8,24},{16,0},{24,8},{1,17},{9,25},{17,1},{25,9},{2,18},{10... | collective-permute-start | bytes 393224 | tf_op jit(solution)/shard_map/ppermute | solution.py:343
  35.8 0.6 collective-permute-start.17
  36.3 0.0 collective-permute-done.11.rest_0_
  36.3 0.0 collective-permute-done.13.rest_1_
  36.3 3.6 %chunk.8 = (f32[128,2048]{1,0:T(8,128)S(1)}, bf16[4,2,64,128]{3,2,1,0:T(8,128)(2,1)S(1)}, bf16[4,2,64,128]{3,2,1,0:T(8,128)(2,1)S(1)}) custom-call(s32[19]{0:T(128)S(1)} %pad_add_fusion.1.where, bf16[1024,128]{1,0:T(8,128)(2,1)S(1)} %get-tuple-element.33.q0, bf16[1024,128]{1,0:T(8,128)(2,1)S(1)} %get-tuple-element.34.do0, ...), custom_call_target="tpu_custom_call", output_to_operand_aliasing={{0}: (9, {})} | custom-call | flops 2684354560 | bytes 262144 | tf_op jit(solution)/shard_map/chunk/pallas_call | solution.py:227
  39.9 1.8 %collective-permute-start.19 = (bf16[4,2,64,128]{3,2,1,0:T(8,128)(2,1)S(1)}, bf16[4,2,64,128]{3,2,1,0:T(8,128)(2,1)S(1)}, u32[]{:S(2)}, u32[]{:S(2)}) collective-permute-start(bf16[4,2,64,128]{3,2,1,0:T(8,128)(2,1)S(1)} %get-tuple-element.53), channel_id=1, source_target_pairs={{0,24},{8,16},{16,8},{24,0},{1,25},{9,17},{17,9},{25,1},{2,26},{10... | collective-permute-start | bytes 393224 | tf_op jit(solution)/shard_map/ppermute | solution.py:343
  41.7 1.2 %collective-permute-start.22 = (bf16[4,2,64,128]{3,2,1,0:T(8,128)(2,1)S(1)}, bf16[4,2,64,128]{3,2,1,0:T(8,128)(2,1)S(1)}, u32[]{:S(2)}, u32[]{:S(2)}) collective-permute-start(bf16[4,2,64,128]{3,2,1,0:T(8,128)(2,1)S(1)} %get-tuple-element.58), channel_id=1, source_target_pairs={{0,24},{8,16},{16,8},{24,0},{1,25},{9,17},{17,9},{25,1},{2,26},{10... | collective-permute-start | bytes 393224 | tf_op jit(solution)/shard_map/ppermute | solution.py:343
  42.9 2.2 %chunk.9 = (f32[128,2048]{1,0:T(8,128)S(1)}, f32[4,2,64,128]{3,2,1,0:T(8,128)S(1)}) custom-call(s32[19]{0:T(128)S(1)} %pad_add_fusion.1.where, bf16[1024,128]{1,0:T(8,128)(2,1)S(1)} %get-tuple-element.33.q0, bf16[1024,128]{1,0:T(8,128)(2,1)S(1)} %get-tuple-element.34.do0, f32[8,256]{1,0:T(8,128)S(1)} %get-tuple-element.35.stats0, ...), custom_call_target="tpu_custom_call", output_to_operand_aliasing={{0}: (9, {})} | custom-call | flops 1342177280 | bytes 262144 | tf_op jit(solution)/shard_map/chunk/pallas_call | solution.py:227
  45.1 0.2 finish_q.1
  45.3 0.1 collective-permute-start.16
  45.4 2.6 %collective-permute-done.22.refs_2_ = bf16[4,2,64,128]{3,2,1,0:T(8,128)(2,1)S(1)} collective-permute-done((bf16[4,2,64,128]{3,2,1,0:T(8,128)(2,1)S(1)}, bf16[4,2,64,128]{3,2,1,0:T(8,128)(2,1)S(1)}, u32[]{:S(2)}, u32[]{:S(2)}) %collective-permute-start.22) | collective-permute-done | bytes 131104 | tf_op jit(solution)/shard_map/ppermute | solution.py:343
  48.0 0.1 collect.3
  48.1 1.4 %collective-permute-start.23 = (bf16[2,2,64,128]{3,2,1,0:T(8,128)(2,1)S(1)}, bf16[2,2,64,128]{3,2,1,0:T(8,128)(2,1)S(1)}, u32[]{:S(2)}, u32[]{:S(2)}) collective-permute-start(bf16[2,2,64,128]{3,2,1,0:T(8,128)(2,1)S(1)} %get-tuple-element.59), channel_id=1, source_target_pairs={{0,2},{1,3},{2,0},{3,1},{4,6},{5,7},{6,4},{7,5},{8,10},{9,11},{10,... | collective-permute-start | bytes 196616 | tf_op jit(solution)/shard_map/ppermute | solution.py:343
  49.5 1.8 %collective-permute-start.24 = (bf16[2,2,64,128]{3,2,1,0:T(8,128)(2,1)S(1)}, bf16[2,2,64,128]{3,2,1,0:T(8,128)(2,1)S(1)}, u32[]{:S(2)}, u32[]{:S(2)}) collective-permute-start(bf16[2,2,64,128]{3,2,1,0:T(8,128)(2,1)S(1)} %get-tuple-element.60), channel_id=1, source_target_pairs={{0,3},{1,2},{2,1},{3,0},{4,7},{5,6},{6,5},{7,4},{8,11},{9,10},{10,... | collective-permute-start | bytes 196616 | tf_op jit(solution)/shard_map/ppermute | solution.py:343
  51.3 0.1 collect.2
  51.4 0.6 collective-permute-start.20
  51.9 2.5 %collective-permute-done.23.refs_2_ = bf16[2,2,64,128]{3,2,1,0:T(8,128)(2,1)S(1)} collective-permute-done((bf16[2,2,64,128]{3,2,1,0:T(8,128)(2,1)S(1)}, bf16[2,2,64,128]{3,2,1,0:T(8,128)(2,1)S(1)}, u32[]{:S(2)}, u32[]{:S(2)}) %collective-permute-start.23) | collective-permute-done | bytes 65568 | tf_op jit(solution)/shard_map/ppermute | solution.py:343
  54.4 1.3 %collective-permute-done.24.refs_3_ = bf16[2,2,64,128]{3,2,1,0:T(8,128)(2,1)S(1)} collective-permute-done((bf16[2,2,64,128]{3,2,1,0:T(8,128)(2,1)S(1)}, bf16[2,2,64,128]{3,2,1,0:T(8,128)(2,1)S(1)}, u32[]{:S(2)}, u32[]{:S(2)}) %collective-permute-start.24) | collective-permute-done | bytes 65568 | tf_op jit(solution)/shard_map/ppermute | solution.py:343
  55.7 0.0 collective-permute-start.28
  55.7 0.6 %collective-permute-done.20.refs_1_ = bf16[2,2,64,128]{3,2,1,0:T(8,128)(2,1)S(1)} collective-permute-done((bf16[2,2,64,128]{3,2,1,0:T(8,128)(2,1)S(1)}, bf16[2,2,64,128]{3,2,1,0:T(8,128)(2,1)S(1)}, u32[]{:S(2)}, u32[]{:S(2)}) %collective-permute-start.20) | collective-permute-done | bytes 65568 | tf_op jit(solution)/shard_map/ppermute | solution.py:343
  56.3 0.6 %collective-permute-done.28.refs_7_ = bf16[2,2,64,128]{3,2,1,0:T(8,128)(2,1)S(1)} collective-permute-done((bf16[2,2,64,128]{3,2,1,0:T(8,128)(2,1)S(1)}, bf16[2,2,64,128]{3,2,1,0:T(8,128)(2,1)S(1)}, u32[]{:S(2)}, u32[]{:S(2)}) %collective-permute-start.28) | collective-permute-done | bytes 65568 | tf_op jit(solution)/shard_map/ppermute | solution.py:343
  56.9 0.6 %collective-permute-done.26.refs_5_ = bf16[2,2,64,128]{3,2,1,0:T(8,128)(2,1)S(1)} collective-permute-done((bf16[2,2,64,128]{3,2,1,0:T(8,128)(2,1)S(1)}, bf16[2,2,64,128]{3,2,1,0:T(8,128)(2,1)S(1)}, u32[]{:S(2)}, u32[]{:S(2)}) %collective-permute-start.26) | collective-permute-done | bytes 65568 | tf_op jit(solution)/shard_map/ppermute | solution.py:343
  57.6 1.3 %unpack_kv.1 = (bf16[64,1024]{1,0:T(8,128)(2,1)}, bf16[64,1024]{1,0:T(8,128)(2,1)}) custom-call(s32[3]{0:T(128)S(1)} %pad_add_fusion.where, bf16[2,2,64,128]{3,2,1,0:T(8,128)(2,1)S(1)} %get-tuple-element.54.refs_0_, bf16[2,2,64,128]{3,2,1,0:T(8,128)(2,1)S(1)} %collective-permute-done.20.refs_1_, bf16[2,2,64,128]{3,2,1,0:T(8,128)(2,1)S(1)} %collective-permute-done.23.refs_2_, ...), custom_call_target="tpu_custom_call" | custom-call | flops 1000000 | bytes 524288 | tf_op jit(solution)/shard_map/unpack_kv/pallas_call | solution.py:331
  58.9 0.0 collective-permute-done.16.theirs
  58.9 1.4 %place_q.1 = bf16[256,1024]{1,0:T(8,128)(2,1)} custom-call(s32[3]{0:T(128)S(1)} %pad_add_fusion.where, bf16[256,512]{1,0:T(8,128)(2,1)S(1)} %get-tuple-element.48.mine, bf16[256,512]{1,0:T(8,128)(2,1)S(1)} %collective-permute-done.16.theirs), custom_call_target="tpu_custom_call" | custom-call | flops 1000000 | bytes 1048576 | tf_op jit(solution)/shard_map/place_q/pallas_call | solution.py:279
  (14 shorter events, 0.0 us)
Async XLA Ops:
  0.7 7.3 %copy-start = (f32[8,256]{1,0:T(8,128)S(1)}, f32[8,256]{1,0:T(8,128)}, u32[]{:S(2)}) copy-start(f32[8,256]{1,0:T(8,128)} %lse.1) | copy-start | bytes 24580
  2.3 9.0 %collective-permute-start.3 = (bf16[2,2,64,128]{3,2,1,0:T(8,128)(2,1)S(1)}, bf16[2,2,64,128]{3,2,1,0:T(8,128)(2,1)S(1)}, u32[]{:S(2)}, u32[]{:S(2)}) collective-permute-start(bf16[2,2,64,128]{3,2,1,0:T(8,128)(2,1)S(1)} %get-tuple-element.40), channel_id=1, source_target_pairs={{0,2},{1,3},{2,0},{3,1},{4,6},{5,7},{6,4},{7,5},{8,10},{9,11},{10,... | collective-permute-start | bytes 196616 | tf_op jit(solution)/shard_map/ppermute | solution.py:343
  6.4 4.9 %collective-permute-start.6 = (bf16[2,2,64,128]{3,2,1,0:T(8,128)(2,1)S(1)}, bf16[2,2,64,128]{3,2,1,0:T(8,128)(2,1)S(1)}, u32[]{:S(2)}, u32[]{:S(2)}) collective-permute-start(bf16[2,2,64,128]{3,2,1,0:T(8,128)(2,1)S(1)} %get-tuple-element.41), channel_id=1, source_target_pairs={{0,1},{1,0},{2,3},{3,2},{4,5},{5,4},{6,7},{7,6},{8,9},{9,8},{10,11... | collective-permute-start | bytes 196616 | tf_op jit(solution)/shard_map/ppermute | solution.py:343
  8.0 6.1 %collective-permute-start.7 = (bf16[2,2,64,128]{3,2,1,0:T(8,128)(2,1)S(1)}, bf16[2,2,64,128]{3,2,1,0:T(8,128)(2,1)S(1)}, u32[]{:S(2)}, u32[]{:S(2)}) collective-permute-start(bf16[2,2,64,128]{3,2,1,0:T(8,128)(2,1)S(1)} %get-tuple-element.42), channel_id=1, source_target_pairs={{0,3},{1,2},{2,1},{3,0},{4,7},{5,6},{6,5},{7,4},{8,11},{9,10},{10,... | collective-permute-start | bytes 196616 | tf_op jit(solution)/shard_map/ppermute | solution.py:343
  8.0 6.1 %collective-permute-start.4 = (bf16[2,2,64,128]{3,2,1,0:T(8,128)(2,1)S(1)}, bf16[2,2,64,128]{3,2,1,0:T(8,128)(2,1)S(1)}, u32[]{:S(2)}, u32[]{:S(2)}) collective-permute-start(bf16[2,2,64,128]{3,2,1,0:T(8,128)(2,1)S(1)} %get-tuple-element.39.refs_0_), channel_id=1, source_target_pairs={{0,4},{4,0},{1,5},{5,1},{2,6},{6,2},{3,7},{7,3},{8,12},{12,8},{9,1... | collective-permute-start | bytes 196616 | tf_op jit(solution)/shard_map/ppermute | solution.py:343
  10.7 12.2 %collective-permute-start = (bf16[1024,128]{1,0:T(8,128)(2,1)S(1)}, bf16[1024,128]{1,0:T(8,128)(2,1)S(1)}, u32[]{:S(2)}, u32[]{:S(2)}) collective-permute-start(bf16[1024,128]{1,0:T(8,128)(2,1)S(1)} %get-tuple-element.36), channel_id=1, source_target_pairs={{0,4},{4,0},{1,5},{5,1},{2,6},{6,2},{3,7},{7,3},{8,12},{12,8},{9,1... | collective-permute-start | bytes 786440 | tf_op jit(solution)/shard_map/ppermute | solution.py:343
  11.3 13.1 %collective-permute-start.1 = (bf16[1024,128]{1,0:T(8,128)(2,1)S(1)}, bf16[1024,128]{1,0:T(8,128)(2,1)S(1)}, u32[]{:S(2)}, u32[]{:S(2)}) collective-permute-start(bf16[1024,128]{1,0:T(8,128)(2,1)S(1)} %get-tuple-element.37), channel_id=1, source_target_pairs={{0,4},{4,0},{1,5},{5,1},{2,6},{6,2},{3,7},{7,3},{8,12},{12,8},{9,1... | collective-permute-start | bytes 786440 | tf_op jit(solution)/shard_map/ppermute | solution.py:343
  11.4 3.2 %collective-permute-start.5 = (bf16[2,2,64,128]{3,2,1,0:T(8,128)(2,1)S(1)}, bf16[2,2,64,128]{3,2,1,0:T(8,128)(2,1)S(1)}, u32[]{:S(2)}, u32[]{:S(2)}) collective-permute-start(bf16[2,2,64,128]{3,2,1,0:T(8,128)(2,1)S(1)} %collective-permute-done.3.refs_1_), channel_id=1, source_target_pairs={{0,4},{4,0},{1,5},{5,1},{2,6},{6,2},{3,7},{7,3},{8,12},{12,8},{9,1... | collective-permute-start | bytes 196616 | tf_op jit(solution)/shard_map/ppermute | solution.py:343
  14.1 2.1 %collective-permute-start.8 = (bf16[2,2,64,128]{3,2,1,0:T(8,128)(2,1)S(1)}, bf16[2,2,64,128]{3,2,1,0:T(8,128)(2,1)S(1)}, u32[]{:S(2)}, u32[]{:S(2)}) collective-permute-start(bf16[2,2,64,128]{3,2,1,0:T(8,128)(2,1)S(1)} %collective-permute-done.6.refs_0_), channel_id=1, source_target_pairs={{0,4},{4,0},{1,5},{5,1},{2,6},{6,2},{3,7},{7,3},{8,12},{12,8},{9,1... | collective-permute-start | bytes 196616 | tf_op jit(solution)/shard_map/ppermute | solution.py:343
  14.1 2.1 %collective-permute-start.9 = (bf16[2,2,64,128]{3,2,1,0:T(8,128)(2,1)S(1)}, bf16[2,2,64,128]{3,2,1,0:T(8,128)(2,1)S(1)}, u32[]{:S(2)}, u32[]{:S(2)}) collective-permute-start(bf16[2,2,64,128]{3,2,1,0:T(8,128)(2,1)S(1)} %collective-permute-done.7.refs_1_), channel_id=1, source_target_pairs={{0,4},{4,0},{1,5},{5,1},{2,6},{6,2},{3,7},{7,3},{8,12},{12,8},{9,1... | collective-permute-start | bytes 196616 | tf_op jit(solution)/shard_map/ppermute | solution.py:343
  14.6 5.5 %collective-permute-start.10 = (bf16[4,2,64,128]{3,2,1,0:T(8,128)(2,1)S(1)}, bf16[4,2,64,128]{3,2,1,0:T(8,128)(2,1)S(1)}, u32[]{:S(2)}, u32[]{:S(2)}) collective-permute-start(bf16[4,2,64,128]{3,2,1,0:T(8,128)(2,1)S(1)} %assemble.2.rest_0_), channel_id=1, source_target_pairs={{0,8},{8,0},{16,24},{24,16},{1,9},{9,1},{17,25},{25,17},{2,10},{10... | collective-permute-start | bytes 393224 | tf_op jit(solution)/shard_map/ppermute | solution.py:343
  16.2 3.6 %copy-start.1 = (s32[16]{0:T(128)S(1)}, s32[16]{0:T(128)}, u32[]{:S(2)}) copy-start(s32[16]{0:T(128)} %param.13) | copy-start | bytes 196
  16.2 5.4 %collective-permute-start.12 = (bf16[4,2,64,128]{3,2,1,0:T(8,128)(2,1)S(1)}, bf16[4,2,64,128]{3,2,1,0:T(8,128)(2,1)S(1)}, u32[]{:S(2)}, u32[]{:S(2)}) collective-permute-start(bf16[4,2,64,128]{3,2,1,0:T(8,128)(2,1)S(1)} %assemble.3.rest_1_), channel_id=1, source_target_pairs={{0,16},{8,24},{16,0},{24,8},{1,17},{9,25},{17,1},{25,9},{2,18},{10... | collective-permute-start | bytes 393224 | tf_op jit(solution)/shard_map/ppermute | solution.py:343
  17.8 1.2 %collective-permute-start.2 = (f32[8,256]{1,0:T(8,128)S(1)}, f32[8,256]{1,0:T(8,128)S(1)}, u32[]{:S(2)}, u32[]{:S(2)}) collective-permute-start(f32[8,256]{1,0:T(8,128)S(1)} %get-tuple-element.38), channel_id=1, source_target_pairs={{0,4},{4,0},{1,5},{5,1},{2,6},{6,2},{3,7},{7,3},{8,12},{12,8},{9,1... | collective-permute-start | bytes 24584 | tf_op jit(solution)/shard_map/ppermute | solution.py:343
  19.0 7.5 %collective-permute-start.15 = (bf16[4,2,64,128]{3,2,1,0:T(8,128)(2,1)S(1)}, bf16[4,2,64,128]{3,2,1,0:T(8,128)(2,1)S(1)}, u32[]{:S(2)}, u32[]{:S(2)}) collective-permute-start(bf16[4,2,64,128]{3,2,1,0:T(8,128)(2,1)S(1)} %assemble.3.rest_1_), channel_id=1, source_target_pairs={{0,8},{8,0},{16,24},{24,16},{1,9},{9,1},{17,25},{25,17},{2,10},{10... | collective-permute-start | bytes 393224 | tf_op jit(solution)/shard_map/ppermute | solution.py:343
  20.1 10.0 %collective-permute-start.14 = (bf16[4,2,64,128]{3,2,1,0:T(8,128)(2,1)S(1)}, bf16[4,2,64,128]{3,2,1,0:T(8,128)(2,1)S(1)}, u32[]{:S(2)}, u32[]{:S(2)}) collective-permute-start(bf16[4,2,64,128]{3,2,1,0:T(8,128)(2,1)S(1)} %assemble.2.rest_0_), channel_id=1, source_target_pairs={{0,16},{8,24},{16,0},{24,8},{1,17},{9,25},{17,1},{25,9},{2,18},{10... | collective-permute-start | bytes 393224 | tf_op jit(solution)/shard_map/ppermute | solution.py:343
  21.6 14.7 %collective-permute-start.11 = (bf16[4,2,64,128]{3,2,1,0:T(8,128)(2,1)S(1)}, bf16[4,2,64,128]{3,2,1,0:T(8,128)(2,1)S(1)}, u32[]{:S(2)}, u32[]{:S(2)}) collective-permute-start(bf16[4,2,64,128]{3,2,1,0:T(8,128)(2,1)S(1)} %collective-permute-done.10.rest_0_), channel_id=1, source_target_pairs={{0,16},{8,24},{16,0},{24,8},{1,17},{9,25},{17,1},{25,9},{2,18},{10... | collective-permute-start | bytes 393224 | tf_op jit(solution)/shard_map/ppermute | solution.py:343
  22.9 13.4 %collective-permute-start.13 = (bf16[4,2,64,128]{3,2,1,0:T(8,128)(2,1)S(1)}, bf16[4,2,64,128]{3,2,1,0:T(8,128)(2,1)S(1)}, u32[]{:S(2)}, u32[]{:S(2)}) collective-permute-start(bf16[4,2,64,128]{3,2,1,0:T(8,128)(2,1)S(1)} %collective-permute-done.12.rest_1_), channel_id=1, source_target_pairs={{0,8},{8,0},{16,24},{24,16},{1,9},{9,1},{17,25},{25,17},{2,10},{10... | collective-permute-start | bytes 393224 | tf_op jit(solution)/shard_map/ppermute | solution.py:343
  33.7 17.6 %collective-permute-start.18 = (bf16[4,2,64,128]{3,2,1,0:T(8,128)(2,1)S(1)}, bf16[4,2,64,128]{3,2,1,0:T(8,128)(2,1)S(1)}, u32[]{:S(2)}, u32[]{:S(2)}) collective-permute-start(bf16[4,2,64,128]{3,2,1,0:T(8,128)(2,1)S(1)} %get-tuple-element.52), channel_id=1, source_target_pairs={{0,16},{8,24},{16,0},{24,8},{1,17},{9,25},{17,1},{25,9},{2,18},{10... | collective-permute-start | bytes 393224 | tf_op jit(solution)/shard_map/ppermute | solution.py:343
  34.6 10.7 %collective-permute-start.21 = (bf16[4,2,64,128]{3,2,1,0:T(8,128)(2,1)S(1)}, bf16[4,2,64,128]{3,2,1,0:T(8,128)(2,1)S(1)}, u32[]{:S(2)}, u32[]{:S(2)}) collective-permute-start(bf16[4,2,64,128]{3,2,1,0:T(8,128)(2,1)S(1)} %get-tuple-element.57), channel_id=1, source_target_pairs={{0,16},{8,24},{16,0},{24,8},{1,17},{9,25},{17,1},{25,9},{2,18},{10... | collective-permute-start | bytes 393224 | tf_op jit(solution)/shard_map/ppermute | solution.py:343
  35.8 12.3 %collective-permute-start.17 = (bf16[8,2,64,128]{3,2,1,0:T(8,128)(2,1)S(1)}, bf16[8,2,64,128]{3,2,1,0:T(8,128)(2,1)S(1)}, u32[]{:S(2)}, u32[]{:S(2)}) collective-permute-start(bf16[8,2,64,128]{3,2,1,0:T(8,128)(2,1)S(1)} %get-tuple-element.51), channel_id=1, source_target_pairs={{0,8},{8,0},{16,24},{24,16},{1,9},{9,1},{17,25},{25,17},{2,10},{10... | collective-permute-start | bytes 786440 | tf_op jit(solution)/shard_map/ppermute | solution.py:343
  39.9 11.3 %collective-permute-start.19 = (bf16[4,2,64,128]{3,2,1,0:T(8,128)(2,1)S(1)}, bf16[4,2,64,128]{3,2,1,0:T(8,128)(2,1)S(1)}, u32[]{:S(2)}, u32[]{:S(2)}) collective-permute-start(bf16[4,2,64,128]{3,2,1,0:T(8,128)(2,1)S(1)} %get-tuple-element.53), channel_id=1, source_target_pairs={{0,24},{8,16},{16,8},{24,0},{1,25},{9,17},{17,9},{25,1},{2,26},{10... | collective-permute-start | bytes 393224 | tf_op jit(solution)/shard_map/ppermute | solution.py:343
  41.7 6.3 %collective-permute-start.22 = (bf16[4,2,64,128]{3,2,1,0:T(8,128)(2,1)S(1)}, bf16[4,2,64,128]{3,2,1,0:T(8,128)(2,1)S(1)}, u32[]{:S(2)}, u32[]{:S(2)}) collective-permute-start(bf16[4,2,64,128]{3,2,1,0:T(8,128)(2,1)S(1)} %get-tuple-element.58), channel_id=1, source_target_pairs={{0,24},{8,16},{16,8},{24,0},{1,25},{9,17},{17,9},{25,1},{2,26},{10... | collective-permute-start | bytes 393224 | tf_op jit(solution)/shard_map/ppermute | solution.py:343
  45.3 13.6 %collective-permute-start.16 = (bf16[256,512]{1,0:T(8,128)(2,1)S(1)}, bf16[256,512]{1,0:T(8,128)(2,1)S(1)}, u32[]{:S(2)}, u32[]{:S(2)}) collective-permute-start(bf16[256,512]{1,0:T(8,128)(2,1)S(1)} %get-tuple-element.49), channel_id=1, source_target_pairs={{0,4},{4,0},{1,5},{5,1},{2,6},{6,2},{3,7},{7,3},{8,12},{12,8},{9,1... | collective-permute-start | bytes 786440 | tf_op jit(solution)/shard_map/ppermute | solution.py:343
  48.1 6.3 %collective-permute-start.23 = (bf16[2,2,64,128]{3,2,1,0:T(8,128)(2,1)S(1)}, bf16[2,2,64,128]{3,2,1,0:T(8,128)(2,1)S(1)}, u32[]{:S(2)}, u32[]{:S(2)}) collective-permute-start(bf16[2,2,64,128]{3,2,1,0:T(8,128)(2,1)S(1)} %get-tuple-element.59), channel_id=1, source_target_pairs={{0,2},{1,3},{2,0},{3,1},{4,6},{5,7},{6,4},{7,5},{8,10},{9,11},{10,... | collective-permute-start | bytes 196616 | tf_op jit(solution)/shard_map/ppermute | solution.py:343
  49.5 6.2 %collective-permute-start.24 = (bf16[2,2,64,128]{3,2,1,0:T(8,128)(2,1)S(1)}, bf16[2,2,64,128]{3,2,1,0:T(8,128)(2,1)S(1)}, u32[]{:S(2)}, u32[]{:S(2)}) collective-permute-start(bf16[2,2,64,128]{3,2,1,0:T(8,128)(2,1)S(1)} %get-tuple-element.60), channel_id=1, source_target_pairs={{0,3},{1,2},{2,1},{3,0},{4,7},{5,6},{6,5},{7,4},{8,11},{9,10},{10,... | collective-permute-start | bytes 196616 | tf_op jit(solution)/shard_map/ppermute | solution.py:343
  51.4 5.0 %collective-permute-start.20 = (bf16[2,2,64,128]{3,2,1,0:T(8,128)(2,1)S(1)}, bf16[2,2,64,128]{3,2,1,0:T(8,128)(2,1)S(1)}, u32[]{:S(2)}, u32[]{:S(2)}) collective-permute-start(bf16[2,2,64,128]{3,2,1,0:T(8,128)(2,1)S(1)} %get-tuple-element.55), channel_id=1, source_target_pairs={{0,1},{1,0},{2,3},{3,2},{4,5},{5,4},{6,7},{7,6},{8,9},{9,8},{10,11... | collective-permute-start | bytes 196616 | tf_op jit(solution)/shard_map/ppermute | solution.py:343
  51.9 4.4 %collective-permute-start.25 = (bf16[2,2,64,128]{3,2,1,0:T(8,128)(2,1)S(1)}, bf16[2,2,64,128]{3,2,1,0:T(8,128)(2,1)S(1)}, u32[]{:S(2)}, u32[]{:S(2)}) collective-permute-start(bf16[2,2,64,128]{3,2,1,0:T(8,128)(2,1)S(1)} %get-tuple-element.54.refs_0_), channel_id=1, source_target_pairs={{0,4},{4,0},{1,5},{5,1},{2,6},{6,2},{3,7},{7,3},{8,12},{12,8},{9,1... | collective-permute-start | bytes 196616 | tf_op jit(solution)/shard_map/ppermute | solution.py:343
  54.4 1.9 %collective-permute-start.27 = (bf16[2,2,64,128]{3,2,1,0:T(8,128)(2,1)S(1)}, bf16[2,2,64,128]{3,2,1,0:T(8,128)(2,1)S(1)}, u32[]{:S(2)}, u32[]{:S(2)}) collective-permute-start(bf16[2,2,64,128]{3,2,1,0:T(8,128)(2,1)S(1)} %collective-permute-done.23.refs_2_), channel_id=1, source_target_pairs={{0,4},{4,0},{1,5},{5,1},{2,6},{6,2},{3,7},{7,3},{8,12},{12,8},{9,1... | collective-permute-start | bytes 196616 | tf_op jit(solution)/shard_map/ppermute | solution.py:343
  55.7 1.3 %collective-permute-start.28 = (bf16[2,2,64,128]{3,2,1,0:T(8,128)(2,1)S(1)}, bf16[2,2,64,128]{3,2,1,0:T(8,128)(2,1)S(1)}, u32[]{:S(2)}, u32[]{:S(2)}) collective-permute-start(bf16[2,2,64,128]{3,2,1,0:T(8,128)(2,1)S(1)} %collective-permute-done.24.refs_3_), channel_id=1, source_target_pairs={{0,4},{4,0},{1,5},{5,1},{2,6},{6,2},{3,7},{7,3},{8,12},{12,8},{9,1... | collective-permute-start | bytes 196616 | tf_op jit(solution)/shard_map/ppermute | solution.py:343
  56.3 1.3 %collective-permute-start.26 = (bf16[2,2,64,128]{3,2,1,0:T(8,128)(2,1)S(1)}, bf16[2,2,64,128]{3,2,1,0:T(8,128)(2,1)S(1)}, u32[]{:S(2)}, u32[]{:S(2)}) collective-permute-start(bf16[2,2,64,128]{3,2,1,0:T(8,128)(2,1)S(1)} %collective-permute-done.20.refs_1_), channel_id=1, source_target_pairs={{0,4},{4,0},{1,5},{5,1},{2,6},{6,2},{3,7},{7,3},{8,12},{12,8},{9,1... | collective-permute-start | bytes 196616 | tf_op jit(solution)/shard_map/ppermute | solution.py:343

commit v5 on v4

--- a/solution.py
+++ b/solution.py
@@ -155,6 +155,8 @@
 
 
 def chunk_kernel(m, groups, first, where, q0, do0, stats0, q1, do1, stats1, *rest):
+    dk_acc, dv_acc = rest[-2:]
+    rest = rest[:-2]
     acc, dkvs = rest[-1 - len(groups)], rest[-len(groups) :]
     picks = [p for group in groups for p in group]
     n_kv = max(p[0] for p in picks) + 1
@@ -179,7 +181,6 @@
     vs = [jnp.concatenate([pieces[p][0][1] for p in t], 0) for t in tiles]
     kts = [k.T for k in ks]
     nt = (((1,), (1,)), ((), ()))
-    dks, dvs = [None] * len(tiles), [None] * len(tiles)
     for b in range(4):
         q_ref, do_ref, stats = (q0, do0, stats0) if b < 2 else (q1, do1, stats1)
         i = b % 2
@@ -204,17 +205,22 @@
             score = jnp.concatenate(scores, 1)
             dv = jnp.dot(prob, dos, preferred_element_type=jnp.float32)
             dk = jnp.dot(score, qs, preferred_element_type=jnp.float32)
-            dvs[t] = dv if dvs[t] is None else dvs[t] + dv
-            dks[t] = dk if dks[t] is None else dks[t] + dk
+            span = slice(t * per_tile * piece, (t + 1) * per_tile * piece)
+            if b == 0:
+                dv_acc[span, :] = dv
+                dk_acc[span, :] = dk
+            else:
+                dv_acc[span, :] += dv
+                dk_acc[span, :] += dk
             term = jnp.dot(kts[t], score, preferred_element_type=jnp.float32)
             dq = term if dq is None else dq + term
         acc[:, b * width : (b + 1) * width] = dq
     targets = [dkv.at[i] for dkv, group in zip(dkvs, groups) for i in range(len(group))]
-    for t, tile in enumerate(tiles):
-        for n, p in enumerate(tile):
-            rows = slice(n * piece, (n + 1) * piece)
-            targets[p][0] = (dks[t][rows] * SCALE).astype(targets[p].dtype)
-            targets[p][1] = dvs[t][rows].astype(targets[p].dtype)
+    for tile in tiles:
+        for p in tile:
+            rows = slice(p * piece, (p + 1) * piece)
+            targets[p][0] = (dk_acc[rows, :] * SCALE).astype(targets[p].dtype)
+            targets[p][1] = dv_acc[rows, :].astype(targets[p].dtype)
 
 
 def chunk(m, groups, where, q_side, kvs, acc, out_dtype):
@@ -230,6 +236,7 @@
         out_specs=[VMEM] * (1 + len(outs)),
         out_shape=[acc_out] + outs,
         input_output_aliases={} if first else {len(args): 0},
+        scratch_shapes=[pltpu.VMEM((rows, HEAD_SIZE), jnp.float32)] * 2,
         compiler_params=params(20),
         cost_estimate=cost(5 * 2 * rows * width * HEAD_SIZE * 2, 4 * kvs[0].size),
         name="chunk",
@@ -370,13 +377,15 @@
     for m in every:
         other[m] = exchange(zr[m], "core", 2, 1)
     last = n_chips - 1
+    near_chips = list(range(last - 1, 0, -1))
     own, sent = [], [[] for _ in range(n_chips)]
     for a, slots in enumerate(halves):
         own.append(assemble([zr[m] for m in slots], [other[m] for m in slots]))
-        for m in range(1, last):
+        for m in near_chips:
             sent[m].append(exchange(own[a], "chip", n_chips, m))
-    for a, (first, second) in enumerate(((1, last ^ 1), (last ^ 1, 1))):
-        sent[last].append(exchange(sent[first][a], "chip", n_chips, second))
+    full = halves[0] + halves[1]
+    whole = assemble([zr[m] for m in full], [other[m] for m in full])
+    sent[last].append(exchange(whole, "chip", n_chips, last))
 
     half_picks = [
         (a, j * len(slots) + i, j, slot)
@@ -386,16 +395,17 @@
     ]
     home = home_halves(n_heads)
     home_picks = [[p for p in half_picks if p[3] in slots] for slots in home]
+    far_picks = [[(0, j * n_heads + full.index(slot), j, slot) for _, _, j, slot in g] for g in home_picks]
     acc = None
     total, received, late = [], [], [[], []]
     acc, dkv = chunk(0, home_picks[:1], info, q_side, own, acc, jnp.float32)
     total.append(dkv)
-    for m in range(1, n_chips):
-        groups = [half_picks] if m < last - 1 else home_picks
+    for m in near_chips + [last]:
+        groups = far_picks if m == last else home_picks if m == near_chips[-1] else [half_picks]
         acc, *parts = chunk(m, groups, info, q_side, sent[m], acc, jnp.bfloat16)
         for a, dkv in enumerate(parts):
             dkv = exchange(dkv, "chip", n_chips, m)
-            (received if m < last - 1 else late[a]).append(dkv)
+            (received if len(parts) == 1 else late[a]).append(dkv)
     acc, dkv = chunk(0, home_picks[1:], info, q_side, own, acc, jnp.float32)
     total.append(dkv)
 

time: 60.6 us -> 61.1 us (level)
  waiting for transfers between devices: 12 us -> 14.9 us
  Pallas kernels: 22.3 us -> 21 us
  starting transfers between devices: 25 us -> 23.9 us
    ppermute x29 -> x28, waiting for transfers between devices: 12 us -> 14.9 us  [exchange(): return lax.ppermute(x, axis, [(i, i ^ m) for i in range(size)])]
    pallas_call x5, Pallas kernels: 15 us -> 13.7 us  [chunk(): pl.pallas_call(functools.partial(chunk_kernel, m, groups, first), in_spec...]
    ppermute x29 -> x28, starting transfers between devices: 25 us -> 23.9 us  [exchange(): return lax.ppermute(x, axis, [(i, i ^ m) for i in range(size)])]
  transfers between devices with their start and end apart: 29 -> 28, of which waited for: 9 -> 9; matrix products, arithmetic and copies ran while one was open for 0% -> 0% of each run, Pallas kernels for 32% -> 30%
where the time goes in v5:
time: 61.1 us; the launch traced here: 60.8 us
  starting transfers between devices  23.9 us (39%)
  Pallas kernels  21 us (34%)
  waiting for transfers between devices  14.9 us (24%)
  between operations  0.81 us (1%)
    ppermute x28, starting transfers between devices, exchange(): return lax.ppermute(x, axis, [(i, i ^ m) for i in range(size)])  23.9 us
    ppermute x28, waiting for transfers between devices, exchange(): return lax.ppermute(x, axis, [(i, i ^ m) for i in range(size)])  14.9 us
    pallas_call x5, Pallas kernels, chunk(): pl.pallas_call(functools.partial(chunk_kernel, m, groups, first), in_spec...  13.7 us
    pallas_call x1, Pallas kernels, prepare(): pl.pallas_call(prepare_kernel, in_specs=[SMEM, ANY, ANY, ANY, VMEM], out_...  2.68 us
    pallas_call x1, Pallas kernels, pack(): pl.pallas_call(pack_kernel, in_specs=[SMEM, ANY, ANY], out_specs=[VMEM] *...  1.58 us
    pallas_call x1, Pallas kernels, place(): pl.pallas_call(place_kernel, in_specs=[SMEM, VMEM, VMEM], out_specs=VMEM,...  1.38 us
    pallas_call x1, Pallas kernels, unpack(): pl.pallas_call(functools.partial(unpack_kernel, n), in_specs=[SMEM] + [VM...  1.3 us
  transfers between devices with their start and end apart: 28, of which 9 were waited for; matrix products, arithmetic and copies ran while one was open for 0% of the time, Pallas kernels for 30%

profile of v5, /device:TPU:0, one launch (start us, length us, event | category | flops | bytes accessed | tf_op | source)
XLA Modules:
  0.0 60.8 jit_solution(15730244249617456826)
XLA Ops:
  0.6 0.1 pad_add_fusion.where
  0.7 1.6 %pack_kv.1 = (bf16[2,2,64,128]{3,2,1,0:T(8,128)(2,1)S(1)}, bf16[2,2,64,128]{3,2,1,0:T(8,128)(2,1)S(1)}, bf16[2,2,64,128]{3,2,1,0:T(8,128)(2,1)S(1)}, bf16[2,2,64,128]{3,2,1,0:T(8,128)(2,1)S(1)}) custom-call(s32[3]{0:T(128)S(1)} %pad_add_fusion.where, bf16[64,1024]{1,0:T(8,128)(2,1)} %keys.1, bf16[64,1024]{1,0:T(8,128)(2,1)} %values.1), custom_call_target="tpu_custom_call" | custom-call | flops 1000000 | bytes 524288 | tf_op jit(solution)/shard_map/pack_kv/pallas_call | solution.py:72
  2.3 3.1 %collective-permute-start.6 = (bf16[2,2,64,128]{3,2,1,0:T(8,128)(2,1)S(1)}, bf16[2,2,64,128]{3,2,1,0:T(8,128)(2,1)S(1)}, u32[]{:S(2)}, u32[]{:S(2)}) collective-permute-start(bf16[2,2,64,128]{3,2,1,0:T(8,128)(2,1)S(1)} %get-tuple-element.41), channel_id=1, source_target_pairs={{0,1},{1,0},{2,3},{3,2},{4,5},{5,4},{6,7},{7,6},{8,9},{9,8},{10,11... | collective-permute-start | bytes 196616 | tf_op jit(solution)/shard_map/ppermute | solution.py:350
  5.4 2.7 %prepare_q.1 = (bf16[1024,128]{1,0:T(8,128)(2,1)S(1)}, bf16[1024,128]{1,0:T(8,128)(2,1)S(1)}, f32[8,256]{1,0:T(8,128)S(1)}, bf16[1024,128]{1,0:T(8,128)(2,1)S(1)...) custom-call(s32[3]{0:T(128)S(1)} %pad_add_fusion.where, bf16[256,1024]{1,0:T(8,128)(2,1)} %q.1, ...), custom_call_target="tpu_custom_call" | custom-call | flops 10000000 | bytes 2097152 | tf_op jit(solution)/shard_map/prepare_q/pallas_call | solution.py:121
  8.1 0.1 collective-permute-start
  8.2 0.5 collective-permute-start.1
  8.7 2.5 %collective-permute-start.7 = (bf16[2,2,64,128]{3,2,1,0:T(8,128)(2,1)S(1)}, bf16[2,2,64,128]{3,2,1,0:T(8,128)(2,1)S(1)}, u32[]{:S(2)}, u32[]{:S(2)}) collective-permute-start(bf16[2,2,64,128]{3,2,1,0:T(8,128)(2,1)S(1)} %get-tuple-element.42), channel_id=1, source_target_pairs={{0,3},{1,2},{2,1},{3,0},{4,7},{5,6},{6,5},{7,4},{8,11},{9,10},{10,... | collective-permute-start | bytes 196616 | tf_op jit(solution)/shard_map/ppermute | solution.py:350
  11.2 0.1 collective-permute-start.3
  11.3 0.0 collective-permute-done.6.refs_0_.refs_2_
  11.3 0.0 collective-permute-start.8
  11.3 3.7 %collective-permute-done.7.refs_1_.refs_3_ = bf16[2,2,64,128]{3,2,1,0:T(8,128)(2,1)S(1)} collective-permute-done((bf16[2,2,64,128]{3,2,1,0:T(8,128)(2,1)S(1)}, bf16[2,2,64,128]{3,2,1,0:T(8,128)(2,1)S(1)}, u32[]{:S(2)}, u32[]{:S(2)}) %collective-permute-start.7) | collective-permute-done | bytes 65568 | tf_op jit(solution)/shard_map/ppermute | solution.py:350
  14.9 0.0 collective-permute-start.9
  14.9 2.9 %collective-permute-done.3.refs_1_ = bf16[2,2,64,128]{3,2,1,0:T(8,128)(2,1)S(1)} collective-permute-done((bf16[2,2,64,128]{3,2,1,0:T(8,128)(2,1)S(1)}, bf16[2,2,64,128]{3,2,1,0:T(8,128)(2,1)S(1)}, u32[]{:S(2)}, u32[]{:S(2)}) %collective-permute-start.3) | collective-permute-done | bytes 65568 | tf_op jit(solution)/shard_map/ppermute | solution.py:350
  17.8 0.0 collective-permute-start.4
  17.8 0.0 collective-permute-done.8.refs_2_.refs_6_
  17.8 0.5 collective-permute-start.5
  18.3 0.0 collective-permute-done.9.refs_3_.refs_7_
  18.3 0.1 collective-permute-start.2
  18.4 0.0 copy-start.1
  18.4 0.6 %collective-permute-done.4.refs_2_.refs_4_ = bf16[2,2,64,128]{3,2,1,0:T(8,128)(2,1)S(1)} collective-permute-done((bf16[2,2,64,128]{3,2,1,0:T(8,128)(2,1)S(1)}, bf16[2,2,64,128]{3,2,1,0:T(8,128)(2,1)S(1)}, u32[]{:S(2)}, u32[]{:S(2)}) %collective-permute-start.4) | collective-permute-done | bytes 65568 | tf_op jit(solution)/shard_map/ppermute | solution.py:350
  19.1 1.5 %collective-permute-start.14 = (bf16[4,2,64,128]{3,2,1,0:T(8,128)(2,1)S(1)}, bf16[4,2,64,128]{3,2,1,0:T(8,128)(2,1)S(1)}, u32[]{:S(2)}, u32[]{:S(2)}) collective-permute-start(bf16[4,2,64,128]{3,2,1,0:T(8,128)(2,1)S(1)} %assemble.4.rest_1_), channel_id=1, source_target_pairs={{0,16},{8,24},{16,0},{24,8},{1,17},{9,25},{17,1},{25,9},{2,18},{10... | collective-permute-start | bytes 393224 | tf_op jit(solution)/shard_map/ppermute | solution.py:350
  20.6 0.0 collective-permute-done.5.refs_3_.refs_5_
  20.6 0.6 collective-permute-start.13
  21.2 0.1 pad_add_fusion.1.where
  21.3 0.0 collective-permute-done.2.stats1
  21.3 1.6 %collective-permute-start.12 = (bf16[4,2,64,128]{3,2,1,0:T(8,128)(2,1)S(1)}, bf16[4,2,64,128]{3,2,1,0:T(8,128)(2,1)S(1)}, u32[]{:S(2)}, u32[]{:S(2)}) collective-permute-start(bf16[4,2,64,128]{3,2,1,0:T(8,128)(2,1)S(1)} %assemble.4.rest_1_), channel_id=1, source_target_pairs={{0,8},{8,0},{16,24},{24,16},{1,9},{9,1},{17,25},{25,17},{2,10},{10... | collective-permute-start | bytes 393224 | tf_op jit(solution)/shard_map/ppermute | solution.py:350
  22.9 0.0 collective-permute-done.q1
  22.9 0.5 collective-permute-start.11
  23.4 0.0 collective-permute-done.1.do1
  23.4 2.4 %collective-permute-start.10 = (bf16[8,2,64,128]{3,2,1,0:T(8,128)(2,1)S(1)}, bf16[8,2,64,128]{3,2,1,0:T(8,128)(2,1)S(1)}, u32[]{:S(2)}, u32[]{:S(2)}) collective-permute-start(bf16[8,2,64,128]{3,2,1,0:T(8,128)(2,1)S(1)} %assemble.5), channel_id=1, source_target_pairs={{0,24},{8,16},{16,8},{24,0},{1,25},{9,17},{17,9},{25,1},{2,26},{10... | collective-permute-start | bytes 786440 | tf_op jit(solution)/shard_map/ppermute | solution.py:350
  25.9 2.0 %chunk.5 = (f32[128,2048]{1,0:T(8,128)S(1)}, f32[4,2,64,128]{3,2,1,0:T(8,128)S(1)}) custom-call(s32[19]{0:T(128)S(1)} %pad_add_fusion.1.where, bf16[1024,128]{1,0:T(8,128)(2,1)S(1)} %get-tuple-element.33.q0, bf16[1024,128]{1,0:T(8,128)(2,1)S(1)} %get-tuple-element.34.do0, f32[8,256]{1,0:T(8,128)S(1)} %get-tuple-element.35.stats0, ...), custom_call_target="tpu_custom_call" | custom-call | flops 1342177280 | bytes 262144 | tf_op jit(solution)/shard_map/chunk/pallas_call | solution.py:233
  27.8 0.0 collective-permute-done.14.rest_1_
  27.8 0.0 collective-permute-done.13.rest_0_
  27.8 3.2 %chunk.6 = (f32[128,2048]{1,0:T(8,128)S(1)}, bf16[8,2,64,128]{3,2,1,0:T(8,128)(2,1)S(1)}) custom-call(s32[19]{0:T(128)S(1)} %pad_add_fusion.1.where, bf16[1024,128]{1,0:T(8,128)(2,1)S(1)} %get-tuple-element.33.q0, bf16[1024,128]{1,0:T(8,128)(2,1)S(1)} %get-tuple-element.34.do0, ...), custom_call_target="tpu_custom_call", output_to_operand_aliasing={{0}: (9, {})} | custom-call | flops 2684354560 | bytes 262144 | tf_op jit(solution)/shard_map/chunk/pallas_call | solution.py:233
  31.1 0.0 collective-permute-done.12.rest_1_
  31.1 0.0 collective-permute-done.11.rest_0_
  31.1 3.2 %chunk.7 = (f32[128,2048]{1,0:T(8,128)S(1)}, bf16[4,2,64,128]{3,2,1,0:T(8,128)(2,1)S(1)}, bf16[4,2,64,128]{3,2,1,0:T(8,128)(2,1)S(1)}) custom-call(s32[19]{0:T(128)S(1)} %pad_add_fusion.1.where, bf16[1024,128]{1,0:T(8,128)(2,1)S(1)} %get-tuple-element.33.q0, bf16[1024,128]{1,0:T(8,128)(2,1)S(1)} %get-tuple-element.34.do0, ...), custom_call_target="tpu_custom_call", output_to_operand_aliasing={{0}: (9, {})} | custom-call | flops 2684354560 | bytes 262144 | tf_op jit(solution)/shard_map/chunk/pallas_call | solution.py:233
  34.4 1.2 %collective-permute-start.17 = (bf16[4,2,64,128]{3,2,1,0:T(8,128)(2,1)S(1)}, bf16[4,2,64,128]{3,2,1,0:T(8,128)(2,1)S(1)}, u32[]{:S(2)}, u32[]{:S(2)}) collective-permute-start(bf16[4,2,64,128]{3,2,1,0:T(8,128)(2,1)S(1)} %get-tuple-element.52), channel_id=1, source_target_pairs={{0,8},{8,0},{16,24},{24,16},{1,9},{9,1},{17,25},{25,17},{2,10},{10... | collective-permute-start | bytes 393224 | tf_op jit(solution)/shard_map/ppermute | solution.py:350
  35.5 0.9 %collective-permute-start.20 = (bf16[4,2,64,128]{3,2,1,0:T(8,128)(2,1)S(1)}, bf16[4,2,64,128]{3,2,1,0:T(8,128)(2,1)S(1)}, u32[]{:S(2)}, u32[]{:S(2)}) collective-permute-start(bf16[4,2,64,128]{3,2,1,0:T(8,128)(2,1)S(1)} %get-tuple-element.57), channel_id=1, source_target_pairs={{0,8},{8,0},{16,24},{24,16},{1,9},{9,1},{17,25},{25,17},{2,10},{10... | collective-permute-start | bytes 393224 | tf_op jit(solution)/shard_map/ppermute | solution.py:350
  36.4 1.1 %collective-permute-start.16 = (bf16[8,2,64,128]{3,2,1,0:T(8,128)(2,1)S(1)}, bf16[8,2,64,128]{3,2,1,0:T(8,128)(2,1)S(1)}, u32[]{:S(2)}, u32[]{:S(2)}) collective-permute-start(bf16[8,2,64,128]{3,2,1,0:T(8,128)(2,1)S(1)} %get-tuple-element.51), channel_id=1, source_target_pairs={{0,16},{8,24},{16,0},{24,8},{1,17},{9,25},{17,1},{25,9},{2,18},{10... | collective-permute-start | bytes 786440 | tf_op jit(solution)/shard_map/ppermute | solution.py:350
  37.6 3.2 %chunk.8 = (f32[128,2048]{1,0:T(8,128)S(1)}, bf16[4,2,64,128]{3,2,1,0:T(8,128)(2,1)S(1)}, bf16[4,2,64,128]{3,2,1,0:T(8,128)(2,1)S(1)}) custom-call(s32[19]{0:T(128)S(1)} %pad_add_fusion.1.where, bf16[1024,128]{1,0:T(8,128)(2,1)S(1)} %get-tuple-element.33.q0, bf16[1024,128]{1,0:T(8,128)(2,1)S(1)} %get-tuple-element.34.do0, ...), custom_call_target="tpu_custom_call", output_to_operand_aliasing={{0}: (8, {})} | custom-call | flops 2684354560 | bytes 524288 | tf_op jit(solution)/shard_map/chunk/pallas_call | solution.py:233
  40.8 1.5 %collective-permute-start.18 = (bf16[4,2,64,128]{3,2,1,0:T(8,128)(2,1)S(1)}, bf16[4,2,64,128]{3,2,1,0:T(8,128)(2,1)S(1)}, u32[]{:S(2)}, u32[]{:S(2)}) collective-permute-start(bf16[4,2,64,128]{3,2,1,0:T(8,128)(2,1)S(1)} %get-tuple-element.53), channel_id=1, source_target_pairs={{0,24},{8,16},{16,8},{24,0},{1,25},{9,17},{17,9},{25,1},{2,26},{10... | collective-permute-start | bytes 393224 | tf_op jit(solution)/shard_map/ppermute | solution.py:350
  42.3 1.5 %collective-permute-start.21 = (bf16[4,2,64,128]{3,2,1,0:T(8,128)(2,1)S(1)}, bf16[4,2,64,128]{3,2,1,0:T(8,128)(2,1)S(1)}, u32[]{:S(2)}, u32[]{:S(2)}) collective-permute-start(bf16[4,2,64,128]{3,2,1,0:T(8,128)(2,1)S(1)} %get-tuple-element.58), channel_id=1, source_target_pairs={{0,24},{8,16},{16,8},{24,0},{1,25},{9,17},{17,9},{25,1},{2,26},{10... | collective-permute-start | bytes 393224 | tf_op jit(solution)/shard_map/ppermute | solution.py:350
  43.8 2.0 %chunk.9 = (f32[128,2048]{1,0:T(8,128)S(1)}, f32[4,2,64,128]{3,2,1,0:T(8,128)S(1)}) custom-call(s32[19]{0:T(128)S(1)} %pad_add_fusion.1.where, bf16[1024,128]{1,0:T(8,128)(2,1)S(1)} %get-tuple-element.33.q0, bf16[1024,128]{1,0:T(8,128)(2,1)S(1)} %get-tuple-element.34.do0, f32[8,256]{1,0:T(8,128)S(1)} %get-tuple-element.35.stats0, ...), custom_call_target="tpu_custom_call", output_to_operand_aliasing={{0}: (9, {})} | custom-call | flops 1342177280 | bytes 262144 | tf_op jit(solution)/shard_map/chunk/pallas_call | solution.py:233
  45.8 0.2 finish_q.1
  46.0 0.0 collective-permute-done.20.refs_1_
  46.1 0.1 collective-permute-start.15
  46.1 2.4 %collective-permute-done.21.refs_2_ = bf16[4,2,64,128]{3,2,1,0:T(8,128)(2,1)S(1)} collective-permute-done((bf16[4,2,64,128]{3,2,1,0:T(8,128)(2,1)S(1)}, bf16[4,2,64,128]{3,2,1,0:T(8,128)(2,1)S(1)}, u32[]{:S(2)}, u32[]{:S(2)}) %collective-permute-start.21) | collective-permute-done | bytes 131104 | tf_op jit(solution)/shard_map/ppermute | solution.py:350
  48.6 0.1 collective-permute-done.16.refs_0_
  48.6 0.1 collect.3
  48.7 1.8 %collective-permute-start.22 = (bf16[2,2,64,128]{3,2,1,0:T(8,128)(2,1)S(1)}, bf16[2,2,64,128]{3,2,1,0:T(8,128)(2,1)S(1)}, u32[]{:S(2)}, u32[]{:S(2)}) collective-permute-start(bf16[2,2,64,128]{3,2,1,0:T(8,128)(2,1)S(1)} %get-tuple-element.59), channel_id=1, source_target_pairs={{0,2},{1,3},{2,0},{3,1},{4,6},{5,7},{6,4},{7,5},{8,10},{9,11},{10,... | collective-permute-start | bytes 196616 | tf_op jit(solution)/shard_map/ppermute | solution.py:350
  50.5 1.0 %collective-permute-start.23 = (bf16[2,2,64,128]{3,2,1,0:T(8,128)(2,1)S(1)}, bf16[2,2,64,128]{3,2,1,0:T(8,128)(2,1)S(1)}, u32[]{:S(2)}, u32[]{:S(2)}) collective-permute-start(bf16[2,2,64,128]{3,2,1,0:T(8,128)(2,1)S(1)} %get-tuple-element.60), channel_id=1, source_target_pairs={{0,3},{1,2},{2,1},{3,0},{4,7},{5,6},{6,5},{7,4},{8,11},{9,10},{10,... | collective-permute-start | bytes 196616 | tf_op jit(solution)/shard_map/ppermute | solution.py:350
  51.6 0.1 collect.2
  51.7 0.7 %collective-permute-start.19 = (bf16[2,2,64,128]{3,2,1,0:T(8,128)(2,1)S(1)}, bf16[2,2,64,128]{3,2,1,0:T(8,128)(2,1)S(1)}, u32[]{:S(2)}, u32[]{:S(2)}) collective-permute-start(bf16[2,2,64,128]{3,2,1,0:T(8,128)(2,1)S(1)} %get-tuple-element.55), channel_id=1, source_target_pairs={{0,1},{1,0},{2,3},{3,2},{4,5},{5,4},{6,7},{7,6},{8,9},{9,8},{10,11... | collective-permute-start | bytes 196616 | tf_op jit(solution)/shard_map/ppermute | solution.py:350
  52.4 0.0 collective-permute-start.24
  52.4 2.2 %collective-permute-done.22.refs_2_ = bf16[2,2,64,128]{3,2,1,0:T(8,128)(2,1)S(1)} collective-permute-done((bf16[2,2,64,128]{3,2,1,0:T(8,128)(2,1)S(1)}, bf16[2,2,64,128]{3,2,1,0:T(8,128)(2,1)S(1)}, u32[]{:S(2)}, u32[]{:S(2)}) %collective-permute-start.22) | collective-permute-done | bytes 65568 | tf_op jit(solution)/shard_map/ppermute | solution.py:350
  54.6 2.1 %collective-permute-done.23.refs_3_ = bf16[2,2,64,128]{3,2,1,0:T(8,128)(2,1)S(1)} collective-permute-done((bf16[2,2,64,128]{3,2,1,0:T(8,128)(2,1)S(1)}, bf16[2,2,64,128]{3,2,1,0:T(8,128)(2,1)S(1)}, u32[]{:S(2)}, u32[]{:S(2)}) %collective-permute-start.23) | collective-permute-done | bytes 65568 | tf_op jit(solution)/shard_map/ppermute | solution.py:350
  56.7 0.0 collective-permute-start.27
  56.7 0.5 collective-permute-start.25
  57.2 0.7 %collective-permute-done.27.refs_7_ = bf16[2,2,64,128]{3,2,1,0:T(8,128)(2,1)S(1)} collective-permute-done((bf16[2,2,64,128]{3,2,1,0:T(8,128)(2,1)S(1)}, bf16[2,2,64,128]{3,2,1,0:T(8,128)(2,1)S(1)}, u32[]{:S(2)}, u32[]{:S(2)}) %collective-permute-start.27) | collective-permute-done | bytes 65568 | tf_op jit(solution)/shard_map/ppermute | solution.py:350
  57.9 0.2 collective-permute-done.25.refs_5_
  58.1 1.3 %unpack_kv.1 = (bf16[64,1024]{1,0:T(8,128)(2,1)}, bf16[64,1024]{1,0:T(8,128)(2,1)}) custom-call(s32[3]{0:T(128)S(1)} %pad_add_fusion.where, bf16[2,2,64,128]{3,2,1,0:T(8,128)(2,1)S(1)} %get-tuple-element.54.refs_0_, bf16[2,2,64,128]{3,2,1,0:T(8,128)(2,1)S(1)} %collective-permute-done.19.refs_1_, bf16[2,2,64,128]{3,2,1,0:T(8,128)(2,1)S(1)} %collective-permute-done.22.refs_2_, ...), custom_call_target="tpu_custom_call" | custom-call | flops 1000000 | bytes 524288 | tf_op jit(solution)/shard_map/unpack_kv/pallas_call | solution.py:338
  59.4 0.0 collective-permute-done.15.theirs
  59.4 1.4 %place_q.1 = bf16[256,1024]{1,0:T(8,128)(2,1)} custom-call(s32[3]{0:T(128)S(1)} %pad_add_fusion.where, bf16[256,512]{1,0:T(8,128)(2,1)S(1)} %get-tuple-element.48.mine, bf16[256,512]{1,0:T(8,128)(2,1)S(1)} %collective-permute-done.15.theirs), custom_call_target="tpu_custom_call" | custom-call | flops 1000000 | bytes 1048576 | tf_op jit(solution)/shard_map/place_q/pallas_call | solution.py:286
  (13 shorter events, 0.1 us)
Async XLA Ops:
  0.7 4.7 %copy-start = (f32[8,256]{1,0:T(8,128)S(1)}, f32[8,256]{1,0:T(8,128)}, u32[]{:S(2)}) copy-start(f32[8,256]{1,0:T(8,128)} %lse.1) | copy-start | bytes 24580
  2.3 9.0 %collective-permute-start.6 = (bf16[2,2,64,128]{3,2,1,0:T(8,128)(2,1)S(1)}, bf16[2,2,64,128]{3,2,1,0:T(8,128)(2,1)S(1)}, u32[]{:S(2)}, u32[]{:S(2)}) collective-permute-start(bf16[2,2,64,128]{3,2,1,0:T(8,128)(2,1)S(1)} %get-tuple-element.41), channel_id=1, source_target_pairs={{0,1},{1,0},{2,3},{3,2},{4,5},{5,4},{6,7},{7,6},{8,9},{9,8},{10,11... | collective-permute-start | bytes 196616 | tf_op jit(solution)/shard_map/ppermute | solution.py:350
  8.1 14.7 %collective-permute-start = (bf16[1024,128]{1,0:T(8,128)(2,1)S(1)}, bf16[1024,128]{1,0:T(8,128)(2,1)S(1)}, u32[]{:S(2)}, u32[]{:S(2)}) collective-permute-start(bf16[1024,128]{1,0:T(8,128)(2,1)S(1)} %get-tuple-element.36), channel_id=1, source_target_pairs={{0,4},{4,0},{1,5},{5,1},{2,6},{6,2},{3,7},{7,3},{8,12},{12,8},{9,1... | collective-permute-start | bytes 786440 | tf_op jit(solution)/shard_map/ppermute | solution.py:350
  8.2 15.2 %collective-permute-start.1 = (bf16[1024,128]{1,0:T(8,128)(2,1)S(1)}, bf16[1024,128]{1,0:T(8,128)(2,1)S(1)}, u32[]{:S(2)}, u32[]{:S(2)}) collective-permute-start(bf16[1024,128]{1,0:T(8,128)(2,1)S(1)} %get-tuple-element.37), channel_id=1, source_target_pairs={{0,4},{4,0},{1,5},{5,1},{2,6},{6,2},{3,7},{7,3},{8,12},{12,8},{9,1... | collective-permute-start | bytes 786440 | tf_op jit(solution)/shard_map/ppermute | solution.py:350
  8.7 6.2 %collective-permute-start.7 = (bf16[2,2,64,128]{3,2,1,0:T(8,128)(2,1)S(1)}, bf16[2,2,64,128]{3,2,1,0:T(8,128)(2,1)S(1)}, u32[]{:S(2)}, u32[]{:S(2)}) collective-permute-start(bf16[2,2,64,128]{3,2,1,0:T(8,128)(2,1)S(1)} %get-tuple-element.42), channel_id=1, source_target_pairs={{0,3},{1,2},{2,1},{3,0},{4,7},{5,6},{6,5},{7,4},{8,11},{9,10},{10,... | collective-permute-start | bytes 196616 | tf_op jit(solution)/shard_map/ppermute | solution.py:350
  11.2 6.7 %collective-permute-start.3 = (bf16[2,2,64,128]{3,2,1,0:T(8,128)(2,1)S(1)}, bf16[2,2,64,128]{3,2,1,0:T(8,128)(2,1)S(1)}, u32[]{:S(2)}, u32[]{:S(2)}) collective-permute-start(bf16[2,2,64,128]{3,2,1,0:T(8,128)(2,1)S(1)} %get-tuple-element.40), channel_id=1, source_target_pairs={{0,2},{1,3},{2,0},{3,1},{4,6},{5,7},{6,4},{7,5},{8,10},{9,11},{10,... | collective-permute-start | bytes 196616 | tf_op jit(solution)/shard_map/ppermute | solution.py:350
  11.3 6.5 %collective-permute-start.8 = (bf16[2,2,64,128]{3,2,1,0:T(8,128)(2,1)S(1)}, bf16[2,2,64,128]{3,2,1,0:T(8,128)(2,1)S(1)}, u32[]{:S(2)}, u32[]{:S(2)}) collective-permute-start(bf16[2,2,64,128]{3,2,1,0:T(8,128)(2,1)S(1)} %collective-permute-done.6.refs_0_.refs_2_), channel_id=1, source_target_pairs={{0,4},{4,0},{1,5},{5,1},{2,6},{6,2},{3,7},{7,3},{8,12},{12,8},{9,1... | collective-permute-start | bytes 196616 | tf_op jit(solution)/shard_map/ppermute | solution.py:350
  14.9 3.4 %collective-permute-start.9 = (bf16[2,2,64,128]{3,2,1,0:T(8,128)(2,1)S(1)}, bf16[2,2,64,128]{3,2,1,0:T(8,128)(2,1)S(1)}, u32[]{:S(2)}, u32[]{:S(2)}) collective-permute-start(bf16[2,2,64,128]{3,2,1,0:T(8,128)(2,1)S(1)} %collective-permute-done.7.refs_1_.refs_3_), channel_id=1, source_target_pairs={{0,4},{4,0},{1,5},{5,1},{2,6},{6,2},{3,7},{7,3},{8,12},{12,8},{9,1... | collective-permute-start | bytes 196616 | tf_op jit(solution)/shard_map/ppermute | solution.py:350
  17.8 1.3 %collective-permute-start.4 = (bf16[2,2,64,128]{3,2,1,0:T(8,128)(2,1)S(1)}, bf16[2,2,64,128]{3,2,1,0:T(8,128)(2,1)S(1)}, u32[]{:S(2)}, u32[]{:S(2)}) collective-permute-start(bf16[2,2,64,128]{3,2,1,0:T(8,128)(2,1)S(1)} %get-tuple-element.39.refs_0_), channel_id=1, source_target_pairs={{0,4},{4,0},{1,5},{5,1},{2,6},{6,2},{3,7},{7,3},{8,12},{12,8},{9,1... | collective-permute-start | bytes 196616 | tf_op jit(solution)/shard_map/ppermute | solution.py:350
  17.8 2.8 %collective-permute-start.5 = (bf16[2,2,64,128]{3,2,1,0:T(8,128)(2,1)S(1)}, bf16[2,2,64,128]{3,2,1,0:T(8,128)(2,1)S(1)}, u32[]{:S(2)}, u32[]{:S(2)}) collective-permute-start(bf16[2,2,64,128]{3,2,1,0:T(8,128)(2,1)S(1)} %collective-permute-done.3.refs_1_), channel_id=1, source_target_pairs={{0,4},{4,0},{1,5},{5,1},{2,6},{6,2},{3,7},{7,3},{8,12},{12,8},{9,1... | collective-permute-start | bytes 196616 | tf_op jit(solution)/shard_map/ppermute | solution.py:350
  18.3 3.0 %collective-permute-start.2 = (f32[8,256]{1,0:T(8,128)S(1)}, f32[8,256]{1,0:T(8,128)S(1)}, u32[]{:S(2)}, u32[]{:S(2)}) collective-permute-start(f32[8,256]{1,0:T(8,128)S(1)} %get-tuple-element.38), channel_id=1, source_target_pairs={{0,4},{4,0},{1,5},{5,1},{2,6},{6,2},{3,7},{7,3},{8,12},{12,8},{9,1... | collective-permute-start | bytes 24584 | tf_op jit(solution)/shard_map/ppermute | solution.py:350
  18.4 2.8 %copy-start.1 = (s32[16]{0:T(128)S(1)}, s32[16]{0:T(128)}, u32[]{:S(2)}) copy-start(s32[16]{0:T(128)} %param.13) | copy-start | bytes 196
  19.1 8.7 %collective-permute-start.14 = (bf16[4,2,64,128]{3,2,1,0:T(8,128)(2,1)S(1)}, bf16[4,2,64,128]{3,2,1,0:T(8,128)(2,1)S(1)}, u32[]{:S(2)}, u32[]{:S(2)}) collective-permute-start(bf16[4,2,64,128]{3,2,1,0:T(8,128)(2,1)S(1)} %assemble.4.rest_1_), channel_id=1, source_target_pairs={{0,16},{8,24},{16,0},{24,8},{1,17},{9,25},{17,1},{25,9},{2,18},{10... | collective-permute-start | bytes 393224 | tf_op jit(solution)/shard_map/ppermute | solution.py:350
  20.6 7.2 %collective-permute-start.13 = (bf16[4,2,64,128]{3,2,1,0:T(8,128)(2,1)S(1)}, bf16[4,2,64,128]{3,2,1,0:T(8,128)(2,1)S(1)}, u32[]{:S(2)}, u32[]{:S(2)}) collective-permute-start(bf16[4,2,64,128]{3,2,1,0:T(8,128)(2,1)S(1)} %assemble.3.rest_0_), channel_id=1, source_target_pairs={{0,16},{8,24},{16,0},{24,8},{1,17},{9,25},{17,1},{25,9},{2,18},{10... | collective-permute-start | bytes 393224 | tf_op jit(solution)/shard_map/ppermute | solution.py:350
  21.3 9.8 %collective-permute-start.12 = (bf16[4,2,64,128]{3,2,1,0:T(8,128)(2,1)S(1)}, bf16[4,2,64,128]{3,2,1,0:T(8,128)(2,1)S(1)}, u32[]{:S(2)}, u32[]{:S(2)}) collective-permute-start(bf16[4,2,64,128]{3,2,1,0:T(8,128)(2,1)S(1)} %assemble.4.rest_1_), channel_id=1, source_target_pairs={{0,8},{8,0},{16,24},{24,16},{1,9},{9,1},{17,25},{25,17},{2,10},{10... | collective-permute-start | bytes 393224 | tf_op jit(solution)/shard_map/ppermute | solution.py:350
  22.9 8.2 %collective-permute-start.11 = (bf16[4,2,64,128]{3,2,1,0:T(8,128)(2,1)S(1)}, bf16[4,2,64,128]{3,2,1,0:T(8,128)(2,1)S(1)}, u32[]{:S(2)}, u32[]{:S(2)}) collective-permute-start(bf16[4,2,64,128]{3,2,1,0:T(8,128)(2,1)S(1)} %assemble.3.rest_0_), channel_id=1, source_target_pairs={{0,8},{8,0},{16,24},{24,16},{1,9},{9,1},{17,25},{25,17},{2,10},{10... | collective-permute-start | bytes 393224 | tf_op jit(solution)/shard_map/ppermute | solution.py:350
  23.4 14.2 %collective-permute-start.10 = (bf16[8,2,64,128]{3,2,1,0:T(8,128)(2,1)S(1)}, bf16[8,2,64,128]{3,2,1,0:T(8,128)(2,1)S(1)}, u32[]{:S(2)}, u32[]{:S(2)}) collective-permute-start(bf16[8,2,64,128]{3,2,1,0:T(8,128)(2,1)S(1)} %assemble.5), channel_id=1, source_target_pairs={{0,24},{8,16},{16,8},{24,0},{1,25},{9,17},{17,9},{25,1},{2,26},{10... | collective-permute-start | bytes 786440 | tf_op jit(solution)/shard_map/ppermute | solution.py:350
  34.4 17.2 %collective-permute-start.17 = (bf16[4,2,64,128]{3,2,1,0:T(8,128)(2,1)S(1)}, bf16[4,2,64,128]{3,2,1,0:T(8,128)(2,1)S(1)}, u32[]{:S(2)}, u32[]{:S(2)}) collective-permute-start(bf16[4,2,64,128]{3,2,1,0:T(8,128)(2,1)S(1)} %get-tuple-element.52), channel_id=1, source_target_pairs={{0,8},{8,0},{16,24},{24,16},{1,9},{9,1},{17,25},{25,17},{2,10},{10... | collective-permute-start | bytes 393224 | tf_op jit(solution)/shard_map/ppermute | solution.py:350
  35.5 10.5 %collective-permute-start.20 = (bf16[4,2,64,128]{3,2,1,0:T(8,128)(2,1)S(1)}, bf16[4,2,64,128]{3,2,1,0:T(8,128)(2,1)S(1)}, u32[]{:S(2)}, u32[]{:S(2)}) collective-permute-start(bf16[4,2,64,128]{3,2,1,0:T(8,128)(2,1)S(1)} %get-tuple-element.57), channel_id=1, source_target_pairs={{0,8},{8,0},{16,24},{24,16},{1,9},{9,1},{17,25},{25,17},{2,10},{10... | collective-permute-start | bytes 393224 | tf_op jit(solution)/shard_map/ppermute | solution.py:350
  36.4 12.2 %collective-permute-start.16 = (bf16[8,2,64,128]{3,2,1,0:T(8,128)(2,1)S(1)}, bf16[8,2,64,128]{3,2,1,0:T(8,128)(2,1)S(1)}, u32[]{:S(2)}, u32[]{:S(2)}) collective-permute-start(bf16[8,2,64,128]{3,2,1,0:T(8,128)(2,1)S(1)} %get-tuple-element.51), channel_id=1, source_target_pairs={{0,16},{8,24},{16,0},{24,8},{1,17},{9,25},{17,1},{25,9},{2,18},{10... | collective-permute-start | bytes 786440 | tf_op jit(solution)/shard_map/ppermute | solution.py:350
  40.8 10.8 %collective-permute-start.18 = (bf16[4,2,64,128]{3,2,1,0:T(8,128)(2,1)S(1)}, bf16[4,2,64,128]{3,2,1,0:T(8,128)(2,1)S(1)}, u32[]{:S(2)}, u32[]{:S(2)}) collective-permute-start(bf16[4,2,64,128]{3,2,1,0:T(8,128)(2,1)S(1)} %get-tuple-element.53), channel_id=1, source_target_pairs={{0,24},{8,16},{16,8},{24,0},{1,25},{9,17},{17,9},{25,1},{2,26},{10... | collective-permute-start | bytes 393224 | tf_op jit(solution)/shard_map/ppermute | solution.py:350
  42.3 6.2 %collective-permute-start.21 = (bf16[4,2,64,128]{3,2,1,0:T(8,128)(2,1)S(1)}, bf16[4,2,64,128]{3,2,1,0:T(8,128)(2,1)S(1)}, u32[]{:S(2)}, u32[]{:S(2)}) collective-permute-start(bf16[4,2,64,128]{3,2,1,0:T(8,128)(2,1)S(1)} %get-tuple-element.58), channel_id=1, source_target_pairs={{0,24},{8,16},{16,8},{24,0},{1,25},{9,17},{17,9},{25,1},{2,26},{10... | collective-permute-start | bytes 393224 | tf_op jit(solution)/shard_map/ppermute | solution.py:350
  46.1 13.4 %collective-permute-start.15 = (bf16[256,512]{1,0:T(8,128)(2,1)S(1)}, bf16[256,512]{1,0:T(8,128)(2,1)S(1)}, u32[]{:S(2)}, u32[]{:S(2)}) collective-permute-start(bf16[256,512]{1,0:T(8,128)(2,1)S(1)} %get-tuple-element.49), channel_id=1, source_target_pairs={{0,4},{4,0},{1,5},{5,1},{2,6},{6,2},{3,7},{7,3},{8,12},{12,8},{9,1... | collective-permute-start | bytes 786440 | tf_op jit(solution)/shard_map/ppermute | solution.py:350
  48.7 5.9 %collective-permute-start.22 = (bf16[2,2,64,128]{3,2,1,0:T(8,128)(2,1)S(1)}, bf16[2,2,64,128]{3,2,1,0:T(8,128)(2,1)S(1)}, u32[]{:S(2)}, u32[]{:S(2)}) collective-permute-start(bf16[2,2,64,128]{3,2,1,0:T(8,128)(2,1)S(1)} %get-tuple-element.59), channel_id=1, source_target_pairs={{0,2},{1,3},{2,0},{3,1},{4,6},{5,7},{6,4},{7,5},{8,10},{9,11},{10,... | collective-permute-start | bytes 196616 | tf_op jit(solution)/shard_map/ppermute | solution.py:350
  50.5 6.2 %collective-permute-start.23 = (bf16[2,2,64,128]{3,2,1,0:T(8,128)(2,1)S(1)}, bf16[2,2,64,128]{3,2,1,0:T(8,128)(2,1)S(1)}, u32[]{:S(2)}, u32[]{:S(2)}) collective-permute-start(bf16[2,2,64,128]{3,2,1,0:T(8,128)(2,1)S(1)} %get-tuple-element.60), channel_id=1, source_target_pairs={{0,3},{1,2},{2,1},{3,0},{4,7},{5,6},{6,5},{7,4},{8,11},{9,10},{10,... | collective-permute-start | bytes 196616 | tf_op jit(solution)/shard_map/ppermute | solution.py:350
  51.7 5.0 %collective-permute-start.19 = (bf16[2,2,64,128]{3,2,1,0:T(8,128)(2,1)S(1)}, bf16[2,2,64,128]{3,2,1,0:T(8,128)(2,1)S(1)}, u32[]{:S(2)}, u32[]{:S(2)}) collective-permute-start(bf16[2,2,64,128]{3,2,1,0:T(8,128)(2,1)S(1)} %get-tuple-element.55), channel_id=1, source_target_pairs={{0,1},{1,0},{2,3},{3,2},{4,5},{5,4},{6,7},{7,6},{8,9},{9,8},{10,11... | collective-permute-start | bytes 196616 | tf_op jit(solution)/shard_map/ppermute | solution.py:350
  52.4 4.8 %collective-permute-start.24 = (bf16[2,2,64,128]{3,2,1,0:T(8,128)(2,1)S(1)}, bf16[2,2,64,128]{3,2,1,0:T(8,128)(2,1)S(1)}, u32[]{:S(2)}, u32[]{:S(2)}) collective-permute-start(bf16[2,2,64,128]{3,2,1,0:T(8,128)(2,1)S(1)} %get-tuple-element.54.refs_0_), channel_id=1, source_target_pairs={{0,4},{4,0},{1,5},{5,1},{2,6},{6,2},{3,7},{7,3},{8,12},{12,8},{9,1... | collective-permute-start | bytes 196616 | tf_op jit(solution)/shard_map/ppermute | solution.py:350
  54.6 2.6 %collective-permute-start.26 = (bf16[2,2,64,128]{3,2,1,0:T(8,128)(2,1)S(1)}, bf16[2,2,64,128]{3,2,1,0:T(8,128)(2,1)S(1)}, u32[]{:S(2)}, u32[]{:S(2)}) collective-permute-start(bf16[2,2,64,128]{3,2,1,0:T(8,128)(2,1)S(1)} %collective-permute-done.22.refs_2_), channel_id=1, source_target_pairs={{0,4},{4,0},{1,5},{5,1},{2,6},{6,2},{3,7},{7,3},{8,12},{12,8},{9,1... | collective-permute-start | bytes 196616 | tf_op jit(solution)/shard_map/ppermute | solution.py:350
  56.7 1.3 %collective-permute-start.27 = (bf16[2,2,64,128]{3,2,1,0:T(8,128)(2,1)S(1)}, bf16[2,2,64,128]{3,2,1,0:T(8,128)(2,1)S(1)}, u32[]{:S(2)}, u32[]{:S(2)}) collective-permute-start(bf16[2,2,64,128]{3,2,1,0:T(8,128)(2,1)S(1)} %collective-permute-done.23.refs_3_), channel_id=1, source_target_pairs={{0,4},{4,0},{1,5},{5,1},{2,6},{6,2},{3,7},{7,3},{8,12},{12,8},{9,1... | collective-permute-start | bytes 196616 | tf_op jit(solution)/shard_map/ppermute | solution.py:350
  56.7 1.4 %collective-permute-start.25 = (bf16[2,2,64,128]{3,2,1,0:T(8,128)(2,1)S(1)}, bf16[2,2,64,128]{3,2,1,0:T(8,128)(2,1)S(1)}, u32[]{:S(2)}, u32[]{:S(2)}) collective-permute-start(bf16[2,2,64,128]{3,2,1,0:T(8,128)(2,1)S(1)} %collective-permute-done.19.refs_1_), channel_id=1, source_target_pairs={{0,4},{4,0},{1,5},{5,1},{2,6},{6,2},{3,7},{7,3},{8,12},{12,8},{9,1... | collective-permute-start | bytes 196616 | tf_op jit(solution)/shard_map/ppermute | solution.py:350

commit v6 on v5

--- a/solution.py
+++ b/solution.py
@@ -400,12 +400,15 @@
     total, received, late = [], [], [[], []]
     acc, dkv = chunk(0, home_picks[:1], info, q_side, own, acc, jnp.float32)
     total.append(dkv)
-    for m in near_chips + [last]:
-        groups = far_picks if m == last else home_picks if m == near_chips[-1] else [half_picks]
+    for m in near_chips:
+        groups = home_picks if m == near_chips[-1] else [half_picks]
         acc, *parts = chunk(m, groups, info, q_side, sent[m], acc, jnp.bfloat16)
         for a, dkv in enumerate(parts):
             dkv = exchange(dkv, "chip", n_chips, m)
             (received if len(parts) == 1 else late[a]).append(dkv)
+    for a, group in enumerate(far_picks):
+        acc, dkv = chunk(last, [group], info, q_side, sent[last], acc, jnp.bfloat16)
+        late[a].append(exchange(dkv, "chip", n_chips, last))
     acc, dkv = chunk(0, home_picks[1:], info, q_side, own, acc, jnp.float32)
     total.append(dkv)
 

time: 61.1 us -> 61.7 us (level)
  Pallas kernels: 21 us -> 21.8 us
    pallas_call x5 -> x6, Pallas kernels: 13.7 us -> 14.5 us  [chunk(): pl.pallas_call(functools.partial(chunk_kernel, m, groups, first), in_spec...]
  transfers between devices with their start and end apart: 28 -> 28, of which waited for: 9 -> 8; matrix products, arithmetic and copies ran while one was open for 0% -> 0% of each run, Pallas kernels for 30% -> 31%
where the time goes in v6:
time: 61.7 us; the launch traced here: 61.4 us
  starting transfers between devices  23.9 us (39%)
  Pallas kernels  21.8 us (35%)
  waiting for transfers between devices  14.7 us (24%)
  between operations  0.82 us (1%)
    ppermute x28, starting transfers between devices, exchange(): return lax.ppermute(x, axis, [(i, i ^ m) for i in range(size)])  23.9 us
    ppermute x28, waiting for transfers between devices, exchange(): return lax.ppermute(x, axis, [(i, i ^ m) for i in range(size)])  14.7 us
    pallas_call x6, Pallas kernels, chunk(): pl.pallas_call(functools.partial(chunk_kernel, m, groups, first), in_spec...  14.5 us
    pallas_call x1, Pallas kernels, prepare(): pl.pallas_call(prepare_kernel, in_specs=[SMEM, ANY, ANY, ANY, VMEM], out_...  2.68 us
    pallas_call x1, Pallas kernels, pack(): pl.pallas_call(pack_kernel, in_specs=[SMEM, ANY, ANY], out_specs=[VMEM] *...  1.58 us
    pallas_call x1, Pallas kernels, place(): pl.pallas_call(place_kernel, in_specs=[SMEM, VMEM, VMEM], out_specs=VMEM,...  1.38 us
    pallas_call x1, Pallas kernels, unpack(): pl.pallas_call(functools.partial(unpack_kernel, n), in_specs=[SMEM] + [VM...  1.3 us
  transfers between devices with their start and end apart: 28, of which 8 were waited for; matrix products, arithmetic and copies ran while one was open for 0% of the time, Pallas kernels for 31%

profile of v6, /device:TPU:0, one launch (start us, length us, event | category | flops | bytes accessed | tf_op | source)
XLA Modules:
  0.0 61.4 jit_solution(16257562567280544154)
XLA Ops:
  0.6 0.1 pad_add_fusion.where
  0.7 1.6 %pack_kv.1 = (bf16[2,2,64,128]{3,2,1,0:T(8,128)(2,1)S(1)}, bf16[2,2,64,128]{3,2,1,0:T(8,128)(2,1)S(1)}, bf16[2,2,64,128]{3,2,1,0:T(8,128)(2,1)S(1)}, bf16[2,2,64,128]{3,2,1,0:T(8,128)(2,1)S(1)}) custom-call(s32[3]{0:T(128)S(1)} %pad_add_fusion.where, bf16[64,1024]{1,0:T(8,128)(2,1)} %keys.1, bf16[64,1024]{1,0:T(8,128)(2,1)} %values.1), custom_call_target="tpu_custom_call" | custom-call | flops 1000000 | bytes 524288 | tf_op jit(solution)/shard_map/pack_kv/pallas_call | solution.py:72
  2.3 3.1 %collective-permute-start.6 = (bf16[2,2,64,128]{3,2,1,0:T(8,128)(2,1)S(1)}, bf16[2,2,64,128]{3,2,1,0:T(8,128)(2,1)S(1)}, u32[]{:S(2)}, u32[]{:S(2)}) collective-permute-start(bf16[2,2,64,128]{3,2,1,0:T(8,128)(2,1)S(1)} %get-tuple-element.42), channel_id=1, source_target_pairs={{0,1},{1,0},{2,3},{3,2},{4,5},{5,4},{6,7},{7,6},{8,9},{9,8},{10,11... | collective-permute-start | bytes 196616 | tf_op jit(solution)/shard_map/ppermute | solution.py:350
  5.4 2.7 %prepare_q.1 = (bf16[1024,128]{1,0:T(8,128)(2,1)S(1)}, bf16[1024,128]{1,0:T(8,128)(2,1)S(1)}, f32[8,256]{1,0:T(8,128)S(1)}, bf16[1024,128]{1,0:T(8,128)(2,1)S(1)...) custom-call(s32[3]{0:T(128)S(1)} %pad_add_fusion.where, bf16[256,1024]{1,0:T(8,128)(2,1)} %q.1, ...), custom_call_target="tpu_custom_call" | custom-call | flops 10000000 | bytes 2097152 | tf_op jit(solution)/shard_map/prepare_q/pallas_call | solution.py:121
  8.1 0.1 collective-permute-start
  8.2 0.5 collective-permute-start.1
  8.7 2.5 %collective-permute-start.7 = (bf16[2,2,64,128]{3,2,1,0:T(8,128)(2,1)S(1)}, bf16[2,2,64,128]{3,2,1,0:T(8,128)(2,1)S(1)}, u32[]{:S(2)}, u32[]{:S(2)}) collective-permute-start(bf16[2,2,64,128]{3,2,1,0:T(8,128)(2,1)S(1)} %get-tuple-element.43), channel_id=1, source_target_pairs={{0,3},{1,2},{2,1},{3,0},{4,7},{5,6},{6,5},{7,4},{8,11},{9,10},{10,... | collective-permute-start | bytes 196616 | tf_op jit(solution)/shard_map/ppermute | solution.py:350
  11.2 0.1 collective-permute-start.3
  11.3 0.0 collective-permute-done.6.refs_0_.refs_2_
  11.3 0.0 collective-permute-start.8
  11.3 3.7 %collective-permute-done.7.refs_1_.refs_3_ = bf16[2,2,64,128]{3,2,1,0:T(8,128)(2,1)S(1)} collective-permute-done((bf16[2,2,64,128]{3,2,1,0:T(8,128)(2,1)S(1)}, bf16[2,2,64,128]{3,2,1,0:T(8,128)(2,1)S(1)}, u32[]{:S(2)}, u32[]{:S(2)}) %collective-permute-start.7) | collective-permute-done | bytes 65568 | tf_op jit(solution)/shard_map/ppermute | solution.py:350
  14.9 2.9 %collective-permute-done.3.refs_1_ = bf16[2,2,64,128]{3,2,1,0:T(8,128)(2,1)S(1)} collective-permute-done((bf16[2,2,64,128]{3,2,1,0:T(8,128)(2,1)S(1)}, bf16[2,2,64,128]{3,2,1,0:T(8,128)(2,1)S(1)}, u32[]{:S(2)}, u32[]{:S(2)}) %collective-permute-start.3) | collective-permute-done | bytes 65568 | tf_op jit(solution)/shard_map/ppermute | solution.py:350
  17.8 0.0 collective-permute-start.4
  17.8 0.0 collective-permute-done.8.refs_2_.refs_6_
  17.8 0.5 collective-permute-start.5
  18.3 0.0 collective-permute-done.9.refs_3_.refs_7_
  18.3 0.1 collective-permute-start.2
  18.4 0.0 copy-start.1
  18.4 0.6 %collective-permute-done.4.refs_2_.refs_4_ = bf16[2,2,64,128]{3,2,1,0:T(8,128)(2,1)S(1)} collective-permute-done((bf16[2,2,64,128]{3,2,1,0:T(8,128)(2,1)S(1)}, bf16[2,2,64,128]{3,2,1,0:T(8,128)(2,1)S(1)}, u32[]{:S(2)}, u32[]{:S(2)}) %collective-permute-start.4) | collective-permute-done | bytes 65568 | tf_op jit(solution)/shard_map/ppermute | solution.py:350
  19.1 1.5 %collective-permute-start.14 = (bf16[4,2,64,128]{3,2,1,0:T(8,128)(2,1)S(1)}, bf16[4,2,64,128]{3,2,1,0:T(8,128)(2,1)S(1)}, u32[]{:S(2)}, u32[]{:S(2)}) collective-permute-start(bf16[4,2,64,128]{3,2,1,0:T(8,128)(2,1)S(1)} %assemble.4.rest_1_), channel_id=1, source_target_pairs={{0,16},{8,24},{16,0},{24,8},{1,17},{9,25},{17,1},{25,9},{2,18},{10... | collective-permute-start | bytes 393224 | tf_op jit(solution)/shard_map/ppermute | solution.py:350
  20.6 0.0 collective-permute-done.5.refs_3_.refs_5_
  20.6 0.6 collective-permute-start.13
  21.2 0.1 pad_add_fusion.1.where
  21.3 0.0 collective-permute-done.2.stats1
  21.3 1.6 %collective-permute-start.12 = (bf16[4,2,64,128]{3,2,1,0:T(8,128)(2,1)S(1)}, bf16[4,2,64,128]{3,2,1,0:T(8,128)(2,1)S(1)}, u32[]{:S(2)}, u32[]{:S(2)}) collective-permute-start(bf16[4,2,64,128]{3,2,1,0:T(8,128)(2,1)S(1)} %assemble.4.rest_1_), channel_id=1, source_target_pairs={{0,8},{8,0},{16,24},{24,16},{1,9},{9,1},{17,25},{25,17},{2,10},{10... | collective-permute-start | bytes 393224 | tf_op jit(solution)/shard_map/ppermute | solution.py:350
  22.9 0.5 collective-permute-start.11
  23.4 0.0 collective-permute-done.1.do1
  23.4 2.4 %collective-permute-start.10 = (bf16[8,2,64,128]{3,2,1,0:T(8,128)(2,1)S(1)}, bf16[8,2,64,128]{3,2,1,0:T(8,128)(2,1)S(1)}, u32[]{:S(2)}, u32[]{:S(2)}) collective-permute-start(bf16[8,2,64,128]{3,2,1,0:T(8,128)(2,1)S(1)} %assemble.5), channel_id=1, source_target_pairs={{0,24},{8,16},{16,8},{24,0},{1,25},{9,17},{17,9},{25,1},{2,26},{10... | collective-permute-start | bytes 786440 | tf_op jit(solution)/shard_map/ppermute | solution.py:350
  25.9 2.0 %chunk.6 = (f32[128,2048]{1,0:T(8,128)S(1)}, f32[4,2,64,128]{3,2,1,0:T(8,128)S(1)}) custom-call(s32[19]{0:T(128)S(1)} %pad_add_fusion.1.where, bf16[1024,128]{1,0:T(8,128)(2,1)S(1)} %get-tuple-element.34.q0, bf16[1024,128]{1,0:T(8,128)(2,1)S(1)} %get-tuple-element.35.do0, f32[8,256]{1,0:T(8,128)S(1)} %get-tuple-element.36.stats0, ...), custom_call_target="tpu_custom_call" | custom-call | flops 1342177280 | bytes 262144 | tf_op jit(solution)/shard_map/chunk/pallas_call | solution.py:233
  27.8 0.0 collective-permute-done.13.rest_0_
  27.8 3.2 %chunk.7 = (f32[128,2048]{1,0:T(8,128)S(1)}, bf16[8,2,64,128]{3,2,1,0:T(8,128)(2,1)S(1)}) custom-call(s32[19]{0:T(128)S(1)} %pad_add_fusion.1.where, bf16[1024,128]{1,0:T(8,128)(2,1)S(1)} %get-tuple-element.34.q0, bf16[1024,128]{1,0:T(8,128)(2,1)S(1)} %get-tuple-element.35.do0, ...), custom_call_target="tpu_custom_call", output_to_operand_aliasing={{0}: (9, {})} | custom-call | flops 2684354560 | bytes 262144 | tf_op jit(solution)/shard_map/chunk/pallas_call | solution.py:233
  31.1 0.0 collective-permute-done.11.rest_0_
  31.1 3.2 %chunk.8 = (f32[128,2048]{1,0:T(8,128)S(1)}, bf16[4,2,64,128]{3,2,1,0:T(8,128)(2,1)S(1)}, bf16[4,2,64,128]{3,2,1,0:T(8,128)(2,1)S(1)}) custom-call(s32[19]{0:T(128)S(1)} %pad_add_fusion.1.where, bf16[1024,128]{1,0:T(8,128)(2,1)S(1)} %get-tuple-element.34.q0, bf16[1024,128]{1,0:T(8,128)(2,1)S(1)} %get-tuple-element.35.do0, ...), custom_call_target="tpu_custom_call", output_to_operand_aliasing={{0}: (9, {})} | custom-call | flops 2684354560 | bytes 262144 | tf_op jit(solution)/shard_map/chunk/pallas_call | solution.py:233
  34.4 1.2 %collective-permute-start.17 = (bf16[4,2,64,128]{3,2,1,0:T(8,128)(2,1)S(1)}, bf16[4,2,64,128]{3,2,1,0:T(8,128)(2,1)S(1)}, u32[]{:S(2)}, u32[]{:S(2)}) collective-permute-start(bf16[4,2,64,128]{3,2,1,0:T(8,128)(2,1)S(1)} %get-tuple-element.54), channel_id=1, source_target_pairs={{0,8},{8,0},{16,24},{24,16},{1,9},{9,1},{17,25},{25,17},{2,10},{10... | collective-permute-start | bytes 393224 | tf_op jit(solution)/shard_map/ppermute | solution.py:350
  35.5 0.9 %collective-permute-start.20 = (bf16[4,2,64,128]{3,2,1,0:T(8,128)(2,1)S(1)}, bf16[4,2,64,128]{3,2,1,0:T(8,128)(2,1)S(1)}, u32[]{:S(2)}, u32[]{:S(2)}) collective-permute-start(bf16[4,2,64,128]{3,2,1,0:T(8,128)(2,1)S(1)} %get-tuple-element.59), channel_id=1, source_target_pairs={{0,8},{8,0},{16,24},{24,16},{1,9},{9,1},{17,25},{25,17},{2,10},{10... | collective-permute-start | bytes 393224 | tf_op jit(solution)/shard_map/ppermute | solution.py:350
  36.4 1.1 %collective-permute-start.16 = (bf16[8,2,64,128]{3,2,1,0:T(8,128)(2,1)S(1)}, bf16[8,2,64,128]{3,2,1,0:T(8,128)(2,1)S(1)}, u32[]{:S(2)}, u32[]{:S(2)}) collective-permute-start(bf16[8,2,64,128]{3,2,1,0:T(8,128)(2,1)S(1)} %get-tuple-element.53), channel_id=1, source_target_pairs={{0,16},{8,24},{16,0},{24,8},{1,17},{9,25},{17,1},{25,9},{2,18},{10... | collective-permute-start | bytes 786440 | tf_op jit(solution)/shard_map/ppermute | solution.py:350
  37.6 2.0 %chunk.9 = (f32[128,2048]{1,0:T(8,128)S(1)}, bf16[4,2,64,128]{3,2,1,0:T(8,128)(2,1)S(1)}) custom-call(s32[19]{0:T(128)S(1)} %pad_add_fusion.1.where, bf16[1024,128]{1,0:T(8,128)(2,1)S(1)} %get-tuple-element.34.q0, bf16[1024,128]{1,0:T(8,128)(2,1)S(1)} %get-tuple-element.35.do0, ...), custom_call_target="tpu_custom_call", output_to_operand_aliasing={{0}: (8, {})} | custom-call | flops 1342177280 | bytes 524288 | tf_op jit(solution)/shard_map/chunk/pallas_call | solution.py:233
  39.6 2.0 %chunk.10 = (f32[128,2048]{1,0:T(8,128)S(1)}, bf16[4,2,64,128]{3,2,1,0:T(8,128)(2,1)S(1)}) custom-call(s32[19]{0:T(128)S(1)} %pad_add_fusion.1.where, bf16[1024,128]{1,0:T(8,128)(2,1)S(1)} %get-tuple-element.34.q0, bf16[1024,128]{1,0:T(8,128)(2,1)S(1)} %get-tuple-element.35.do0, ...), custom_call_target="tpu_custom_call", output_to_operand_aliasing={{0}: (8, {})} | custom-call | flops 1342177280 | bytes 524288 | tf_op jit(solution)/shard_map/chunk/pallas_call | solution.py:233
  41.6 1.5 %collective-permute-start.18 = (bf16[4,2,64,128]{3,2,1,0:T(8,128)(2,1)S(1)}, bf16[4,2,64,128]{3,2,1,0:T(8,128)(2,1)S(1)}, u32[]{:S(2)}, u32[]{:S(2)}) collective-permute-start(bf16[4,2,64,128]{3,2,1,0:T(8,128)(2,1)S(1)} %get-tuple-element.55), channel_id=1, source_target_pairs={{0,24},{8,16},{16,8},{24,0},{1,25},{9,17},{17,9},{25,1},{2,26},{10... | collective-permute-start | bytes 393224 | tf_op jit(solution)/shard_map/ppermute | solution.py:350
  43.1 1.5 %collective-permute-start.21 = (bf16[4,2,64,128]{3,2,1,0:T(8,128)(2,1)S(1)}, bf16[4,2,64,128]{3,2,1,0:T(8,128)(2,1)S(1)}, u32[]{:S(2)}, u32[]{:S(2)}) collective-permute-start(bf16[4,2,64,128]{3,2,1,0:T(8,128)(2,1)S(1)} %get-tuple-element.60), channel_id=1, source_target_pairs={{0,24},{8,16},{16,8},{24,0},{1,25},{9,17},{17,9},{25,1},{2,26},{10... | collective-permute-start | bytes 393224 | tf_op jit(solution)/shard_map/ppermute | solution.py:350
  44.6 2.0 %chunk.11 = (f32[128,2048]{1,0:T(8,128)S(1)}, f32[4,2,64,128]{3,2,1,0:T(8,128)S(1)}) custom-call(s32[19]{0:T(128)S(1)} %pad_add_fusion.1.where, bf16[1024,128]{1,0:T(8,128)(2,1)S(1)} %get-tuple-element.34.q0, bf16[1024,128]{1,0:T(8,128)(2,1)S(1)} %get-tuple-element.35.do0, f32[8,256]{1,0:T(8,128)S(1)} %get-tuple-element.36.stats0, ...), custom_call_target="tpu_custom_call", output_to_operand_aliasing={{0}: (9, {})} | custom-call | flops 1342177280 | bytes 262144 | tf_op jit(solution)/shard_map/chunk/pallas_call | solution.py:233
  46.6 0.2 finish_q.1
  46.8 0.0 collective-permute-done.20.refs_1_
  46.8 0.1 collective-permute-start.15
  46.9 2.3 %collective-permute-done.21.refs_2_ = bf16[4,2,64,128]{3,2,1,0:T(8,128)(2,1)S(1)} collective-permute-done((bf16[4,2,64,128]{3,2,1,0:T(8,128)(2,1)S(1)}, bf16[4,2,64,128]{3,2,1,0:T(8,128)(2,1)S(1)}, u32[]{:S(2)}, u32[]{:S(2)}) %collective-permute-start.21) | collective-permute-done | bytes 131104 | tf_op jit(solution)/shard_map/ppermute | solution.py:350
  49.2 0.0 collective-permute-done.16.refs_0_
  49.2 0.1 collect.3
  49.3 1.8 %collective-permute-start.22 = (bf16[2,2,64,128]{3,2,1,0:T(8,128)(2,1)S(1)}, bf16[2,2,64,128]{3,2,1,0:T(8,128)(2,1)S(1)}, u32[]{:S(2)}, u32[]{:S(2)}) collective-permute-start(bf16[2,2,64,128]{3,2,1,0:T(8,128)(2,1)S(1)} %get-tuple-element.61), channel_id=1, source_target_pairs={{0,2},{1,3},{2,0},{3,1},{4,6},{5,7},{6,4},{7,5},{8,10},{9,11},{10,... | collective-permute-start | bytes 196616 | tf_op jit(solution)/shard_map/ppermute | solution.py:350
  51.2 1.0 %collective-permute-start.23 = (bf16[2,2,64,128]{3,2,1,0:T(8,128)(2,1)S(1)}, bf16[2,2,64,128]{3,2,1,0:T(8,128)(2,1)S(1)}, u32[]{:S(2)}, u32[]{:S(2)}) collective-permute-start(bf16[2,2,64,128]{3,2,1,0:T(8,128)(2,1)S(1)} %get-tuple-element.62), channel_id=1, source_target_pairs={{0,3},{1,2},{2,1},{3,0},{4,7},{5,6},{6,5},{7,4},{8,11},{9,10},{10,... | collective-permute-start | bytes 196616 | tf_op jit(solution)/shard_map/ppermute | solution.py:350
  52.2 0.0 collective-permute-done.17.refs_1_
  52.2 0.1 collect.2
  52.3 0.7 %collective-permute-start.19 = (bf16[2,2,64,128]{3,2,1,0:T(8,128)(2,1)S(1)}, bf16[2,2,64,128]{3,2,1,0:T(8,128)(2,1)S(1)}, u32[]{:S(2)}, u32[]{:S(2)}) collective-permute-start(bf16[2,2,64,128]{3,2,1,0:T(8,128)(2,1)S(1)} %get-tuple-element.57), channel_id=1, source_target_pairs={{0,1},{1,0},{2,3},{3,2},{4,5},{5,4},{6,7},{7,6},{8,9},{9,8},{10,11... | collective-permute-start | bytes 196616 | tf_op jit(solution)/shard_map/ppermute | solution.py:350
  53.0 0.0 collective-permute-start.24
  53.0 2.4 %collective-permute-done.22.refs_2_ = bf16[2,2,64,128]{3,2,1,0:T(8,128)(2,1)S(1)} collective-permute-done((bf16[2,2,64,128]{3,2,1,0:T(8,128)(2,1)S(1)}, bf16[2,2,64,128]{3,2,1,0:T(8,128)(2,1)S(1)}, u32[]{:S(2)}, u32[]{:S(2)}) %collective-permute-start.22) | collective-permute-done | bytes 65568 | tf_op jit(solution)/shard_map/ppermute | solution.py:350
  55.4 0.0 collective-permute-start.26
  55.4 1.9 %collective-permute-done.23.refs_3_ = bf16[2,2,64,128]{3,2,1,0:T(8,128)(2,1)S(1)} collective-permute-done((bf16[2,2,64,128]{3,2,1,0:T(8,128)(2,1)S(1)}, bf16[2,2,64,128]{3,2,1,0:T(8,128)(2,1)S(1)}, u32[]{:S(2)}, u32[]{:S(2)}) %collective-permute-start.23) | collective-permute-done | bytes 65568 | tf_op jit(solution)/shard_map/ppermute | solution.py:350
  57.3 0.0 collective-permute-start.27
  57.3 0.0 collective-permute-done.19.refs_1_
  57.3 0.5 collective-permute-start.25
  57.8 0.0 collective-permute-done.24.refs_4_
  57.8 0.7 %collective-permute-done.27.refs_7_ = bf16[2,2,64,128]{3,2,1,0:T(8,128)(2,1)S(1)} collective-permute-done((bf16[2,2,64,128]{3,2,1,0:T(8,128)(2,1)S(1)}, bf16[2,2,64,128]{3,2,1,0:T(8,128)(2,1)S(1)}, u32[]{:S(2)}, u32[]{:S(2)}) %collective-permute-start.27) | collective-permute-done | bytes 65568 | tf_op jit(solution)/shard_map/ppermute | solution.py:350
  58.6 0.2 collective-permute-done.25.refs_5_
  58.7 1.3 %unpack_kv.1 = (bf16[64,1024]{1,0:T(8,128)(2,1)}, bf16[64,1024]{1,0:T(8,128)(2,1)}) custom-call(s32[3]{0:T(128)S(1)} %pad_add_fusion.where, bf16[2,2,64,128]{3,2,1,0:T(8,128)(2,1)S(1)} %get-tuple-element.56.refs_0_, bf16[2,2,64,128]{3,2,1,0:T(8,128)(2,1)S(1)} %collective-permute-done.19.refs_1_, bf16[2,2,64,128]{3,2,1,0:T(8,128)(2,1)S(1)} %collective-permute-done.22.refs_2_, ...), custom_call_target="tpu_custom_call" | custom-call | flops 1000000 | bytes 524288 | tf_op jit(solution)/shard_map/unpack_kv/pallas_call | solution.py:338
  60.0 1.4 %place_q.1 = bf16[256,1024]{1,0:T(8,128)(2,1)} custom-call(s32[3]{0:T(128)S(1)} %pad_add_fusion.where, bf16[256,512]{1,0:T(8,128)(2,1)S(1)} %get-tuple-element.50.mine, bf16[256,512]{1,0:T(8,128)(2,1)S(1)} %collective-permute-done.15.theirs), custom_call_target="tpu_custom_call" | custom-call | flops 1000000 | bytes 1048576 | tf_op jit(solution)/shard_map/place_q/pallas_call | solution.py:286
  (14 shorter events, 0.1 us)
Async XLA Ops:
  0.7 4.7 %copy-start = (f32[8,256]{1,0:T(8,128)S(1)}, f32[8,256]{1,0:T(8,128)}, u32[]{:S(2)}) copy-start(f32[8,256]{1,0:T(8,128)} %lse.1) | copy-start | bytes 24580
  2.3 9.0 %collective-permute-start.6 = (bf16[2,2,64,128]{3,2,1,0:T(8,128)(2,1)S(1)}, bf16[2,2,64,128]{3,2,1,0:T(8,128)(2,1)S(1)}, u32[]{:S(2)}, u32[]{:S(2)}) collective-permute-start(bf16[2,2,64,128]{3,2,1,0:T(8,128)(2,1)S(1)} %get-tuple-element.42), channel_id=1, source_target_pairs={{0,1},{1,0},{2,3},{3,2},{4,5},{5,4},{6,7},{7,6},{8,9},{9,8},{10,11... | collective-permute-start | bytes 196616 | tf_op jit(solution)/shard_map/ppermute | solution.py:350
  8.1 14.7 %collective-permute-start = (bf16[1024,128]{1,0:T(8,128)(2,1)S(1)}, bf16[1024,128]{1,0:T(8,128)(2,1)S(1)}, u32[]{:S(2)}, u32[]{:S(2)}) collective-permute-start(bf16[1024,128]{1,0:T(8,128)(2,1)S(1)} %get-tuple-element.37), channel_id=1, source_target_pairs={{0,4},{4,0},{1,5},{5,1},{2,6},{6,2},{3,7},{7,3},{8,12},{12,8},{9,1... | collective-permute-start | bytes 786440 | tf_op jit(solution)/shard_map/ppermute | solution.py:350
  8.2 15.2 %collective-permute-start.1 = (bf16[1024,128]{1,0:T(8,128)(2,1)S(1)}, bf16[1024,128]{1,0:T(8,128)(2,1)S(1)}, u32[]{:S(2)}, u32[]{:S(2)}) collective-permute-start(bf16[1024,128]{1,0:T(8,128)(2,1)S(1)} %get-tuple-element.38), channel_id=1, source_target_pairs={{0,4},{4,0},{1,5},{5,1},{2,6},{6,2},{3,7},{7,3},{8,12},{12,8},{9,1... | collective-permute-start | bytes 786440 | tf_op jit(solution)/shard_map/ppermute | solution.py:350
  8.7 6.2 %collective-permute-start.7 = (bf16[2,2,64,128]{3,2,1,0:T(8,128)(2,1)S(1)}, bf16[2,2,64,128]{3,2,1,0:T(8,128)(2,1)S(1)}, u32[]{:S(2)}, u32[]{:S(2)}) collective-permute-start(bf16[2,2,64,128]{3,2,1,0:T(8,128)(2,1)S(1)} %get-tuple-element.43), channel_id=1, source_target_pairs={{0,3},{1,2},{2,1},{3,0},{4,7},{5,6},{6,5},{7,4},{8,11},{9,10},{10,... | collective-permute-start | bytes 196616 | tf_op jit(solution)/shard_map/ppermute | solution.py:350
  11.2 6.7 %collective-permute-start.3 = (bf16[2,2,64,128]{3,2,1,0:T(8,128)(2,1)S(1)}, bf16[2,2,64,128]{3,2,1,0:T(8,128)(2,1)S(1)}, u32[]{:S(2)}, u32[]{:S(2)}) collective-permute-start(bf16[2,2,64,128]{3,2,1,0:T(8,128)(2,1)S(1)} %get-tuple-element.41), channel_id=1, source_target_pairs={{0,2},{1,3},{2,0},{3,1},{4,6},{5,7},{6,4},{7,5},{8,10},{9,11},{10,... | collective-permute-start | bytes 196616 | tf_op jit(solution)/shard_map/ppermute | solution.py:350
  11.3 6.5 %collective-permute-start.8 = (bf16[2,2,64,128]{3,2,1,0:T(8,128)(2,1)S(1)}, bf16[2,2,64,128]{3,2,1,0:T(8,128)(2,1)S(1)}, u32[]{:S(2)}, u32[]{:S(2)}) collective-permute-start(bf16[2,2,64,128]{3,2,1,0:T(8,128)(2,1)S(1)} %collective-permute-done.6.refs_0_.refs_2_), channel_id=1, source_target_pairs={{0,4},{4,0},{1,5},{5,1},{2,6},{6,2},{3,7},{7,3},{8,12},{12,8},{9,1... | collective-permute-start | bytes 196616 | tf_op jit(solution)/shard_map/ppermute | solution.py:350
  14.9 3.4 %collective-permute-start.9 = (bf16[2,2,64,128]{3,2,1,0:T(8,128)(2,1)S(1)}, bf16[2,2,64,128]{3,2,1,0:T(8,128)(2,1)S(1)}, u32[]{:S(2)}, u32[]{:S(2)}) collective-permute-start(bf16[2,2,64,128]{3,2,1,0:T(8,128)(2,1)S(1)} %collective-permute-done.7.refs_1_.refs_3_), channel_id=1, source_target_pairs={{0,4},{4,0},{1,5},{5,1},{2,6},{6,2},{3,7},{7,3},{8,12},{12,8},{9,1... | collective-permute-start | bytes 196616 | tf_op jit(solution)/shard_map/ppermute | solution.py:350
  17.8 1.3 %collective-permute-start.4 = (bf16[2,2,64,128]{3,2,1,0:T(8,128)(2,1)S(1)}, bf16[2,2,64,128]{3,2,1,0:T(8,128)(2,1)S(1)}, u32[]{:S(2)}, u32[]{:S(2)}) collective-permute-start(bf16[2,2,64,128]{3,2,1,0:T(8,128)(2,1)S(1)} %get-tuple-element.40.refs_0_), channel_id=1, source_target_pairs={{0,4},{4,0},{1,5},{5,1},{2,6},{6,2},{3,7},{7,3},{8,12},{12,8},{9,1... | collective-permute-start | bytes 196616 | tf_op jit(solution)/shard_map/ppermute | solution.py:350
  17.8 2.8 %collective-permute-start.5 = (bf16[2,2,64,128]{3,2,1,0:T(8,128)(2,1)S(1)}, bf16[2,2,64,128]{3,2,1,0:T(8,128)(2,1)S(1)}, u32[]{:S(2)}, u32[]{:S(2)}) collective-permute-start(bf16[2,2,64,128]{3,2,1,0:T(8,128)(2,1)S(1)} %collective-permute-done.3.refs_1_), channel_id=1, source_target_pairs={{0,4},{4,0},{1,5},{5,1},{2,6},{6,2},{3,7},{7,3},{8,12},{12,8},{9,1... | collective-permute-start | bytes 196616 | tf_op jit(solution)/shard_map/ppermute | solution.py:350
  18.3 3.0 %collective-permute-start.2 = (f32[8,256]{1,0:T(8,128)S(1)}, f32[8,256]{1,0:T(8,128)S(1)}, u32[]{:S(2)}, u32[]{:S(2)}) collective-permute-start(f32[8,256]{1,0:T(8,128)S(1)} %get-tuple-element.39), channel_id=1, source_target_pairs={{0,4},{4,0},{1,5},{5,1},{2,6},{6,2},{3,7},{7,3},{8,12},{12,8},{9,1... | collective-permute-start | bytes 24584 | tf_op jit(solution)/shard_map/ppermute | solution.py:350
  18.4 2.8 %copy-start.1 = (s32[16]{0:T(128)S(1)}, s32[16]{0:T(128)}, u32[]{:S(2)}) copy-start(s32[16]{0:T(128)} %param.13) | copy-start | bytes 196
  19.1 8.7 %collective-permute-start.14 = (bf16[4,2,64,128]{3,2,1,0:T(8,128)(2,1)S(1)}, bf16[4,2,64,128]{3,2,1,0:T(8,128)(2,1)S(1)}, u32[]{:S(2)}, u32[]{:S(2)}) collective-permute-start(bf16[4,2,64,128]{3,2,1,0:T(8,128)(2,1)S(1)} %assemble.4.rest_1_), channel_id=1, source_target_pairs={{0,16},{8,24},{16,0},{24,8},{1,17},{9,25},{17,1},{25,9},{2,18},{10... | collective-permute-start | bytes 393224 | tf_op jit(solution)/shard_map/ppermute | solution.py:350
  20.6 7.2 %collective-permute-start.13 = (bf16[4,2,64,128]{3,2,1,0:T(8,128)(2,1)S(1)}, bf16[4,2,64,128]{3,2,1,0:T(8,128)(2,1)S(1)}, u32[]{:S(2)}, u32[]{:S(2)}) collective-permute-start(bf16[4,2,64,128]{3,2,1,0:T(8,128)(2,1)S(1)} %assemble.3.rest_0_), channel_id=1, source_target_pairs={{0,16},{8,24},{16,0},{24,8},{1,17},{9,25},{17,1},{25,9},{2,18},{10... | collective-permute-start | bytes 393224 | tf_op jit(solution)/shard_map/ppermute | solution.py:350
  21.3 9.8 %collective-permute-start.12 = (bf16[4,2,64,128]{3,2,1,0:T(8,128)(2,1)S(1)}, bf16[4,2,64,128]{3,2,1,0:T(8,128)(2,1)S(1)}, u32[]{:S(2)}, u32[]{:S(2)}) collective-permute-start(bf16[4,2,64,128]{3,2,1,0:T(8,128)(2,1)S(1)} %assemble.4.rest_1_), channel_id=1, source_target_pairs={{0,8},{8,0},{16,24},{24,16},{1,9},{9,1},{17,25},{25,17},{2,10},{10... | collective-permute-start | bytes 393224 | tf_op jit(solution)/shard_map/ppermute | solution.py:350
  22.9 8.2 %collective-permute-start.11 = (bf16[4,2,64,128]{3,2,1,0:T(8,128)(2,1)S(1)}, bf16[4,2,64,128]{3,2,1,0:T(8,128)(2,1)S(1)}, u32[]{:S(2)}, u32[]{:S(2)}) collective-permute-start(bf16[4,2,64,128]{3,2,1,0:T(8,128)(2,1)S(1)} %assemble.3.rest_0_), channel_id=1, source_target_pairs={{0,8},{8,0},{16,24},{24,16},{1,9},{9,1},{17,25},{25,17},{2,10},{10... | collective-permute-start | bytes 393224 | tf_op jit(solution)/shard_map/ppermute | solution.py:350
  23.4 14.2 %collective-permute-start.10 = (bf16[8,2,64,128]{3,2,1,0:T(8,128)(2,1)S(1)}, bf16[8,2,64,128]{3,2,1,0:T(8,128)(2,1)S(1)}, u32[]{:S(2)}, u32[]{:S(2)}) collective-permute-start(bf16[8,2,64,128]{3,2,1,0:T(8,128)(2,1)S(1)} %assemble.5), channel_id=1, source_target_pairs={{0,24},{8,16},{16,8},{24,0},{1,25},{9,17},{17,9},{25,1},{2,26},{10... | collective-permute-start | bytes 786440 | tf_op jit(solution)/shard_map/ppermute | solution.py:350
  34.4 17.8 %collective-permute-start.17 = (bf16[4,2,64,128]{3,2,1,0:T(8,128)(2,1)S(1)}, bf16[4,2,64,128]{3,2,1,0:T(8,128)(2,1)S(1)}, u32[]{:S(2)}, u32[]{:S(2)}) collective-permute-start(bf16[4,2,64,128]{3,2,1,0:T(8,128)(2,1)S(1)} %get-tuple-element.54), channel_id=1, source_target_pairs={{0,8},{8,0},{16,24},{24,16},{1,9},{9,1},{17,25},{25,17},{2,10},{10... | collective-permute-start | bytes 393224 | tf_op jit(solution)/shard_map/ppermute | solution.py:350
  35.5 11.3 %collective-permute-start.20 = (bf16[4,2,64,128]{3,2,1,0:T(8,128)(2,1)S(1)}, bf16[4,2,64,128]{3,2,1,0:T(8,128)(2,1)S(1)}, u32[]{:S(2)}, u32[]{:S(2)}) collective-permute-start(bf16[4,2,64,128]{3,2,1,0:T(8,128)(2,1)S(1)} %get-tuple-element.59), channel_id=1, source_target_pairs={{0,8},{8,0},{16,24},{24,16},{1,9},{9,1},{17,25},{25,17},{2,10},{10... | collective-permute-start | bytes 393224 | tf_op jit(solution)/shard_map/ppermute | solution.py:350
  36.4 12.8 %collective-permute-start.16 = (bf16[8,2,64,128]{3,2,1,0:T(8,128)(2,1)S(1)}, bf16[8,2,64,128]{3,2,1,0:T(8,128)(2,1)S(1)}, u32[]{:S(2)}, u32[]{:S(2)}) collective-permute-start(bf16[8,2,64,128]{3,2,1,0:T(8,128)(2,1)S(1)} %get-tuple-element.53), channel_id=1, source_target_pairs={{0,16},{8,24},{16,0},{24,8},{1,17},{9,25},{17,1},{25,9},{2,18},{10... | collective-permute-start | bytes 786440 | tf_op jit(solution)/shard_map/ppermute | solution.py:350
  41.6 10.6 %collective-permute-start.18 = (bf16[4,2,64,128]{3,2,1,0:T(8,128)(2,1)S(1)}, bf16[4,2,64,128]{3,2,1,0:T(8,128)(2,1)S(1)}, u32[]{:S(2)}, u32[]{:S(2)}) collective-permute-start(bf16[4,2,64,128]{3,2,1,0:T(8,128)(2,1)S(1)} %get-tuple-element.55), channel_id=1, source_target_pairs={{0,24},{8,16},{16,8},{24,0},{1,25},{9,17},{17,9},{25,1},{2,26},{10... | collective-permute-start | bytes 393224 | tf_op jit(solution)/shard_map/ppermute | solution.py:350
  43.1 6.1 %collective-permute-start.21 = (bf16[4,2,64,128]{3,2,1,0:T(8,128)(2,1)S(1)}, bf16[4,2,64,128]{3,2,1,0:T(8,128)(2,1)S(1)}, u32[]{:S(2)}, u32[]{:S(2)}) collective-permute-start(bf16[4,2,64,128]{3,2,1,0:T(8,128)(2,1)S(1)} %get-tuple-element.60), channel_id=1, source_target_pairs={{0,24},{8,16},{16,8},{24,0},{1,25},{9,17},{17,9},{25,1},{2,26},{10... | collective-permute-start | bytes 393224 | tf_op jit(solution)/shard_map/ppermute | solution.py:350
  46.8 13.2 %collective-permute-start.15 = (bf16[256,512]{1,0:T(8,128)(2,1)S(1)}, bf16[256,512]{1,0:T(8,128)(2,1)S(1)}, u32[]{:S(2)}, u32[]{:S(2)}) collective-permute-start(bf16[256,512]{1,0:T(8,128)(2,1)S(1)} %get-tuple-element.51), channel_id=1, source_target_pairs={{0,4},{4,0},{1,5},{5,1},{2,6},{6,2},{3,7},{7,3},{8,12},{12,8},{9,1... | collective-permute-start | bytes 786440 | tf_op jit(solution)/shard_map/ppermute | solution.py:350
  49.3 6.1 %collective-permute-start.22 = (bf16[2,2,64,128]{3,2,1,0:T(8,128)(2,1)S(1)}, bf16[2,2,64,128]{3,2,1,0:T(8,128)(2,1)S(1)}, u32[]{:S(2)}, u32[]{:S(2)}) collective-permute-start(bf16[2,2,64,128]{3,2,1,0:T(8,128)(2,1)S(1)} %get-tuple-element.61), channel_id=1, source_target_pairs={{0,2},{1,3},{2,0},{3,1},{4,6},{5,7},{6,4},{7,5},{8,10},{9,11},{10,... | collective-permute-start | bytes 196616 | tf_op jit(solution)/shard_map/ppermute | solution.py:350
  51.2 6.1 %collective-permute-start.23 = (bf16[2,2,64,128]{3,2,1,0:T(8,128)(2,1)S(1)}, bf16[2,2,64,128]{3,2,1,0:T(8,128)(2,1)S(1)}, u32[]{:S(2)}, u32[]{:S(2)}) collective-permute-start(bf16[2,2,64,128]{3,2,1,0:T(8,128)(2,1)S(1)} %get-tuple-element.62), channel_id=1, source_target_pairs={{0,3},{1,2},{2,1},{3,0},{4,7},{5,6},{6,5},{7,4},{8,11},{9,10},{10,... | collective-permute-start | bytes 196616 | tf_op jit(solution)/shard_map/ppermute | solution.py:350
  52.3 5.0 %collective-permute-start.19 = (bf16[2,2,64,128]{3,2,1,0:T(8,128)(2,1)S(1)}, bf16[2,2,64,128]{3,2,1,0:T(8,128)(2,1)S(1)}, u32[]{:S(2)}, u32[]{:S(2)}) collective-permute-start(bf16[2,2,64,128]{3,2,1,0:T(8,128)(2,1)S(1)} %get-tuple-element.57), channel_id=1, source_target_pairs={{0,1},{1,0},{2,3},{3,2},{4,5},{5,4},{6,7},{7,6},{8,9},{9,8},{10,11... | collective-permute-start | bytes 196616 | tf_op jit(solution)/shard_map/ppermute | solution.py:350
  53.0 4.8 %collective-permute-start.24 = (bf16[2,2,64,128]{3,2,1,0:T(8,128)(2,1)S(1)}, bf16[2,2,64,128]{3,2,1,0:T(8,128)(2,1)S(1)}, u32[]{:S(2)}, u32[]{:S(2)}) collective-permute-start(bf16[2,2,64,128]{3,2,1,0:T(8,128)(2,1)S(1)} %get-tuple-element.56.refs_0_), channel_id=1, source_target_pairs={{0,4},{4,0},{1,5},{5,1},{2,6},{6,2},{3,7},{7,3},{8,12},{12,8},{9,1... | collective-permute-start | bytes 196616 | tf_op jit(solution)/shard_map/ppermute | solution.py:350
  55.4 2.4 %collective-permute-start.26 = (bf16[2,2,64,128]{3,2,1,0:T(8,128)(2,1)S(1)}, bf16[2,2,64,128]{3,2,1,0:T(8,128)(2,1)S(1)}, u32[]{:S(2)}, u32[]{:S(2)}) collective-permute-start(bf16[2,2,64,128]{3,2,1,0:T(8,128)(2,1)S(1)} %collective-permute-done.22.refs_2_), channel_id=1, source_target_pairs={{0,4},{4,0},{1,5},{5,1},{2,6},{6,2},{3,7},{7,3},{8,12},{12,8},{9,1... | collective-permute-start | bytes 196616 | tf_op jit(solution)/shard_map/ppermute | solution.py:350
  57.3 1.3 %collective-permute-start.27 = (bf16[2,2,64,128]{3,2,1,0:T(8,128)(2,1)S(1)}, bf16[2,2,64,128]{3,2,1,0:T(8,128)(2,1)S(1)}, u32[]{:S(2)}, u32[]{:S(2)}) collective-permute-start(bf16[2,2,64,128]{3,2,1,0:T(8,128)(2,1)S(1)} %collective-permute-done.23.refs_3_), channel_id=1, source_target_pairs={{0,4},{4,0},{1,5},{5,1},{2,6},{6,2},{3,7},{7,3},{8,12},{12,8},{9,1... | collective-permute-start | bytes 196616 | tf_op jit(solution)/shard_map/ppermute | solution.py:350
  57.3 1.4 %collective-permute-start.25 = (bf16[2,2,64,128]{3,2,1,0:T(8,128)(2,1)S(1)}, bf16[2,2,64,128]{3,2,1,0:T(8,128)(2,1)S(1)}, u32[]{:S(2)}, u32[]{:S(2)}) collective-permute-start(bf16[2,2,64,128]{3,2,1,0:T(8,128)(2,1)S(1)} %collective-permute-done.19.refs_1_), channel_id=1, source_target_pairs={{0,4},{4,0},{1,5},{5,1},{2,6},{6,2},{3,7},{7,3},{8,12},{12,8},{9,1... | collective-permute-start | bytes 196616 | tf_op jit(solution)/shard_map/ppermute | solution.py:350
